TPU v7x, 32 devices: a whole 2x2x4 slice. The times are simulated.
32 devices in a mesh: layer: 2 (over y), gx: 4 (over z), gy: 4 (over x, core).
Axes of the slice: x: 2, y: 2, z: 4, core: 2. Of those that a mesh axis runs over, the one named last changes fastest.
Arguments:
- rhs: float32 [2, 512, 512], P('layer', 'gx', 'gy'), may hold values from -7 to 7
- start: float32 [2, 512, 512], P('layer', 'gx', 'gy'), may hold values from -4 to 4
- valid: int32 [8, 512, 512], P(None, 'gx', 'gy'), may hold values 0 or 1
- reg: float32 [2], P('layer'), may hold values from 0.25 to 2
- shifts: int32 [8, 2, 2], replicated, may hold values from -16 to 16, as said below
- frac: int32 [8, 2, 2], replicated, may hold values from 0 to 255
Outputs:
- solution: float32 [2, 512, 512], P('layer', 'gx', 'gy')
- residual: float32 [2, 512, 512], P('layer', 'gx', 'gy')
Inputs may be any that keep to these rules, and one draw needn't show every extreme that they name: `shifts`: offsets in whole grid points; some guide star reaches offset 16 along the first dimension and minus 16 along the second on some layer.
All inputs are finite; a program needn't handle non-finite values. No bound on the sum of `valid` on one device may be relied on, other than what follows from the above.
Results may differ from a plain program's by a relative error of at most 0.00011.
Values sent between devices are 32-bit elements; how exact they have to be, the bound alone decides.
No kernel may reach another device: no remote copies, remote signals or barrier semaphores. Data moves between devices by JAX's collectives and lax.ppermute only.
A program may use at most 64 MiB of HBM per device.

v0:
```python
import jax
import jax.numpy as jnp
from jax import lax
from jax.sharding import PartitionSpec as P

GUIDES = 8
SHIFT_MAX = 16
LEVELS = 3
ITERS = 2


def extended(cells, sides, width):
    for axis, dim in sides:
        count = lax.axis_size(axis)
        ends = count - 1
        head = lax.slice_in_dim(cells, 0, width, axis=dim)
        tail = lax.slice_in_dim(cells, cells.shape[dim] - width, cells.shape[dim], axis=dim)
        cells = jnp.concatenate(
            [
                lax.ppermute(tail, axis, [(i, (i + 1) % count) for i in range(ends)]),
                cells,
                lax.ppermute(head, axis, [((i + 1) % count, i) for i in range(ends)]),
            ],
            axis=dim,
        )
    return cells


def interp(plane, offset, fraction, sign, tile_rows, tile_cols):
    width = SHIFT_MAX + 1
    frac_row = fraction[0].astype(jnp.float32) / 256.0
    frac_col = fraction[1].astype(jnp.float32) / 256.0
    result = jnp.zeros((tile_rows, tile_cols), jnp.float32)
    for step_row, step_col, factor in (
        (0, 0, (1.0 - frac_row) * (1.0 - frac_col)),
        (1, 0, frac_row * (1.0 - frac_col)),
        (0, 1, (1.0 - frac_row) * frac_col),
        (1, 1, frac_row * frac_col),
    ):
        begin_row = width + sign * (offset[0] + step_row)
        begin_col = width + sign * (offset[1] + step_col)
        pieces = lax.dynamic_slice(plane, (begin_row, begin_col), (tile_rows, tile_cols))
        result = result + factor * pieces
    return result


def neighbours(padded):
    return (
        padded[2:, 1:-1]
        + padded[:-2, 1:-1]
        + padded[1:-1, 2:]
        + padded[1:-1, :-2]
        - 4.0 * padded[1:-1, 1:-1]
    )


def bilaplace(values):
    tile_rows, tile_cols = values.shape
    padded = extended(values, (("gx", 0), ("gy", 1)), 2)
    inner = neighbours(padded)
    row_at = lax.axis_index("gx") * tile_rows + jnp.arange(tile_rows + 2, dtype=jnp.int32) - 1
    col_at = lax.axis_index("gy") * tile_cols + jnp.arange(tile_cols + 2, dtype=jnp.int32) - 1
    row_ok = (row_at >= 0) & (row_at < tile_rows * lax.axis_size("gx"))
    col_ok = (col_at >= 0) & (col_at < tile_cols * lax.axis_size("gy"))
    inner = jnp.where(row_ok[:, None] & col_ok[None, :], inner, 0.0)
    return neighbours(inner)


def level_op(values, weight, level):
    return 4.0 * values + weight * bilaplace(values) / 16.0**level


def vcycle(right, weight, level):
    diag = 4.0 + 20.0 * weight / 16.0**level
    guess = 0.5 * right / diag
    if level == LEVELS - 1:
        return guess + 0.5 * (right - level_op(guess, weight, level)) / diag
    leftover = right - level_op(guess, weight, level)
    rows_now, cols_now = leftover.shape
    coarse = leftover.reshape(rows_now // 2, 2, cols_now // 2, 2).sum(axis=(1, 3)) * 0.25
    correction = vcycle(coarse, weight, level + 1)
    guess = guess + jnp.repeat(jnp.repeat(correction, 2, axis=0), 2, axis=1)
    return guess + 0.5 * (right - level_op(guess, weight, level)) / diag


def global_sum(values):
    return lax.psum(jnp.sum(values), ("layer", "gx", "gy"))


def shards(rhs, start, valid, reg, shifts, frac):
    width = SHIFT_MAX + 1
    layer_index = lax.axis_index("layer")
    layer_count = lax.axis_size("layer")
    tile_rows, tile_cols = (rhs.shape[1], rhs.shape[2])
    own_shift = lax.dynamic_index_in_dim(shifts, layer_index, 1, keepdims=False)
    own_frac = lax.dynamic_index_in_dim(frac, layer_index, 1, keepdims=False)
    weight = reg[0]
    share_rows = GUIDES // layer_count

    def footprints(padded_x, begin_at):
        planes = []
        for offset_row in range(share_rows * lax.axis_size("layer")):
            guide = begin_at + offset_row
            planes.append(
                interp(
                    padded_x,
                    lax.dynamic_index_in_dim(own_shift, guide, 0, keepdims=False),
                    lax.dynamic_index_in_dim(own_frac, guide, 0, keepdims=False),
                    1,
                    tile_rows,
                    tile_cols,
                )
            )
        return jnp.stack(planes)

    def add_back(summed, pieces, begin_at):
        for offset_row in range(pieces.shape[0]):
            guide = begin_at + offset_row
            summed = summed + interp(
                pieces[offset_row],
                lax.dynamic_index_in_dim(own_shift, guide, 0, keepdims=False),
                lax.dynamic_index_in_dim(own_frac, guide, 0, keepdims=False),
                -1,
                tile_rows,
                tile_cols,
            )
        return summed

    def operator_a(field):
        padded_x = extended(field, (("gx", 0), ("gy", 1)), width)
        empty = jnp.zeros((tile_rows, tile_cols), jnp.float32)
        share = lax.psum_scatter(
            footprints(padded_x, jnp.int32(0)), "layer", scatter_dimension=0, tiled=True
        )
        own_valid = lax.dynamic_slice_in_dim(valid, layer_index * share_rows, share_rows, 0)
        measured = share * own_valid.astype(jnp.float32)
        padded_m = extended(measured, (("gx", 1), ("gy", 2)), width)
        backs = add_back(empty, lax.all_gather(padded_m, "layer", axis=0, tiled=True), jnp.int32(0))
        return backs + weight * bilaplace(field) + 0.1 * field

    solution = start[0]
    residual = rhs[0] - operator_a(solution)
    precond = vcycle(residual, weight, 0)
    direction = precond
    rz_now = global_sum(residual * precond)
    for step in range(ITERS):
        image = operator_a(direction)
        alpha = rz_now / global_sum(direction * image)
        solution = solution + alpha * direction
        residual = residual - alpha * image
        if step + 1 < ITERS:
            precond = vcycle(residual, weight, 0)
            rz_next = global_sum(residual * precond)
            direction = precond + rz_next / rz_now * direction
            rz_now = rz_next
    return (solution[None], residual[None])


def solution(mesh):
    in_specs = (
        P("layer", "gx", "gy"),
        P("layer", "gx", "gy"),
        P(None, "gx", "gy"),
        P("layer"),
        P(),
        P(),
    )
    out_specs = (P("layer", "gx", "gy"), P("layer", "gx", "gy"))
    return jax.shard_map(shards, mesh=mesh, in_specs=in_specs, out_specs=out_specs, check_vma=False)
```

profile of v0, /device:TPU:0, one launch (start us, length us, event | category | flops | bytes accessed | tf_op | source)
XLA Modules:
  0.0 619.7 jit_solution(5234667422359590248)
XLA Ops:
  8.3 4.9 collective-permute-start
  71.4 4.4 collective-permute-start.8
  98.2 4.5 collective-permute-start.10
  105.1 4.3 collective-permute-start.4
  114.0 4.7 collective-permute-done.5
  128.0 16.6 %all_gather.9 = f32[8,162,162]{2,1,0:T(8,128)S(1)} all-gather(f32[4,162,162]{2,1,0:T(8,128)S(1)} %copy.45), channel_id=1, replica_groups=mesh['layer'=2,'gx'=4,'gy'=4] {'layer'}, dimensions={0}, use_global_device_ids=true | all-gather | bytes 1259712 | tf_op jit(solution)/shard_map/all_gather | solution.py:138
  158.0 4.3 collective-permute-done.13
  169.5 5.5 reshape.972
  182.7 4.2 collective-permute-done.17
  198.8 4.2 collective-permute-done.21
  213.9 4.2 collective-permute-done.25
  229.6 4.3 collective-permute-done.29
  245.6 4.3 collective-permute-done.33
  263.1 4.3 collective-permute-done.41
  279.3 4.1 collective-permute-done.36
  283.4 4.1 collective-permute-done.37
  294.5 16.6 %all_gather.10 = f32[8,162,162]{2,1,0:T(8,128)S(1)} all-gather(f32[4,162,162]{2,1,0:T(8,128)S(1)} %copy.60), channel_id=1, replica_groups=mesh['layer'=2,'gx'=4,'gy'=4] {'layer'}, dimensions={0}, use_global_device_ids=true | all-gather | bytes 1259712 | tf_op jit(solution)/shard_map/all_gather | solution.py:138
  319.7 40.3 %all-reduce = (f32[]{:T(128)}, f32[]{:T(128)}) all-reduce(f32[]{:T(128)} %get-tuple-element.9, f32[]{:T(128)} %get-tuple-element.8), channel_id=1, replica_groups=mesh['layer'=2,'gx'=4,'gy'=4] {'layer','gx','gy'}, use_global_device_ids=true, to_apply=%region_4.5 | all-reduce | flops 2 | bytes 16 | tf_op jit(solution)/shard_map/psum | solution.py:87
  366.5 4.3 collective-permute-done.45
  378.4 5.5 reshape.978
  390.9 4.2 collective-permute-done.49
  409.0 4.2 collective-permute-done.53
  424.2 4.2 collective-permute-done.57
  439.9 4.3 collective-permute-done.61
  452.5 39.9 %psum.30 = f32[]{:T(128)} all-reduce(f32[]{:T(128)} %get-tuple-element.14), channel_id=1, replica_groups=mesh['layer'=2,'gx'=4,'gy'=4] {'layer','gx','gy'}, use_global_device_ids=true, to_apply=%region_11.12 | all-reduce | flops 1 | bytes 8 | tf_op jit(solution)/shard_map/psum | solution.py:87
  499.7 4.3 collective-permute-done.65
  506.7 4.3 collective-permute-done.67
  517.7 4.3 collective-permute-done.73
  532.5 4.8 collective-permute-done.68
  537.3 4.1 collective-permute-done.69
  547.7 16.9 %all_gather.11 = f32[8,162,162]{2,1,0:T(8,128)S(1)} all-gather(f32[4,162,162]{2,1,0:T(8,128)S(1)} %copy.73), channel_id=1, replica_groups=mesh['layer'=2,'gx'=4,'gy'=4] {'layer'}, dimensions={0}, use_global_device_ids=true | all-gather | bytes 1259712 | tf_op jit(solution)/shard_map/all_gather | solution.py:138
  570.2 40.2 %psum.31 = f32[]{:T(128)} all-reduce(f32[]{:T(128)} %get-tuple-element.12), channel_id=1, replica_groups=mesh['layer'=2,'gx'=4,'gy'=4] {'layer','gx','gy'}, use_global_device_ids=true, to_apply=%region_14.15 | all-reduce | flops 1 | bytes 8 | tf_op jit(solution)/shard_map/psum | solution.py:87
  (435 shorter events, 244.2 us)
Async XLA Ops:
  7.2 96.8 %reduce-scatter.4.cloned.1.call-start = ((), (), s32[]{:S(2)}) async-start(), calls=%async_computation.3 | async-start | bytes 786432 | tf_op jit(solution)/shard_map/reduce_scatter | solution.py:132
  8.3 49.8 %collective-permute-start = (f32[17,128]{0,1:T(8,128)S(1)}, f32[17,128]{0,1:T(8,128)S(1)}, u32[]{:S(2)}, u32[]{:S(2)}) collective-permute-start(f32[17,128]{0,1:T(8,128)S(1)} %get-tuple-element.189), channel_id=1, source_target_pairs={{0,4},{4,8},{8,12},{1,5},{5,9},{9,13},{2,6},{6,10},{10,14},{3,7},{... | collective-permute-start | bytes 26120 | tf_op jit(solution)/shard_map/ppermute | solution.py:20
  13.2 44.9 %collective-permute-start.1 = (f32[17,128]{0,1:T(8,128)S(1)}, f32[17,128]{0,1:T(8,128)S(1)}, u32[]{:S(2)}, u32[]{:S(2)}) collective-permute-start(f32[17,128]{0,1:T(8,128)S(1)} %get-tuple-element.190), channel_id=1, source_target_pairs={{4,0},{8,4},{12,8},{5,1},{9,5},{13,9},{6,2},{10,6},{14,10},{7,3},{... | collective-permute-start | bytes 26120 | tf_op jit(solution)/shard_map/ppermute | solution.py:22
  58.2 10.8 %collective-permute-start.2 = (f32[162,17]{0,1:T(8,128)S(1)}, f32[162,17]{0,1:T(8,128)S(1)}, u32[]{:S(2)}, u32[]{:S(2)}) collective-permute-start(f32[162,17]{0,1:T(8,128)S(1)} %get-tuple-element.73), channel_id=1, source_target_pairs={{0,1},{1,2},{2,3},{4,5},{5,6},{6,7},{8,9},{9,10},{10,11},{12,13},{... | collective-permute-start | bytes 33056 | tf_op jit(solution)/shard_map/ppermute | solution.py:20
  59.7 9.3 %collective-permute-start.3 = (f32[162,17]{0,1:T(8,128)S(1)}, f32[162,17]{0,1:T(8,128)S(1)}, u32[]{:S(2)}, u32[]{:S(2)}) collective-permute-start(f32[162,17]{0,1:T(8,128)S(1)} %get-tuple-element.74), channel_id=1, source_target_pairs={{1,0},{2,1},{3,2},{5,4},{6,5},{7,6},{9,8},{10,9},{11,10},{13,12},{... | collective-permute-start | bytes 33056 | tf_op jit(solution)/shard_map/ppermute | solution.py:22
  71.3 202.0 %reduce-scatter.6.cloned.1.call-start = ((), (), s32[]{:S(2)}) async-start(), calls=%async_computation.4 | async-start | bytes 786432 | tf_op jit(solution)/shard_map/reduce_scatter | solution.py:132
  71.4 26.7 %collective-permute-start.8 = (f32[2,128]{0,1:T(8,128)S(1)}, f32[2,128]{0,1:T(8,128)S(1)}, u32[]{:S(2)}, u32[]{:S(2)}) collective-permute-start(f32[2,128]{0,1:T(8,128)S(1)} %get-tuple-element.191), channel_id=1, source_target_pairs={{0,4},{4,8},{8,12},{1,5},{5,9},{9,13},{2,6},{6,10},{10,14},{3,7},{... | collective-permute-start | bytes 3080 | tf_op jit(solution)/shard_map/ppermute | solution.py:20
  75.8 22.3 %collective-permute-start.9 = (f32[2,128]{0,1:T(8,128)S(1)}, f32[2,128]{0,1:T(8,128)S(1)}, u32[]{:S(2)}, u32[]{:S(2)}) collective-permute-start(f32[2,128]{0,1:T(8,128)S(1)} %get-tuple-element.192), channel_id=1, source_target_pairs={{4,0},{8,4},{12,8},{5,1},{9,5},{13,9},{6,2},{10,6},{14,10},{7,3},{... | collective-permute-start | bytes 3080 | tf_op jit(solution)/shard_map/ppermute | solution.py:22
  98.2 12.5 %collective-permute-start.10 = (f32[132,2]{0,1:T(2,128)S(1)}, f32[132,2]{0,1:T(2,128)S(1)}, u32[]{:S(2)}, u32[]{:S(2)}) collective-permute-start(f32[132,2]{0,1:T(2,128)S(1)} %get-tuple-element.75), channel_id=1, source_target_pairs={{0,1},{1,2},{2,3},{4,5},{5,6},{6,7},{8,9},{9,10},{10,11},{12,13},{... | collective-permute-start | bytes 3176 | tf_op jit(solution)/shard_map/ppermute | solution.py:20
  102.7 8.0 %collective-permute-start.11 = (f32[132,2]{0,1:T(2,128)S(1)}, f32[132,2]{0,1:T(2,128)S(1)}, u32[]{:S(2)}, u32[]{:S(2)}) collective-permute-start(f32[132,2]{0,1:T(2,128)S(1)} %get-tuple-element.76), channel_id=1, source_target_pairs={{1,0},{2,1},{3,2},{5,4},{6,5},{7,6},{9,8},{10,9},{11,10},{13,12},{... | collective-permute-start | bytes 3176 | tf_op jit(solution)/shard_map/ppermute | solution.py:22
  105.1 8.9 %collective-permute-start.4 = (f32[4,17,128]{1,2,0:T(8,128)S(1)}, f32[4,17,128]{1,2,0:T(8,128)S(1)}, u32[]{:S(2)}, u32[]{:S(2)}) collective-permute-start(f32[4,17,128]{1,2,0:T(8,128)S(1)} %get-tuple-element.55), channel_id=1, source_target_pairs={{0,4},{4,8},{8,12},{1,5},{5,9},{9,13},{2,6},{6,10},{10,14},{3,7},{... | collective-permute-start | bytes 104456 | tf_op jit(solution)/shard_map/ppermute | solution.py:20
  109.4 9.3 %collective-permute-start.5 = (f32[4,17,128]{1,2,0:T(8,128)S(1)}, f32[4,17,128]{1,2,0:T(8,128)S(1)}, u32[]{:S(2)}, u32[]{:S(2)}) collective-permute-start(f32[4,17,128]{1,2,0:T(8,128)S(1)} %get-tuple-element.56), channel_id=1, source_target_pairs={{4,0},{8,4},{12,8},{5,1},{9,5},{13,9},{6,2},{10,6},{14,10},{7,3},{... | collective-permute-start | bytes 104456 | tf_op jit(solution)/shard_map/ppermute | solution.py:22
  156.1 6.2 collective-permute-start.13
  227.8 6.2 collective-permute-start.29
  243.7 6.2 collective-permute-start.33
  259.1 267.7 %reduce-scatter.8.cloned.1.call-start = ((), (), s32[]{:S(2)}) async-start(), calls=%async_computation.5 | async-start | bytes 786432 | tf_op jit(solution)/shard_map/reduce_scatter | solution.py:132
  261.2 6.2 collective-permute-start.41
  267.4 11.7 %collective-permute-start.42 = (f32[132,2]{0,1:T(2,128)S(1)}, f32[132,2]{0,1:T(2,128)S(1)}, u32[]{:S(2)}, u32[]{:S(2)}) collective-permute-start(f32[132,2]{0,1:T(2,128)S(1)} %get-tuple-element.67), channel_id=1, source_target_pairs={{0,1},{1,2},{2,3},{4,5},{5,6},{6,7},{8,9},{9,10},{10,11},{12,13},{... | collective-permute-start | bytes 3176 | tf_op jit(solution)/shard_map/ppermute | solution.py:20
  270.8 8.3 %collective-permute-start.43 = (f32[132,2]{0,1:T(2,128)S(1)}, f32[132,2]{0,1:T(2,128)S(1)}, u32[]{:S(2)}, u32[]{:S(2)}) collective-permute-start(f32[132,2]{0,1:T(2,128)S(1)} %get-tuple-element.68), channel_id=1, source_target_pairs={{1,0},{2,1},{3,2},{5,4},{6,5},{7,6},{9,8},{10,9},{11,10},{13,12},{... | collective-permute-start | bytes 3176 | tf_op jit(solution)/shard_map/ppermute | solution.py:22
  274.4 8.9 %collective-permute-start.36 = (f32[4,17,128]{1,2,0:T(8,128)S(1)}, f32[4,17,128]{1,2,0:T(8,128)S(1)}, u32[]{:S(2)}, u32[]{:S(2)}) collective-permute-start(f32[4,17,128]{1,2,0:T(8,128)S(1)} %get-tuple-element.53), channel_id=1, source_target_pairs={{0,4},{4,8},{8,12},{1,5},{5,9},{9,13},{2,6},{6,10},{10,14},{3,7},{... | collective-permute-start | bytes 104456 | tf_op jit(solution)/shard_map/ppermute | solution.py:20
  277.8 9.7 %collective-permute-start.37 = (f32[4,17,128]{1,2,0:T(8,128)S(1)}, f32[4,17,128]{1,2,0:T(8,128)S(1)}, u32[]{:S(2)}, u32[]{:S(2)}) collective-permute-start(f32[4,17,128]{1,2,0:T(8,128)S(1)} %get-tuple-element.54), channel_id=1, source_target_pairs={{4,0},{8,4},{12,8},{5,1},{9,5},{13,9},{6,2},{10,6},{14,10},{7,3},{... | collective-permute-start | bytes 104456 | tf_op jit(solution)/shard_map/ppermute | solution.py:22
  364.6 6.2 collective-permute-start.45
  372.2 5.6 collective-permute-start.47
  438.0 6.2 collective-permute-start.61
  493.9 5.8 collective-permute-start.64
  497.8 6.2 collective-permute-start.65
  505.3 5.6 collective-permute-start.67
  515.8 6.2 collective-permute-start.73
  522.1 10.3 %collective-permute-start.74 = (f32[132,2]{0,1:T(2,128)S(1)}, f32[132,2]{0,1:T(2,128)S(1)}, u32[]{:S(2)}, u32[]{:S(2)}) collective-permute-start(f32[132,2]{0,1:T(2,128)S(1)} %get-tuple-element.59), channel_id=1, source_target_pairs={{0,1},{1,2},{2,3},{4,5},{5,6},{6,7},{8,9},{9,10},{10,11},{12,13},{... | collective-permute-start | bytes 3176 | tf_op jit(solution)/shard_map/ppermute | solution.py:20
  525.5 6.9 %collective-permute-start.75 = (f32[132,2]{0,1:T(2,128)S(1)}, f32[132,2]{0,1:T(2,128)S(1)}, u32[]{:S(2)}, u32[]{:S(2)}) collective-permute-start(f32[132,2]{0,1:T(2,128)S(1)} %get-tuple-element.60), channel_id=1, source_target_pairs={{1,0},{2,1},{3,2},{5,4},{6,5},{7,6},{9,8},{10,9},{11,10},{13,12},{... | collective-permute-start | bytes 3176 | tf_op jit(solution)/shard_map/ppermute | solution.py:22
  528.0 9.3 %collective-permute-start.68 = (f32[4,17,128]{1,2,0:T(8,128)S(1)}, f32[4,17,128]{1,2,0:T(8,128)S(1)}, u32[]{:S(2)}, u32[]{:S(2)}) collective-permute-start(f32[4,17,128]{1,2,0:T(8,128)S(1)} %get-tuple-element.51), channel_id=1, source_target_pairs={{0,4},{4,8},{8,12},{1,5},{5,9},{9,13},{2,6},{6,10},{10,14},{3,7},{... | collective-permute-start | bytes 104456 | tf_op jit(solution)/shard_map/ppermute | solution.py:20
  531.0 10.3 %collective-permute-start.69 = (f32[4,17,128]{1,2,0:T(8,128)S(1)}, f32[4,17,128]{1,2,0:T(8,128)S(1)}, u32[]{:S(2)}, u32[]{:S(2)}) collective-permute-start(f32[4,17,128]{1,2,0:T(8,128)S(1)} %get-tuple-element.52), channel_id=1, source_target_pairs={{4,0},{8,4},{12,8},{5,1},{9,5},{13,9},{6,2},{10,6},{14,10},{7,3},{... | collective-permute-start | bytes 104456 | tf_op jit(solution)/shard_map/ppermute | solution.py:22
  (52 other events, 320.5 us)
Sparse Core Ops, SparseCore 0:
  71.4 19.6 reduce-scatter.3
  259.2 14.0 reduce-scatter.5
  513.3 13.1 reduce-scatter.7
where the time goes:
time: 624 us; the launch traced here: 620 us
  blocking collectives  171 us (27%)
  starting transfers between devices  157 us (25%)
  waiting for transfers between devices  134 us (21%)
  between operations  90.7 us (15%)
  local copies, waits for them, and re-layouts  41.1 us (7%)
  other arithmetic  26.1 us (4%)
    psum x3, blocking collectives, global_sum(): return lax.psum(jnp.sum(values), ('layer', 'gx', 'gy'))  120 us
    ppermute x38, waiting for transfers between devices, extended(): lax.ppermute(head, axis, [((i + 1) % count, i) for i in range(ends)])  116 us
    ppermute x38, starting transfers between devices, extended(): lax.ppermute(tail, axis, [(i, (i + 1) % count) for i in range(ends)])  107 us
    all_gather x3, blocking collectives, operator_a(): lax.all_gather(padded_m, 'layer', axis=0, tiled=True)  50.2 us
    ppermute x38, starting transfers between devices, extended(): lax.ppermute(head, axis, [((i + 1) % count, i) for i in range(ends)])  49.5 us
    unnamed x111, local copies, waits for them, and re-layouts  17 us
    ppermute x38, waiting for transfers between devices, extended(): lax.ppermute(tail, axis, [(i, (i + 1) % count) for i in range(ends)])  16.8 us
    reshape x4, local copies, waits for them, and re-layouts, vcycle(): leftover.reshape(rows_now // 2, 2, cols_now // 2, 2).sum(axis=(1, 3)) * 0.25  13.2 us
  transfers between devices with their start and end apart: 79, of which 44 were waited for; matrix products, arithmetic and copies ran while one was open for 1% of the time, Pallas kernels for 0%

commit v1 on v0

v1 whole, which is shorter than its diff:
```python
import functools

import jax
import jax.numpy as jnp
from jax import lax
from jax.experimental import pallas as pl
from jax.experimental.pallas import tpu as pltpu
from jax.sharding import PartitionSpec as P

GUIDES = 8
SHIFT_MAX = 16
LANES = 128
HALF = LANES // 2
QUART = LANES // 4
VROWS = 72
F32 = jnp.float32
BF16 = jnp.bfloat16
DOT = functools.partial(jnp.dot, preferred_element_type=F32)


def lane_iota(shape=(1, LANES)):
    return lax.broadcasted_iota(jnp.int32, shape, len(shape) - 1)


def roll(x, amount):
    amount = amount % LANES if isinstance(amount, int) else amount & (LANES - 1)
    if isinstance(amount, int) and amount == 0:
        return x
    return pltpu.roll(x, amount, x.ndim - 1)


def spans(low, high, size):
    return [(r, min(size, high - r)) for r in range(low, high, size)]


def order_matrix(inverse):
    source = lax.broadcasted_iota(jnp.int32, (LANES, LANES), 0)
    target = lax.broadcasted_iota(jnp.int32, (LANES, LANES), 1)
    if inverse:
        source, target = target, source
    wanted = 2 * (target & (HALF - 1)) + (target >= HALF).astype(jnp.int32)
    return (source == wanted).astype(F32).astype(BF16)


def exact_dot(values, matrix):
    high = values.astype(BF16)
    rest = values - high.astype(F32)
    mid = rest.astype(BF16)
    low = (rest - mid.astype(F32)).astype(BF16)
    return DOT(high, matrix) + (DOT(mid, matrix) + DOT(low, matrix))


def pack_inputs(start_ref, rhs_ref, valid_ref, reg_ref, xr_ref, own_ref, up_ref, down_ref):
    rows = start_ref.shape[1]
    matrix = order_matrix(False)
    xr_ref[pl.ds(0, rows), :] = exact_dot(start_ref[0], matrix)
    xr_ref[pl.ds(rows, rows), :] = exact_dot(rhs_ref[0], matrix)
    xr_ref[pl.ds(2 * rows, 8), :] = jnp.full((8, LANES), reg_ref[0], F32)
    for g in range(valid_ref.shape[0]):
        plane = DOT(valid_ref[g].astype(F32).astype(BF16), matrix)
        own_ref[g] = plane
        up_ref[pl.ds(g * VROWS, VROWS), :] = plane[:VROWS]
        down_ref[pl.ds(g * VROWS, VROWS), :] = plane[rows - VROWS :]


def pair_strips(first, second):
    keep = (lane_iota() & (HALF - 1)) < QUART
    left = jnp.where(keep, first, roll(second, QUART))
    right = jnp.where(keep, roll(first, -QUART), second)
    return left, right


def pack_pairs(meta_ref, parts, out_left, out_right, base, halo, rows):
    top_ok = meta_ref[0].astype(F32)
    bottom_ok = meta_ref[1].astype(F32)
    total = rows + 2 * halo
    for k in range((len(parts) + 1) // 2):
        pair = (parts[2 * k], parts[min(2 * k + 1, len(parts) - 1)])
        for at, low, high, which, scale in (
            (0, 0, halo, 0, top_ok),
            (halo, 0, rows, 1, None),
            (halo + rows, 0, halo, 2, bottom_ok),
        ):
            for r, n in spans(low, high, 32):
                first, second = (part[which](r, n) for part in pair)
                left, right = pair_strips(first, second)
                if scale is not None:
                    left, right = left * scale, right * scale
                out_left[pl.ds(base + k * total + at + r, n), :] = left
                out_right[pl.ds(base + k * total + at + r, n), :] = right
    return base + ((len(parts) + 1) // 2) * total


def rows_of(ref, start):
    return lambda r, n: ref[pl.ds(start + r, n), :]


def planes_of(meta_ref, part, position, left_of, right_of, halo, rows):
    top_ok = meta_ref[0].astype(F32)
    bottom_ok = meta_ref[1].astype(F32)
    left_ok = meta_ref[2].astype(F32)
    right_ok = meta_ref[3].astype(F32)
    lane = lane_iota()
    for at, count, which, scale in ((0, halo, 0, top_ok), (halo, rows, 1, None), (halo + rows, halo, 2, bottom_ok)):
        for r, n in spans(0, count, 32):
            own = part[which](r, n)
            if scale is not None:
                own = own * scale
            left = left_of(at + r, n) * left_ok
            right = right_of(at + r, n) * right_ok
            back = QUART * position
            even = jnp.where(
                lane < QUART,
                roll(left, -back),
                jnp.where(lane < 3 * QUART, roll(own, QUART), roll(right, 3 * QUART - back)),
            )
            odd = jnp.where(
                lane < QUART,
                roll(left, HALF - back),
                jnp.where(lane < 3 * QUART, roll(own, -QUART), roll(right, QUART - back)),
            )
            yield at + r - halo, n, even, odd


def five_point(ref, at, n):
    even, odd = ref[0, pl.ds(at, n), :], ref[1, pl.ds(at, n), :]
    sum_even = ref[0, pl.ds(at - 1, n), :] + ref[0, pl.ds(at + 1, n), :] + (odd + roll(odd, 1))
    sum_odd = ref[1, pl.ds(at - 1, n), :] + ref[1, pl.ds(at + 1, n), :] + (even + roll(even, -1))
    return sum_even - 4.0 * even, sum_odd - 4.0 * odd, even, odd


def five_coarse(ref, at, n, step):
    here = ref[pl.ds(at, n), :]
    sides = roll(here, step) + roll(here, -step)
    return ref[pl.ds(at - 1, n), :] + ref[pl.ds(at + 1, n), :] + sides - 4.0 * here, here


def mask_rows(meta_ref, row_at, n, rows):
    top_ok = meta_ref[0].astype(F32)
    bottom_ok = meta_ref[1].astype(F32)
    left_ok = meta_ref[2].astype(F32)
    right_ok = meta_ref[3].astype(F32)
    row = row_at + lax.broadcasted_iota(jnp.int32, (n, LANES), 0)
    lane = lane_iota((n, LANES))
    by_row = jnp.where(row < 0, top_ok, jnp.where(row >= rows, bottom_ok, 1.0))
    return by_row * jnp.where(lane < QUART, left_ok, jnp.where(lane >= 3 * QUART, right_ok, 1.0))


def guide_loop(meta_ref, shifts_ref, frac_ref, x_ref, x_base, valid_ref, m_ref, m_base, acc_ref, acc_base, p_rows, outs, slots, out_slots, square_ref=None, rows=None):
    count = slots

    def coefficients(g, slot):
        layer = lax.rem(meta_ref[4] - slot + count, count)
        at = (g * count + layer) * 2
        return (
            shifts_ref[at],
            shifts_ref[at + 1],
            frac_ref[at].astype(F32) * (1.0 / 256.0),
            frac_ref[at + 1].astype(F32) * (1.0 / 256.0),
        )

    def taps(ref, index, at, u, odd, column, n, step):
        first = pl.ds(at, n)
        second = pl.ds(at + step, n)
        here = ref[index + (odd, first, slice(None))]
        plane_a = here + u * (ref[index + (odd, second, slice(None))] - here)
        here = ref[index + (1 - odd, first, slice(None))]
        plane_b = here + u * (ref[index + (1 - odd, second, slice(None))] - here)
        return (
            roll(plane_a, LANES - column),
            roll(plane_b, LANES - column - odd),
            roll(plane_a, LANES - column - 1),
        )

    def body(g, carry):
        fixed = []
        for slot in range(count):
            a, b, u, v = coefficients(g, slot)
            fixed.append((a, u, v, b & 1, lax.shift_right_arithmetic(b, 1)))
        for r, n in spans(*p_rows, 16):
            even = odd = None
            for slot in range(count):
                a, u, v, parity, column = fixed[slot]
                q0, q1, q2 = taps(x_ref, (slot,), r + x_base + a, u, parity, column, n, 1)
                this_even = q0 + v * (q1 - q0)
                this_odd = q1 + v * (q2 - q1)
                even = this_even if even is None else even + this_even
                odd = this_odd if odd is None else odd + this_odd
            m_even = even * valid_ref[g, 0, pl.ds(r + VROWS, n), :]
            m_odd = odd * valid_ref[g, 1, pl.ds(r + VROWS, n), :]
            m_ref[0, pl.ds(r + m_base, n), :] = m_even
            m_ref[1, pl.ds(r + m_base, n), :] = m_odd
            if square_ref is not None:
                for k in range(0, n, 8):
                    if 0 <= r + k < rows:
                        sl = slice(k, k + 8)
                        square_ref[...] += m_even[sl] * even[sl] + m_odd[sl] * odd[sl]
        for slot in range(out_slots):
            a, b, u, v = coefficients(g, slot)
            back = -b - 1
            parity, column = back & 1, lax.shift_right_arithmetic(back, 1)
            for r, n in spans(*outs, 16):
                q0, q1, q2 = taps(m_ref, (), r + m_base - a, u, parity, column, n, -1)
                acc_ref[slot, 0, pl.ds(r + acc_base, n), :] += q1 + v * (q0 - q1)
                acc_ref[slot, 1, pl.ds(r + acc_base, n), :] += q2 + v * (q1 - q2)
        return carry

    lax.fori_loop(0, valid_ref.shape[0], body, 0)


def zero_rows(ref, index, ranges):
    for low, high in ranges:
        if high > low:
            ref[index + (pl.ds(low, high - low), slice(None))] = jnp.zeros((high - low, LANES), F32)


def clear_planes(ref, index):
    for plane in range(2):
        for r, n in spans(0, ref.shape[-2], 64):
            ref[index + (plane, pl.ds(r, n), slice(None))] = jnp.zeros((n, LANES), F32)


def vcycle(h_ref, out_ref, weight, depth, rows, masks, work):
    g_ref, w_ref, t_ref, h1, g1, w1, t1, h2, g2 = work
    mask0, mask1, mask2 = masks
    size0 = rows + 2 * depth
    size1, size2 = size0 // 2, size0 // 4
    lane = lane_iota()
    s0 = 0.5 / (4.0 + 20.0 * weight)
    weight1, weight2 = weight * (1.0 / 16.0), weight * (1.0 / 256.0)
    s1 = 0.5 / (4.0 + 20.0 * weight1)
    s2 = 0.5 / (4.0 + 20.0 * weight2)

    for r, n in spans(8, 8 + size0, 16):
        lap_even, lap_odd, _, _ = five_point(h_ref, r, n)
        mask = mask0[pl.ds(r, n), :]
        g_ref[0, pl.ds(r, n), :] = mask * lap_even
        g_ref[1, pl.ds(r, n), :] = mask * lap_odd
    for r, n in spans(8, 8 + size0, 16):
        bi_even, bi_odd, _, _ = five_point(g_ref, r, n)
        h_both = h_ref[0, pl.ds(r, n), :] + h_ref[1, pl.ds(r, n), :]
        t_ref[pl.ds(r, n), :] = mask0[pl.ds(r, n), :] * (
            h_both - s0 * (4.0 * h_both + weight * (bi_even + bi_odd))
        )
    h1[pl.ds(8, size1), :] = 0.25 * (t_ref[pl.ds(8, size1, stride=2), :] + t_ref[pl.ds(9, size1, stride=2), :])
    for r, n in spans(8, 8 + size1, 32):
        lap, _ = five_coarse(h1, r, n, 1)
        g1[pl.ds(r, n), :] = mask1[pl.ds(r, n), :] * lap
    for r, n in spans(8, 8 + size1, 32):
        bi, _ = five_coarse(g1, r, n, 1)
        here = h1[pl.ds(r, n), :]
        t1[pl.ds(r, n), :] = mask1[pl.ds(r, n), :] * (here - s1 * (4.0 * here + weight1 * bi))
    both = t1[pl.ds(8, size2, stride=2), :] + t1[pl.ds(9, size2, stride=2), :]
    h2[pl.ds(8, size2), :] = 0.25 * (both + jnp.where((lane & 1) == 0, roll(both, -1), roll(both, 1)))
    lap, _ = five_coarse(h2, 8, size2, 2)
    g2[pl.ds(8, size2), :] = mask2[pl.ds(8, size2), :] * lap
    bi, _ = five_coarse(g2, 8, size2, 2)
    here = h2[pl.ds(8, size2), :]
    e2 = mask2[pl.ds(8, size2), :] * (s2 * (2.0 * here - s2 * (4.0 * here + weight2 * bi)))
    t1[pl.ds(8, size2, stride=2), :] = e2
    t1[pl.ds(9, size2, stride=2), :] = e2
    for r, n in spans(8, 8 + size1, 32):
        w1[pl.ds(r, n), :] = s1 * h1[pl.ds(r, n), :] + t1[pl.ds(r, n), :]
    for r, n in spans(8, 8 + size1, 32):
        lap, _ = five_coarse(w1, r, n, 1)
        g1[pl.ds(r, n), :] = mask1[pl.ds(r, n), :] * lap
    for r, n in spans(8, 8 + size1, 32):
        bi, _ = five_coarse(g1, r, n, 1)
        here = w1[pl.ds(r, n), :]
        t1[pl.ds(r, n), :] = mask1[pl.ds(r, n), :] * (
            here + s1 * (h1[pl.ds(r, n), :] - 4.0 * here - weight1 * bi)
        )
    e1 = t1[pl.ds(8, size1), :]
    t_ref[pl.ds(8, size1, stride=2), :] = e1
    t_ref[pl.ds(9, size1, stride=2), :] = e1
    for r, n in spans(8, 8 + size0, 16):
        copied = t_ref[pl.ds(r, n), :]
        for plane in range(2):
            w_ref[plane, pl.ds(r, n), :] = s0 * h_ref[plane, pl.ds(r, n), :] + copied
    for r, n in spans(8, 8 + size0, 16):
        lap_even, lap_odd, _, _ = five_point(w_ref, r, n)
        mask = mask0[pl.ds(r, n), :]
        g_ref[0, pl.ds(r, n), :] = mask * lap_even
        g_ref[1, pl.ds(r, n), :] = mask * lap_odd
    for r, n in spans(8, 8 + size0, 16):
        bi = five_point(g_ref, r, n)[:2]
        mask = mask0[pl.ds(r, n), :]
        for plane in range(2):
            here = w_ref[plane, pl.ds(r, n), :]
            out_ref[plane, pl.ds(r, n), :] = mask * (
                here + s0 * (h_ref[plane, pl.ds(r, n), :] - 4.0 * here - weight * bi[plane])
            )


def vcycle_scratch(depth, rows):
    size0 = rows + 2 * depth
    one = lambda size: pltpu.VMEM((size + 16, LANES), F32)
    two = pltpu.VMEM((2, size0 + 16, LANES), F32)
    size1, size2 = size0 // 2, size0 // 4
    work = [two, two, one(size0), one(size1), one(size1), one(size1), one(size1), one(size2), one(size2)]
    return work, [one(size0), one(size1), one(size2)]


def prepare_vcycle(meta_ref, depth, rows, masks, work):
    size0 = rows + 2 * depth
    sizes = (size0, size0 // 2, size0 // 4)
    for level, (mask, size) in enumerate(zip(masks, sizes)):
        for r, n in spans(0, size + 16, 64):
            mask[pl.ds(r, n), :] = mask_rows(meta_ref, r - 8 - (depth >> level), n, rows >> level)
    g_ref, w_ref, t_ref, h1, g1, w1, t1, h2, g2 = work
    for ref in (g_ref, w_ref):
        for plane in range(2):
            zero_rows(ref, (plane,), ((0, 8), (size0 + 8, size0 + 16)))
    for ref, size in ((h1, sizes[1]), (g1, sizes[1]), (w1, sizes[1]), (h2, sizes[2]), (g2, sizes[2])):
        zero_rows(ref, (), ((0, 8), (size + 8, size + 16)))


def bilaplace_into(x_ref, x_base, g_ref, low, high, mask_of):
    for r, n in spans(low - 8, high + 8, 16):
        lap_even, lap_odd, _, _ = five_point(x_ref, r + x_base, n)
        mask = mask_of(r, n)
        g_ref[0, pl.ds(r - low + 8, n), :] = mask * lap_even
        g_ref[1, pl.ds(r - low + 8, n), :] = mask * lap_odd


def tile_of(even, odd):
    return jnp.where(lane_iota() < HALF, roll(even, -QUART), roll(odd, QUART))


def fold(values):
    total = values[0:8]
    for k in range(8, values.shape[0], 8):
        total = total + values[k : k + 8]
    return total


def inner_mask():
    lane = lane_iota()
    return ((lane >= QUART) & (lane < 3 * QUART)).astype(F32)


X_HALO, R_HALO, Z_HALO = 56, 24, 88
DEPTH1, DEPTH2 = 24, 56
Y_HALO = 40


def first_parts(xr_refs, top_ref, bottom_ref, rows, what):
    halo, skip = (X_HALO, 0) if what == 0 else (R_HALO, X_HALO)
    parts = []
    for k, ref in enumerate(xr_refs):
        at = k * (X_HALO + R_HALO) + skip
        parts.append((rows_of(top_ref, at), rows_of(ref, what * rows), rows_of(bottom_ref, at)))
    return parts


def pack_first(slots, rows, meta_ref, *refs):
    xr_refs, (top_ref, bottom_ref, left_ref, right_ref) = refs[:slots], refs[slots:]
    base = pack_pairs(
        meta_ref, first_parts(xr_refs, top_ref, bottom_ref, rows, 0), left_ref, right_ref, 0, X_HALO, rows
    )
    pack_pairs(
        meta_ref, first_parts(xr_refs, top_ref, bottom_ref, rows, 1), left_ref, right_ref, base, R_HALO, rows
    )


def valid_parts(own_ref, top_ref, bottom_ref):
    return [
        (
            rows_of(top_ref, g * VROWS),
            (lambda g: lambda r, n: own_ref[g, pl.ds(r, n), :])(g),
            rows_of(bottom_ref, g * VROWS),
        )
        for g in range(own_ref.shape[0])
    ]


def pack_valid(meta_ref, own_ref, top_ref, bottom_ref, left_ref, right_ref):
    pack_pairs(
        meta_ref, valid_parts(own_ref, top_ref, bottom_ref), left_ref, right_ref, 0, VROWS, own_ref.shape[1]
    )


def spread_valid(meta_ref, own_ref, top_ref, bottom_ref, left_ref, right_ref, out_ref):
    rows = own_ref.shape[1]
    total = rows + 2 * VROWS
    for g, part in enumerate(valid_parts(own_ref, top_ref, bottom_ref)):
        base = (g // 2) * total
        for r, n, even, odd in planes_of(
            meta_ref, part, g % 2, rows_of(left_ref, base), rows_of(right_ref, base), VROWS, rows
        ):
            out_ref[g, 0, pl.ds(r + VROWS, n), :] = even
            out_ref[g, 1, pl.ds(r + VROWS, n), :] = odd


def stage_first(slots, rows, meta_ref, shifts_ref, frac_ref, *refs):
    xr_refs, refs = refs[:slots], refs[slots:]
    top_ref, bottom_ref, left_ref, right_ref, valid_ref = refs[:5]
    z_ref, up_ref, down_ref, res_ref, dot_ref = refs[5:10]
    x_ref, m_ref, acc_ref, z_planes, *rest = refs[10:]
    work, masks = rest[:9], rest[9:12]
    x_base, m_base, acc_base = X_HALO + 8, 48, DEPTH1 + 8
    prepare_vcycle(meta_ref, DEPTH1, rows, masks, work)
    total = rows + 2 * X_HALO
    for k, part in enumerate(first_parts(xr_refs, top_ref, bottom_ref, rows, 0)):
        base = (k // 2) * total
        for r, n, even, odd in planes_of(
            meta_ref, part, k % 2, rows_of(left_ref, base), rows_of(right_ref, base), X_HALO, rows
        ):
            x_ref[k, 0, pl.ds(r + x_base, n), :] = even
            x_ref[k, 1, pl.ds(r + x_base, n), :] = odd
        for plane in range(2):
            zero_rows(x_ref, (k, plane), ((0, 8), (total + 8, total + 16)))
        clear_planes(acc_ref, (k,))
    for plane in range(2):
        zero_rows(m_ref, (plane,), ((0, 8), (rows + 88, rows + 96)))
    guide_loop(
        meta_ref, shifts_ref, frac_ref, x_ref, x_base, valid_ref, m_ref, m_base, acc_ref, acc_base,
        (-40, rows + 40), (-DEPTH1, rows + DEPTH1), slots, slots,
    )
    first_total = ((slots + 1) // 2) * total
    total_r = rows + 2 * R_HALO
    g_ref = work[0]
    dot_ref[...] = jnp.zeros((8, LANES), F32)
    inner = inner_mask()
    for k, part in enumerate(first_parts(xr_refs, top_ref, bottom_ref, rows, 1)):
        weight = xr_refs[k][pl.ds(2 * rows, 1), :]
        bilaplace_into(
            x_ref.at[k], x_base, g_ref, -DEPTH1, rows + DEPTH1,
            lambda r, n: masks[0][pl.ds(r + DEPTH1 + 8, n), :],
        )
        base = first_total + (k // 2) * total_r
        h_ref = acc_ref.at[k]
        for r, n, even, odd in planes_of(
            meta_ref, part, k % 2, rows_of(left_ref, base), rows_of(right_ref, base), R_HALO, rows
        ):
            at = r + DEPTH1 + 8
            bi = five_point(g_ref, at, n)[:2]
            mask = masks[0][pl.ds(at, n), :]
            for plane, right in enumerate((even, odd)):
                h_ref[plane, pl.ds(at, n), :] = mask * (
                    right
                    - acc_ref[k, plane, pl.ds(at, n), :]
                    - weight * bi[plane]
                    - 0.1 * x_ref[k, plane, pl.ds(r + x_base, n), :]
                )
        for plane in range(2):
            zero_rows(g_ref, (plane,), ((0, 8), (rows + 2 * DEPTH1 + 8, rows + 2 * DEPTH1 + 16)))
        vcycle(h_ref, z_planes, weight, DEPTH1, rows, masks, work)
        for r, n in spans(0, rows, 32):
            at = r + DEPTH1 + 8
            res = h_ref[0, pl.ds(at, n), :], h_ref[1, pl.ds(at, n), :]
            z = z_planes[0, pl.ds(at, n), :], z_planes[1, pl.ds(at, n), :]
            dot_ref[...] += inner * fold(res[0] * z[0] + res[1] * z[1])
            z_ref[k, pl.ds(r, n), :] = tile_of(*z)
            if k == 0:
                res_ref[pl.ds(r, n), :] = tile_of(*res)
        up_ref[pl.ds(k * Z_HALO, Z_HALO), :] = z_ref[k, pl.ds(0, Z_HALO), :]
        down_ref[pl.ds(k * Z_HALO, Z_HALO), :] = z_ref[k, pl.ds(rows - Z_HALO, Z_HALO), :]


def second_parts(z_ref, top_ref, bottom_ref):
    return [
        (
            rows_of(top_ref, k * Z_HALO),
            (lambda k: lambda r, n: z_ref[k, pl.ds(r, n), :])(k),
            rows_of(bottom_ref, k * Z_HALO),
        )
        for k in range(z_ref.shape[0])
    ]


def pack_second(meta_ref, z_ref, top_ref, bottom_ref, left_ref, right_ref):
    pack_pairs(
        meta_ref, second_parts(z_ref, top_ref, bottom_ref), left_ref, right_ref, 0, Z_HALO, z_ref.shape[1]
    )


def stage_second(slots, rows, meta_ref, shifts_ref, frac_ref, *refs):
    xr_refs, refs = refs[:slots], refs[slots:]
    z_ref, top_ref, bottom_ref, left_ref, right_ref, valid_ref = refs[:6]
    y_ref, out_left, out_right, image_ref, dot_zq, dot_yq = refs[6:12]
    x_ref, m_ref, acc_ref, y_planes, *rest = refs[12:]
    work, masks = rest[:9], rest[9:12]
    x_base, m_base, acc_base = Z_HALO, 80, DEPTH2 + 8
    prepare_vcycle(meta_ref, DEPTH2, rows, masks, work)
    total = rows + 2 * Z_HALO
    for k, part in enumerate(second_parts(z_ref, top_ref, bottom_ref)):
        base = (k // 2) * total
        for r, n, even, odd in planes_of(
            meta_ref, part, k % 2, rows_of(left_ref, base), rows_of(right_ref, base), Z_HALO, rows
        ):
            x_ref[k, 0, pl.ds(r + x_base, n), :] = even
            x_ref[k, 1, pl.ds(r + x_base, n), :] = odd
        for plane in range(2):
            zero_rows(x_ref, (k, plane), ((total, total + 8),))
        clear_planes(acc_ref, (k,))
    for plane in range(2):
        zero_rows(m_ref, (plane,), ((0, 8), (rows + 152, rows + 160)))
    guide_loop(
        meta_ref, shifts_ref, frac_ref, x_ref, x_base, valid_ref, m_ref, m_base, acc_ref, acc_base,
        (-VROWS, rows + VROWS), (-DEPTH2, rows + DEPTH2), slots, slots,
    )
    g_ref = work[0]
    dot_zq[...] = jnp.zeros((8, LANES), F32)
    dot_yq[...] = jnp.zeros((8, LANES), F32)
    inner = inner_mask()
    for k in range(slots):
        weight = xr_refs[k][pl.ds(2 * rows, 1), :]
        bilaplace_into(
            x_ref.at[k], x_base, g_ref, -DEPTH2, rows + DEPTH2,
            lambda r, n: masks[0][pl.ds(r + DEPTH2 + 8, n), :],
        )
        h_ref = acc_ref.at[k]
        for r, n in spans(-DEPTH2, rows + DEPTH2, 16):
            at = r + DEPTH2 + 8
            bi = five_point(g_ref, at, n)[:2]
            mask = masks[0][pl.ds(at, n), :]
            for plane in range(2):
                h_ref[plane, pl.ds(at, n), :] = mask * (
                    acc_ref[k, plane, pl.ds(at, n), :]
                    + weight * bi[plane]
                    + 0.1 * x_ref[k, plane, pl.ds(r + x_base, n), :]
                )
        for plane in range(2):
            zero_rows(g_ref, (plane,), ((0, 8), (rows + 2 * DEPTH2 + 8, rows + 2 * DEPTH2 + 16)))
        vcycle(h_ref, y_planes.at[k], weight, DEPTH2, rows, masks, work)
        for r, n in spans(0, rows, 32):
            at = r + DEPTH2 + 8
            q = h_ref[0, pl.ds(at, n), :], h_ref[1, pl.ds(at, n), :]
            y = y_planes[k, 0, pl.ds(at, n), :], y_planes[k, 1, pl.ds(at, n), :]
            z = x_ref[k, 0, pl.ds(r + x_base, n), :], x_ref[k, 1, pl.ds(r + x_base, n), :]
            dot_zq[...] += inner * fold(z[0] * q[0] + z[1] * q[1])
            dot_yq[...] += inner * fold(y[0] * q[0] + y[1] * q[1])
            if k == 0:
                image_ref[pl.ds(r, n), :] = tile_of(*q)
        for r, n in spans(-Y_HALO, rows + Y_HALO, 16):
            for plane in range(2):
                y_ref[k, plane, pl.ds(r + Y_HALO, n), :] = y_planes[k, plane, pl.ds(r + DEPTH2 + 8, n), :]
    lane = lane_iota()
    total_y = rows + 2 * Y_HALO
    for pair in range((slots + 1) // 2):
        first, second = 2 * pair, min(2 * pair + 1, slots - 1)
        for r, n in spans(0, total_y, 16):
            e0, o0 = y_ref[first, 0, pl.ds(r, n), :], y_ref[first, 1, pl.ds(r, n), :]
            e1, o1 = y_ref[second, 0, pl.ds(r, n), :], y_ref[second, 1, pl.ds(r, n), :]
            out_left[pl.ds(pair * total_y + r, n), :] = jnp.where(
                lane < HALF,
                jnp.where(lane < QUART, roll(e0, -QUART), e1),
                jnp.where(lane < 3 * QUART, roll(o0, QUART), roll(o1, HALF)),
            )
            out_right[pl.ds(pair * total_y + r, n), :] = jnp.where(
                lane < HALF,
                jnp.where(lane < QUART, roll(e0, HALF), roll(e1, -QUART)),
                jnp.where(lane < 3 * QUART, o0, roll(o1, QUART)),
            )


def stage_third(slots, rows, meta_ref, shifts_ref, frac_ref, *refs):
    xr_refs, refs = refs[:slots], refs[slots:]
    y_ref, left_ref, right_ref, valid_ref, dot_rz, dot_zq, dot_yq = refs[:7]
    image_ref, sums_ref = refs[7:9]
    x_ref, m_ref, acc_ref, g_ref, square_ref, mask_ref = refs[9:]
    x_base, m_base = Y_HALO, 24
    left_ok = meta_ref[2].astype(F32)
    right_ok = meta_ref[3].astype(F32)
    lane = lane_iota()
    total = rows + 2 * Y_HALO
    for k in range(slots):
        base = (k // 2) * total
        back = QUART * (k % 2)
        for r, n in spans(0, total, 16):
            left = left_ref[pl.ds(base + r, n), :] * left_ok
            right = right_ref[pl.ds(base + r, n), :] * right_ok
            x_ref[k, 0, pl.ds(r, n), :] = jnp.where(
                lane < QUART,
                roll(left, -back),
                jnp.where(lane < 3 * QUART, y_ref[k, 0, pl.ds(r, n), :], roll(right, 3 * QUART - back)),
            )
            x_ref[k, 1, pl.ds(r, n), :] = jnp.where(
                lane < QUART,
                roll(left, HALF - back),
                jnp.where(lane < 3 * QUART, y_ref[k, 1, pl.ds(r, n), :], roll(right, QUART - back)),
            )
        for plane in range(2):
            zero_rows(x_ref, (k, plane), ((total, total + 8),))
    clear_planes(acc_ref, (0,))
    square_ref[...] = jnp.zeros((8, LANES), F32)
    for r, n in spans(-8, rows + 8, 48):
        mask_ref[pl.ds(r + 8, n), :] = mask_rows(meta_ref, r, n, rows)
    guide_loop(
        meta_ref, shifts_ref, frac_ref, x_ref, x_base, valid_ref, m_ref, m_base, acc_ref, 0,
        (-24, rows + 24), (0, rows), slots, 1, square_ref, rows,
    )
    for k in reversed(range(slots)):
        weight = xr_refs[k][pl.ds(2 * rows, 1), :]
        bilaplace_into(x_ref.at[k], x_base, g_ref, 0, rows, lambda r, n: mask_ref[pl.ds(r + 8, n), :])
        for r, n in spans(0, rows, 16):
            x = x_ref[k, 0, pl.ds(r + x_base, n), :], x_ref[k, 1, pl.ds(r + x_base, n), :]
            bi_even, bi_odd, g_even, g_odd = five_point(g_ref, r + 8, n)
            square_ref[...] += fold(
                weight * (g_even * g_even + g_odd * g_odd) + 0.1 * (x[0] * x[0] + x[1] * x[1])
            )
            if k == 0:
                image_ref[pl.ds(r, n), :] = tile_of(
                    acc_ref[0, 0, pl.ds(r, n), :] + weight * bi_even + 0.1 * x[0],
                    acc_ref[0, 1, pl.ds(r, n), :] + weight * bi_odd + 0.1 * x[1],
                )
    row = lax.broadcasted_iota(jnp.int32, (8, LANES), 0)
    packed = jnp.zeros((8, LANES), F32)
    for at, part in enumerate((dot_rz[...], dot_zq[...], dot_yq[...], square_ref[...] * inner_mask())):
        packed = jnp.where(row == at, jnp.sum(part, axis=0, keepdims=True), packed)
    for d in range(sums_ref.shape[0]):
        sums_ref[d] = packed


def finish(start_ref, z_ref, res_ref, q_ref, y_ref, p_ref, sums_ref, solution_ref, residual_ref):
    rows = start_ref.shape[1]
    total = sums_ref[0]
    for d in range(1, sums_ref.shape[0]):
        total = total + sums_ref[d]
    total = jnp.sum(total, axis=1, keepdims=True)
    rz, zq, yq, yp = (total[k : k + 1] for k in range(4))
    alpha = rz / zq
    rz_next = alpha * alpha * yq - rz
    grown = 1.0 + rz_next / rz
    alpha_next = rz_next / (grown * grown * zq - 2.0 * alpha * grown * yq + alpha * alpha * yp)
    matrix = order_matrix(True)
    c_z = alpha + alpha_next * grown
    c_y = alpha_next * alpha
    y = tile_of(y_ref[0, 0, pl.ds(Y_HALO, rows), :], y_ref[0, 1, pl.ds(Y_HALO, rows), :])
    solution_ref[0] = start_ref[0] + exact_dot(c_z * z_ref[0] - c_y * y, matrix)
    residual_ref[0] = exact_dot(res_ref[...] - (c_z * q_ref[...] - c_y * p_ref[...]), matrix)


def call(kernel, outs, *args, scratch=(), scalars=0):
    space = lambda k: pltpu.SMEM if k < scalars else pltpu.VMEM
    shapes = [jax.ShapeDtypeStruct(shape, F32) for shape in outs]
    return pl.pallas_call(
        kernel,
        out_shape=shapes,
        in_specs=[pl.BlockSpec(memory_space=space(k)) for k in range(len(args))],
        out_specs=[pl.BlockSpec(memory_space=pltpu.VMEM)] * len(outs),
        scratch_shapes=list(scratch),
    )(*args)


def around(up, down, axis):
    n = lax.axis_size(axis)
    before = lax.ppermute(down, axis, [(i, (i + 1) % n) for i in range(n)])
    after = lax.ppermute(up, axis, [(i, (i - 1) % n) for i in range(n)])
    return before, after


def shards(rhs, start, valid, reg, shifts, frac):
    rows = rhs.shape[1]
    guides = valid.shape[0]
    slots = lax.axis_size("layer")
    gx, gy = lax.axis_index("gx"), lax.axis_index("gy")
    n_gx, n_gy = lax.axis_size("gx"), lax.axis_size("gy")
    at = jnp.arange(8, dtype=jnp.int32)
    meta = jnp.where(
        at == 4,
        lax.axis_index("layer"),
        jnp.where(
            at == 0,
            (gx > 0).astype(jnp.int32),
            jnp.where(
                at == 1,
                (gx < n_gx - 1).astype(jnp.int32),
                jnp.where(at == 2, (gy > 0).astype(jnp.int32), (gy < n_gy - 1).astype(jnp.int32)),
            ),
        ),
    )
    shifts, frac = shifts.reshape(-1), frac.reshape(-1)
    pairs = (slots + 1) // 2
    vmem = lambda *shape: pltpu.VMEM(shape, F32)

    packed = pl.pallas_call(
        pack_inputs,
        out_shape=[
            jax.ShapeDtypeStruct(shape, F32)
            for shape in ((2 * rows + 8, LANES), (guides, rows, LANES), (guides * VROWS, LANES), (guides * VROWS, LANES))
        ],
        in_specs=[pl.BlockSpec(memory_space=pltpu.VMEM)] * 3 + [pl.BlockSpec(memory_space=pltpu.SMEM)],
        out_specs=[pl.BlockSpec(memory_space=pltpu.VMEM)] * 4,
    )(start, rhs, valid, reg)
    xr, valid_own, valid_up, valid_down = packed
    xrs = [xr] + [
        lax.ppermute(xr, "layer", [(i, (i + k) % slots) for i in range(slots)]) for k in range(1, slots)
    ]
    valid_top, valid_bottom = around(valid_up, valid_down, "gx")
    up = jnp.concatenate([part for x in xrs for part in (x[:X_HALO], x[rows : rows + R_HALO])])
    down = jnp.concatenate(
        [part for x in xrs for part in (x[rows - X_HALO : rows], x[2 * rows - R_HALO : 2 * rows])]
    )
    top, bottom = around(up, down, "gx")
    strip = (pairs * (2 * rows + 2 * X_HALO + 2 * R_HALO), LANES)
    left, right = call(
        functools.partial(pack_first, slots, rows), (strip, strip), meta, *xrs, top, bottom, scalars=1
    )
    left, right = around(left, right, "gy")
    strip = ((guides + 1) // 2 * (rows + 2 * VROWS), LANES)
    valid_left, valid_right = call(
        pack_valid, (strip, strip), meta, valid_own, valid_top, valid_bottom, scalars=1
    )
    valid_left, valid_right = around(valid_left, valid_right, "gy")
    (spread,) = call(
        spread_valid,
        ((guides, 2, rows + 2 * VROWS, LANES),),
        meta, valid_own, valid_top, valid_bottom, valid_left, valid_right,
        scalars=1,
    )

    work, masks = vcycle_scratch(DEPTH1, rows)
    size = rows + 2 * DEPTH1 + 16
    z, z_up, z_down, res, dot_rz = call(
        functools.partial(stage_first, slots, rows),
        ((slots, rows, LANES), (slots * Z_HALO, LANES), (slots * Z_HALO, LANES), (rows, LANES), (8, LANES)),
        meta, shifts, frac, *xrs, top, bottom, left, right, spread,
        scalars=3,
        scratch=[
            vmem(slots, 2, rows + 2 * X_HALO + 16, LANES),
            vmem(2, rows + 96, LANES),
            vmem(slots, 2, size, LANES),
            vmem(2, size, LANES),
            *work, *masks,
        ],
    )
    z_top, z_bottom = around(z_up, z_down, "gx")
    strip = (pairs * (rows + 2 * Z_HALO), LANES)
    z_left, z_right = call(pack_second, (strip, strip), meta, z, z_top, z_bottom, scalars=1)
    z_left, z_right = around(z_left, z_right, "gy")

    work, masks = vcycle_scratch(DEPTH2, rows)
    size = rows + 2 * DEPTH2 + 16
    strip = (pairs * (rows + 2 * Y_HALO), LANES)
    y, y_left, y_right, image, dot_zq, dot_yq = call(
        functools.partial(stage_second, slots, rows),
        ((slots, 2, rows + 2 * Y_HALO, LANES), strip, strip, (rows, LANES), (8, LANES), (8, LANES)),
        meta, shifts, frac, *xrs, z, z_top, z_bottom, z_left, z_right, spread,
        scalars=3,
        scratch=[
            vmem(slots, 2, rows + 2 * Z_HALO + 8, LANES),
            vmem(2, rows + 160, LANES),
            vmem(slots, 2, size, LANES),
            vmem(slots, 2, size, LANES),
            *work, *masks,
        ],
    )
    y_left, y_right = around(y_left, y_right, "gy")

    image_y, sums = call(
        functools.partial(stage_third, slots, rows),
        ((rows, LANES), (n_gx * n_gy, 8, LANES)),
        meta, shifts, frac, *xrs, y, y_left, y_right, spread, dot_rz, dot_zq, dot_yq,
        scalars=3,
        scratch=[
            vmem(slots, 2, rows + 2 * Y_HALO + 8, LANES),
            vmem(2, rows + 48, LANES),
            vmem(1, 2, rows, LANES),
            vmem(2, rows + 16, LANES),
            vmem(8, LANES),
            vmem(rows + 16, LANES),
        ],
    )
    sums = lax.all_to_all(sums, ("gx", "gy"), 0, 0)
    return call(
        finish, ((1, rows, LANES), (1, rows, LANES)), start, z, res, image, y, image_y, sums
    )


def solution(mesh):
    in_specs = (
        P("layer", "gx", "gy"),
        P("layer", "gx", "gy"),
        P(None, "gx", "gy"),
        P("layer"),
        P(),
        P(),
    )
    out_specs = (P("layer", "gx", "gy"), P("layer", "gx", "gy"))

    def run(*args):
        return tuple(jax.shard_map(shards, mesh=mesh, in_specs=in_specs, out_specs=out_specs, check_vma=False)(*args))

    return run
```

time: 624 us -> 112 us (0.18)
  blocking collectives: 171 us -> 11.3 us
  starting transfers between devices: 157 us -> 18.3 us
  waiting for transfers between devices: 134 us -> 28.6 us
  between operations: 90.7 us -> 1.37 us
  Pallas kernels: 0 us -> 41.4 us
  local copies, waits for them, and re-layouts: 41.1 us -> 9.99 us
  other arithmetic: 26.1 us -> 0.55 us
    ppermute x76 -> x15, starting transfers between devices: 157 us -> 18.3 us  [the longest x7 12.5 us: around(): after = lax.ppermute(up, axis, [(i, (i - 1) % n) for i in range(n)])]
    psum x3 -> x0, blocking collectives: 120 us -> none  [global_sum(): return lax.psum(jnp.sum(values), ('layer', 'gx', 'gy'))]
    ppermute x76 -> x15, waiting for transfers between devices: 133 us -> 28.6 us  [the longest x7 18.9 us: around(): before = lax.ppermute(down, axis, [(i, (i + 1) % n) for i in range(n)])]
    all_gather x3 -> x0, blocking collectives: 50.2 us -> none  [operator_a(): lax.all_gather(padded_m, 'layer', axis=0, tiled=True)]
    pallas_call x0 -> x9, Pallas kernels: none -> 41.4 us  [the longest x8 38.9 us: call(): pl.pallas_call(kernel, out_shape=shapes, in_specs=[pl.BlockSpec(memory_sp...]
    reshape x10 -> x2, local copies, waits for them, and re-layouts: 13.6 us -> 1.29 us  [shards(): shifts, frac = (shifts.reshape(-1), frac.reshape(-1))]
    all_to_all x0 -> x1, blocking collectives: none -> 11.3 us  [shards(): sums = lax.all_to_all(sums, ('gx', 'gy'), 0, 0)]
    unnamed x111 -> x36, local copies, waits for them, and re-layouts: 17 us -> 7.2 us
  transfers between devices with their start and end apart: 79 -> 15, of which waited for: 44 -> 8; matrix products, arithmetic and copies ran while one was open for 1% -> 3% of each run, Pallas kernels for 0% -> 6%
where the time goes in v1:
time: 112 us; the launch traced here: 111 us
  Pallas kernels  41.4 us (37%)
  waiting for transfers between devices  28.6 us (26%)
  starting transfers between devices  18.3 us (16%)
  blocking collectives  11.3 us (10%)
  local copies, waits for them, and re-layouts  9.99 us (9%)
  between operations  1.37 us (1%)
    pallas_call x8, Pallas kernels, call(): pl.pallas_call(kernel, out_shape=shapes, in_specs=[pl.BlockSpec(memory_sp...  38.9 us
    ppermute x7, waiting for transfers between devices, around(): before = lax.ppermute(down, axis, [(i, (i + 1) % n) for i in range(n)])  18.9 us
    ppermute x7, starting transfers between devices, around(): after = lax.ppermute(up, axis, [(i, (i - 1) % n) for i in range(n)])  12.5 us
    all_to_all x1, blocking collectives, shards(): sums = lax.all_to_all(sums, ('gx', 'gy'), 0, 0)  11.3 us
    ppermute x7, waiting for transfers between devices, around(): after = lax.ppermute(up, axis, [(i, (i - 1) % n) for i in range(n)])  9.62 us
    unnamed x36, local copies, waits for them, and re-layouts  7.2 us
    ppermute x1, starting transfers between devices, shards(): lax.ppermute(xr, 'layer', [(i, (i + k) % slots) for i in range(slots)])  2.97 us
    ppermute x7, starting transfers between devices, around(): before = lax.ppermute(down, axis, [(i, (i + 1) % n) for i in range(n)])  2.83 us
  transfers between devices with their start and end apart: 15, of which 8 were waited for; matrix products, arithmetic and copies ran while one was open for 3% of the time, Pallas kernels for 6%

profile of v1, /device:TPU:0, one launch (start us, length us, event | category | flops | bytes accessed | tf_op | source)
XLA Modules:
  0.0 111.4 jit_solution(13890006092771769671)
XLA Ops:
  1.3 2.4 %shard_map.77 = (f32[264,128]{1,0:T(8,128)}, f32[8,128,128]{2,1,0:T(8,128)}, f32[576,128]{1,0:T(8,128)}, f32[576,128]{1,0:T(8,128)}) custom-call(f32[1,128,128]{2,1,0:T(8,128)} %start_ref.3, f32[1,128,128]{2,1,0:T(8,128)} %rhs_ref.1, s32[8,128,128]{2,1,0:T(8,128)} %valid_ref.1, f32[1]{0:T(128)S(6)} %copy.12.reg_ref), custom_call_target="tpu_custom_call" | custom-call | tf_op jit(solution)/shard_map/pallas_call | solution.py:678
  3.7 3.0 %collective-permute-start = (f32[264,128]{1,0:T(8,128)}, f32[264,128]{1,0:T(8,128)S(1)}, u32[]{:S(2)}, u32[]{:S(2)}) collective-permute-start(f32[264,128]{1,0:T(8,128)} %get-tuple-element.25.refs_0_), channel_id=1, source_target_pairs={{0,16},{16,0},{1,17},{17,1},{2,18},{18,2},{3,19},{19,3},{4,20},{20... | collective-permute-start | bytes 405512 | tf_op jit(solution)/shard_map/ppermute | solution.py:689
  6.7 1.6 %collective-permute-start.5 = (f32[576,128]{1,0:T(8,128)}, f32[576,128]{1,0:T(8,128)S(1)}, u32[]{:S(2)}, u32[]{:S(2)}) collective-permute-start(f32[576,128]{1,0:T(8,128)} %get-tuple-element.29), channel_id=1, source_target_pairs={{0,4},{4,8},{8,12},{12,0},{1,5},{5,9},{9,13},{13,1},{2,6},{6,10},{... | collective-permute-start | bytes 884744 | tf_op jit(solution)/shard_map/ppermute | solution.py:649
  8.3 2.2 %collective-permute-start.6 = (f32[576,128]{1,0:T(8,128)}, f32[576,128]{1,0:T(8,128)S(1)}, u32[]{:S(2)}, u32[]{:S(2)}) collective-permute-start(f32[576,128]{1,0:T(8,128)} %get-tuple-element.30), channel_id=1, source_target_pairs={{0,12},{4,0},{8,4},{12,8},{1,13},{5,1},{9,5},{13,9},{2,14},{6,2},{... | collective-permute-start | bytes 884744 | tf_op jit(solution)/shard_map/ppermute | solution.py:650
  10.5 0.8 fusion
  11.3 0.7 fusion.1
  12.6 6.1 %collective-permute-done.5.top_ref = f32[576,128]{1,0:T(8,128)S(1)} collective-permute-done((f32[576,128]{1,0:T(8,128)}, f32[576,128]{1,0:T(8,128)S(1)}, u32[]{:S(2)}, u32[]{:S(2)}) %collective-permute-start.5) | collective-permute-done | bytes 294944 | tf_op jit(solution)/shard_map/ppermute | solution.py:649
  18.7 4.3 %collective-permute-done.6.bottom_ref = f32[576,128]{1,0:T(8,128)S(1)} collective-permute-done((f32[576,128]{1,0:T(8,128)}, f32[576,128]{1,0:T(8,128)S(1)}, u32[]{:S(2)}, u32[]{:S(2)}) %collective-permute-start.6) | collective-permute-done | bytes 294944 | tf_op jit(solution)/shard_map/ppermute | solution.py:650
  23.7 2.6 %shard_map.79 = (f32[1088,128]{1,0:T(8,128)}, f32[1088,128]{1,0:T(8,128)}) custom-call(s32[8]{0:T(128)} %compare_select_fusion.3.meta_ref, f32[8,128,128]{2,1,0:T(8,128)} %get-tuple-element.28.own_ref, f32[576,128]{1,0:T(8,128)} %copy-done.1, f32[576,128]{1,0:T(8,128)} %copy-done.2), custom_call_target="tpu_custom_call" | custom-call | tf_op jit(solution)/shard_map/pallas_call | solution.py:638
  26.3 1.7 %collective-permute-start.8 = (f32[1088,128]{1,0:T(8,128)}, f32[1088,128]{1,0:T(8,128)S(1)}, u32[]{:S(2)}, u32[]{:S(2)}) collective-permute-start(f32[1088,128]{1,0:T(8,128)} %get-tuple-element.32), channel_id=1, source_target_pairs={{0,3},{1,0},{2,1},{3,2},{4,7},{5,4},{6,5},{7,6},{8,11},{9,8},{10,9... | collective-permute-start | bytes 1671176 | tf_op jit(solution)/shard_map/ppermute | solution.py:650
  28.1 2.5 %collective-permute-start.2 = (f32[160,128]{1,0:T(8,128)S(1)}, f32[160,128]{1,0:T(8,128)S(1)}, u32[]{:S(2)}, u32[]{:S(2)}) collective-permute-start(f32[160,128]{1,0:T(8,128)S(1)} %pad_maximum_fusion.1), channel_id=1, source_target_pairs={{0,12},{4,0},{8,4},{12,8},{1,13},{5,1},{9,5},{13,9},{2,14},{6,2},{... | collective-permute-start | bytes 245768 | tf_op jit(solution)/shard_map/ppermute | solution.py:650
  30.6 2.6 %collective-permute-done.2.refs_3_ = f32[160,128]{1,0:T(8,128)S(1)} collective-permute-done((f32[160,128]{1,0:T(8,128)S(1)}, f32[160,128]{1,0:T(8,128)S(1)}, u32[]{:S(2)}, u32[]{:S(2)}) %collective-permute-start.2) | collective-permute-done | bytes 81952 | tf_op jit(solution)/shard_map/ppermute | solution.py:650
  33.1 3.6 %collective-permute-done.1.refs_2_ = f32[160,128]{1,0:T(8,128)S(1)} collective-permute-done((f32[160,128]{1,0:T(8,128)S(1)}, f32[160,128]{1,0:T(8,128)S(1)}, u32[]{:S(2)}, u32[]{:S(2)}) %collective-permute-start.1) | collective-permute-done | bytes 81952 | tf_op jit(solution)/shard_map/ppermute | solution.py:649
  37.4 2.0 %shard_map.78 = (f32[416,128]{1,0:T(8,128)}, f32[416,128]{1,0:T(8,128)}) custom-call(s32[8]{0:T(128)} %compare_select_fusion.3.meta_ref, f32[264,128]{1,0:T(8,128)} %get-tuple-element.25.refs_0_, f32[264,128]{1,0:T(8,128)} %copy-done, f32[160,128]{1,0:T(8,128)} %copy-done.8, f32[160,128]{1,0:T(8,128)} %copy-done.7), custom_call_target="tpu_custom_call" | custom-call | tf_op jit(solution)/shard_map/pallas_call | solution.py:638
  39.4 1.7 %collective-permute-start.4 = (f32[416,128]{1,0:T(8,128)}, f32[416,128]{1,0:T(8,128)S(1)}, u32[]{:S(2)}, u32[]{:S(2)}) collective-permute-start(f32[416,128]{1,0:T(8,128)} %get-tuple-element.27), channel_id=1, source_target_pairs={{0,3},{1,0},{2,1},{3,2},{4,7},{5,4},{6,5},{7,6},{8,11},{9,8},{10,9... | collective-permute-start | bytes 638984 | tf_op jit(solution)/shard_map/ppermute | solution.py:650
  42.7 0.8 copy-done.3
  43.5 0.8 copy-done.4
  44.3 4.5 %shard_map.80.refs_6_.refs_7_.refs_5_ = f32[8,2,272,128]{3,2,1,0:T(8,128)} custom-call(s32[8]{0:T(128)} %compare_select_fusion.3.meta_ref, f32[8,128,128]{2,1,0:T(8,128)} %get-tuple-element.28.own_ref, f32[576,128]{1,0:T(8,128)} %copy-done.1, f32[576,128]{1,0:T(8,128)} %copy-done.2, f32[1088,128]{1,0:T(8,128)} %copy-done.3, f32[1088,128]{1,0:T(8,128)} %copy-done.4), custom_call_target="tpu_custom_call" | custom-call | tf_op jit(solution)/shard_map/pallas_call | solution.py:638
  50.1 9.3 %shard_map.81 = (f32[2,128,128]{2,1,0:T(8,128)}, f32[176,128]{1,0:T(8,128)}, f32[176,128]{1,0:T(8,128)}, f32[128,128]{1,0:T(8,128)}, f32[8,128]{1,0:T(8,128)}) custom-call(s32[8]{0:T(128)} %compare_select_fusion.3.meta_ref, s32[32]{0:T(128)} %reshape.10.shifts_ref, s32[32]{0:T(128)} %reshape.11.frac_ref, f32[264,128]{1,0:T(8,128)} %get-tuple-element.25.refs_0_, ...), custom_call_target="tpu_custom_call" | custom-call | tf_op jit(solution)/shard_map/pallas_call | solution.py:638
  59.5 1.3 %collective-permute-start.10 = (f32[176,128]{1,0:T(8,128)}, f32[176,128]{1,0:T(8,128)S(1)}, u32[]{:S(2)}, u32[]{:S(2)}) collective-permute-start(f32[176,128]{1,0:T(8,128)} %get-tuple-element.36), channel_id=1, source_target_pairs={{0,12},{4,0},{8,4},{12,8},{1,13},{5,1},{9,5},{13,9},{2,14},{6,2},{... | collective-permute-start | bytes 270344 | tf_op jit(solution)/shard_map/ppermute | solution.py:650
  60.7 0.8 collective-permute-start.9
  61.5 2.7 %collective-permute-done.10.bottom_ref.refs_4_ = f32[176,128]{1,0:T(8,128)S(1)} collective-permute-done((f32[176,128]{1,0:T(8,128)}, f32[176,128]{1,0:T(8,128)S(1)}, u32[]{:S(2)}, u32[]{:S(2)}) %collective-permute-start.10) | collective-permute-done | bytes 90144 | tf_op jit(solution)/shard_map/ppermute | solution.py:650
  64.2 3.1 %collective-permute-done.9.top_ref.refs_3_ = f32[176,128]{1,0:T(8,128)S(1)} collective-permute-done((f32[176,128]{1,0:T(8,128)}, f32[176,128]{1,0:T(8,128)S(1)}, u32[]{:S(2)}, u32[]{:S(2)}) %collective-permute-start.9) | collective-permute-done | bytes 90144 | tf_op jit(solution)/shard_map/ppermute | solution.py:649
  67.9 1.9 %shard_map.82 = (f32[304,128]{1,0:T(8,128)}, f32[304,128]{1,0:T(8,128)}) custom-call(s32[8]{0:T(128)} %compare_select_fusion.3.meta_ref, f32[2,128,128]{2,1,0:T(8,128)} %get-tuple-element.33.z_ref.refs_2_, f32[176,128]{1,0:T(8,128)} %copy-done.6, f32[176,128]{1,0:T(8,128)} %copy-done.5), custom_call_target="tpu_custom_call" | custom-call | tf_op jit(solution)/shard_map/pallas_call | solution.py:638
  69.8 1.7 %collective-permute-start.12 = (f32[304,128]{1,0:T(8,128)}, f32[304,128]{1,0:T(8,128)S(1)}, u32[]{:S(2)}, u32[]{:S(2)}) collective-permute-start(f32[304,128]{1,0:T(8,128)} %get-tuple-element.38), channel_id=1, source_target_pairs={{0,3},{1,0},{2,1},{3,2},{4,7},{5,4},{6,5},{7,6},{8,11},{9,8},{10,9... | collective-permute-start | bytes 466952 | tf_op jit(solution)/shard_map/ppermute | solution.py:650
  71.5 3.5 %collective-permute-done.11.refs_5_ = f32[304,128]{1,0:T(8,128)S(1)} collective-permute-done((f32[304,128]{1,0:T(8,128)}, f32[304,128]{1,0:T(8,128)S(1)}, u32[]{:S(2)}, u32[]{:S(2)}) %collective-permute-start.11) | collective-permute-done | bytes 155680 | tf_op jit(solution)/shard_map/ppermute | solution.py:649
  76.4 10.6 %shard_map.83 = (f32[2,2,208,128]{3,2,1,0:T(8,128)}, f32[208,128]{1,0:T(8,128)}, f32[208,128]{1,0:T(8,128)}, f32[128,128]{1,0:T(8,128)}, f32[8,128]{1,0:T(8,128)}, /*index=5*/f32[8,128]{1,0:T(8,128)}) custom-call(s32[8]{0:T(128)} %compare_select_fusion.3.meta_ref, s32[32]{0:T(128)} %reshape.10.shifts_ref, s32[32]{0:T(128)} %reshape.11.frac_ref, ...), custom_call_target="tpu_custom_call" | custom-call | tf_op jit(solution)/shard_map/pallas_call | solution.py:638
  87.4 1.3 %collective-permute-start.14 = (f32[208,128]{1,0:T(8,128)}, f32[208,128]{1,0:T(8,128)S(1)}, u32[]{:S(2)}, u32[]{:S(2)}) collective-permute-start(f32[208,128]{1,0:T(8,128)} %get-tuple-element.42), channel_id=1, source_target_pairs={{0,3},{1,0},{2,1},{3,2},{4,7},{5,4},{6,5},{7,6},{8,11},{9,8},{10,9... | collective-permute-start | bytes 319496 | tf_op jit(solution)/shard_map/ppermute | solution.py:650
  88.7 2.6 %collective-permute-done.13.refs_3_ = f32[208,128]{1,0:T(8,128)S(1)} collective-permute-done((f32[208,128]{1,0:T(8,128)}, f32[208,128]{1,0:T(8,128)S(1)}, u32[]{:S(2)}, u32[]{:S(2)}) %collective-permute-start.13) | collective-permute-done | bytes 106528 | tf_op jit(solution)/shard_map/ppermute | solution.py:649
  92.0 5.9 %shard_map.84 = (f32[128,128]{1,0:T(8,128)}, f32[16,8,128]{2,1,0:T(8,128)}) custom-call(s32[8]{0:T(128)} %compare_select_fusion.3.meta_ref, s32[32]{0:T(128)} %reshape.10.shifts_ref, s32[32]{0:T(128)} %reshape.11.frac_ref, f32[264,128]{1,0:T(8,128)} %get-tuple-element.25.refs_0_, f32[264,128]{1,0:T(8,128)} %copy-done, ...), custom_call_target="tpu_custom_call" | custom-call | tf_op jit(solution)/shard_map/pallas_call | solution.py:638
  97.9 11.3 %all_to_all.5.sums_ref = f32[16,8,128]{2,1,0:T(8,128)} all-to-all(f32[16,8,128]{2,1,0:T(8,128)} %get-tuple-element.47), channel_id=1, replica_groups=mesh['layer'=2,'gx'=4,'gy'=4] {'gx','gy'}, dimensions={0} | all-to-all | bytes 131072 | tf_op jit(solution)/shard_map/all_to_all | solution.py:766
  109.2 2.2 %shard_map.85 = (f32[1,128,128]{2,1,0:T(8,128)}, f32[1,128,128]{2,1,0:T(8,128)}) custom-call(f32[1,128,128]{2,1,0:T(8,128)} %start_ref.3, f32[2,128,128]{2,1,0:T(8,128)} %get-tuple-element.33.z_ref.refs_2_, f32[128,128]{1,0:T(8,128)} %get-tuple-element.34.res_ref, f32[128,128]{1,0:T(8,128)} %get-tuple-element.39.q_ref, ...), custom_call_target="tpu_custom_call" | custom-call | tf_op jit(solution)/shard_map/pallas_call | solution.py:638
  (53 shorter events, 7.9 us)
Async XLA Ops:
  0.6 40.5 %copy-start.15 = (s32[8,2,2]{0,2,1:T(2,128)S(1)}, s32[8,2,2]{0,2,1:T(2,128)}, u32[]{:S(2)}) copy-start(s32[8,2,2]{0,2,1:T(2,128)} %param.10) | copy-start | bytes 388
  0.6 41.2 %copy-start.16 = (s32[8,2,2]{0,2,1:T(2,128)S(1)}, s32[8,2,2]{0,2,1:T(2,128)}, u32[]{:S(2)}) copy-start(s32[8,2,2]{0,2,1:T(2,128)} %param.11) | copy-start | bytes 388
  3.7 8.8 %collective-permute-start = (f32[264,128]{1,0:T(8,128)}, f32[264,128]{1,0:T(8,128)S(1)}, u32[]{:S(2)}, u32[]{:S(2)}) collective-permute-start(f32[264,128]{1,0:T(8,128)} %get-tuple-element.25.refs_0_), channel_id=1, source_target_pairs={{0,16},{16,0},{1,17},{17,1},{2,18},{18,2},{3,19},{19,3},{4,20},{20... | collective-permute-start | bytes 405512 | tf_op jit(solution)/shard_map/ppermute | solution.py:689
  6.7 12.0 %collective-permute-start.5 = (f32[576,128]{1,0:T(8,128)}, f32[576,128]{1,0:T(8,128)S(1)}, u32[]{:S(2)}, u32[]{:S(2)}) collective-permute-start(f32[576,128]{1,0:T(8,128)} %get-tuple-element.29), channel_id=1, source_target_pairs={{0,4},{4,8},{8,12},{12,0},{1,5},{5,9},{9,13},{13,1},{2,6},{6,10},{... | collective-permute-start | bytes 884744 | tf_op jit(solution)/shard_map/ppermute | solution.py:649
  8.3 14.7 %collective-permute-start.6 = (f32[576,128]{1,0:T(8,128)}, f32[576,128]{1,0:T(8,128)S(1)}, u32[]{:S(2)}, u32[]{:S(2)}) collective-permute-start(f32[576,128]{1,0:T(8,128)} %get-tuple-element.30), channel_id=1, source_target_pairs={{0,12},{4,0},{8,4},{12,8},{1,13},{5,1},{9,5},{13,9},{2,14},{6,2},{... | collective-permute-start | bytes 884744 | tf_op jit(solution)/shard_map/ppermute | solution.py:650
  12.6 24.2 %copy-start = (f32[264,128]{1,0:T(8,128)}, f32[264,128]{1,0:T(8,128)S(1)}, u32[]{:S(2)}) copy-start(f32[264,128]{1,0:T(8,128)S(1)} %collective-permute-done.refs_1_) | copy-start | bytes 405508
  18.7 4.3 %copy-start.1 = (f32[576,128]{1,0:T(8,128)}, f32[576,128]{1,0:T(8,128)S(1)}, u32[]{:S(2)}) copy-start(f32[576,128]{1,0:T(8,128)S(1)} %collective-permute-done.5.top_ref) | copy-start | bytes 884740
  23.0 0.7 copy-start.2
  26.3 16.3 %collective-permute-start.7 = (f32[1088,128]{1,0:T(8,128)}, f32[1088,128]{1,0:T(8,128)S(1)}, u32[]{:S(2)}, u32[]{:S(2)}) collective-permute-start(f32[1088,128]{1,0:T(8,128)} %get-tuple-element.31), channel_id=1, source_target_pairs={{0,1},{1,2},{2,3},{3,0},{4,5},{5,6},{6,7},{7,4},{8,9},{9,10},{10,1... | collective-permute-start | bytes 1671176 | tf_op jit(solution)/shard_map/ppermute | solution.py:649
  26.3 16.3 %collective-permute-start.8 = (f32[1088,128]{1,0:T(8,128)}, f32[1088,128]{1,0:T(8,128)S(1)}, u32[]{:S(2)}, u32[]{:S(2)}) collective-permute-start(f32[1088,128]{1,0:T(8,128)} %get-tuple-element.32), channel_id=1, source_target_pairs={{0,3},{1,0},{2,1},{3,2},{4,7},{5,4},{6,5},{7,6},{8,11},{9,8},{10,9... | collective-permute-start | bytes 1671176 | tf_op jit(solution)/shard_map/ppermute | solution.py:650
  28.1 5.1 %collective-permute-start.2 = (f32[160,128]{1,0:T(8,128)S(1)}, f32[160,128]{1,0:T(8,128)S(1)}, u32[]{:S(2)}, u32[]{:S(2)}) collective-permute-start(f32[160,128]{1,0:T(8,128)S(1)} %pad_maximum_fusion.1), channel_id=1, source_target_pairs={{0,12},{4,0},{8,4},{12,8},{1,13},{5,1},{9,5},{13,9},{2,14},{6,2},{... | collective-permute-start | bytes 245768 | tf_op jit(solution)/shard_map/ppermute | solution.py:650
  30.5 6.2 %collective-permute-start.1 = (f32[160,128]{1,0:T(8,128)S(1)}, f32[160,128]{1,0:T(8,128)S(1)}, u32[]{:S(2)}, u32[]{:S(2)}) collective-permute-start(f32[160,128]{1,0:T(8,128)S(1)} %pad_maximum_fusion), channel_id=1, source_target_pairs={{0,4},{4,8},{8,12},{12,0},{1,5},{5,9},{9,13},{13,1},{2,6},{6,10},{... | collective-permute-start | bytes 245768 | tf_op jit(solution)/shard_map/ppermute | solution.py:649
  33.1 3.6 %copy-start.7 = (f32[160,128]{1,0:T(8,128)}, f32[160,128]{1,0:T(8,128)S(1)}, u32[]{:S(2)}) copy-start(f32[160,128]{1,0:T(8,128)S(1)} %collective-permute-done.2.refs_3_) | copy-start | bytes 245764
  36.8 0.6 copy-start.8
  39.4 9.3 %collective-permute-start.3 = (f32[416,128]{1,0:T(8,128)}, f32[416,128]{1,0:T(8,128)S(1)}, u32[]{:S(2)}, u32[]{:S(2)}) collective-permute-start(f32[416,128]{1,0:T(8,128)} %get-tuple-element.26), channel_id=1, source_target_pairs={{0,1},{1,2},{2,3},{3,0},{4,5},{5,6},{6,7},{7,4},{8,9},{9,10},{10,1... | collective-permute-start | bytes 638984 | tf_op jit(solution)/shard_map/ppermute | solution.py:649
  39.4 9.3 %collective-permute-start.4 = (f32[416,128]{1,0:T(8,128)}, f32[416,128]{1,0:T(8,128)S(1)}, u32[]{:S(2)}, u32[]{:S(2)}) collective-permute-start(f32[416,128]{1,0:T(8,128)} %get-tuple-element.27), channel_id=1, source_target_pairs={{0,3},{1,0},{2,1},{3,2},{4,7},{5,4},{6,5},{7,6},{8,11},{9,8},{10,9... | collective-permute-start | bytes 638984 | tf_op jit(solution)/shard_map/ppermute | solution.py:650
  42.7 0.8 copy-start.3
  43.5 0.8 copy-start.4
  48.7 0.7 copy-start.9
  49.4 0.7 copy-start.10
  59.5 4.7 %collective-permute-start.10 = (f32[176,128]{1,0:T(8,128)}, f32[176,128]{1,0:T(8,128)S(1)}, u32[]{:S(2)}, u32[]{:S(2)}) collective-permute-start(f32[176,128]{1,0:T(8,128)} %get-tuple-element.36), channel_id=1, source_target_pairs={{0,12},{4,0},{8,4},{12,8},{1,13},{5,1},{9,5},{13,9},{2,14},{6,2},{... | collective-permute-start | bytes 270344 | tf_op jit(solution)/shard_map/ppermute | solution.py:650
  60.7 6.5 %collective-permute-start.9 = (f32[176,128]{1,0:T(8,128)}, f32[176,128]{1,0:T(8,128)S(1)}, u32[]{:S(2)}, u32[]{:S(2)}) collective-permute-start(f32[176,128]{1,0:T(8,128)} %get-tuple-element.35), channel_id=1, source_target_pairs={{0,4},{4,8},{8,12},{12,0},{1,5},{5,9},{9,13},{13,1},{2,6},{6,10},{... | collective-permute-start | bytes 270344 | tf_op jit(solution)/shard_map/ppermute | solution.py:649
  64.2 3.1 %copy-start.5 = (f32[176,128]{1,0:T(8,128)}, f32[176,128]{1,0:T(8,128)S(1)}, u32[]{:S(2)}) copy-start(f32[176,128]{1,0:T(8,128)S(1)} %collective-permute-done.10.bottom_ref.refs_4_) | copy-start | bytes 270340
  67.3 0.6 copy-start.6
  69.8 5.3 %collective-permute-start.11 = (f32[304,128]{1,0:T(8,128)}, f32[304,128]{1,0:T(8,128)S(1)}, u32[]{:S(2)}, u32[]{:S(2)}) collective-permute-start(f32[304,128]{1,0:T(8,128)} %get-tuple-element.37), channel_id=1, source_target_pairs={{0,1},{1,2},{2,3},{3,0},{4,5},{5,6},{6,7},{7,4},{8,9},{9,10},{10,1... | collective-permute-start | bytes 466952 | tf_op jit(solution)/shard_map/ppermute | solution.py:649
  69.8 5.3 %collective-permute-start.12 = (f32[304,128]{1,0:T(8,128)}, f32[304,128]{1,0:T(8,128)S(1)}, u32[]{:S(2)}, u32[]{:S(2)}) collective-permute-start(f32[304,128]{1,0:T(8,128)} %get-tuple-element.38), channel_id=1, source_target_pairs={{0,3},{1,0},{2,1},{3,2},{4,7},{5,4},{6,5},{7,6},{8,11},{9,8},{10,9... | collective-permute-start | bytes 466952 | tf_op jit(solution)/shard_map/ppermute | solution.py:650
  75.0 0.7 copy-start.11
  75.7 0.7 copy-start.12
  86.9 4.4 %collective-permute-start.13 = (f32[208,128]{1,0:T(8,128)}, f32[208,128]{1,0:T(8,128)S(1)}, u32[]{:S(2)}, u32[]{:S(2)}) collective-permute-start(f32[208,128]{1,0:T(8,128)} %get-tuple-element.41), channel_id=1, source_target_pairs={{0,1},{1,2},{2,3},{3,0},{4,5},{5,6},{6,7},{7,4},{8,9},{9,10},{10,1... | collective-permute-start | bytes 319496 | tf_op jit(solution)/shard_map/ppermute | solution.py:649
  87.4 3.9 %collective-permute-start.14 = (f32[208,128]{1,0:T(8,128)}, f32[208,128]{1,0:T(8,128)S(1)}, u32[]{:S(2)}, u32[]{:S(2)}) collective-permute-start(f32[208,128]{1,0:T(8,128)} %get-tuple-element.42), channel_id=1, source_target_pairs={{0,3},{1,0},{2,1},{3,2},{4,7},{5,4},{6,5},{7,6},{8,11},{9,8},{10,9... | collective-permute-start | bytes 319496 | tf_op jit(solution)/shard_map/ppermute | solution.py:650
  91.3 0.6 copy-start.13
  91.3 0.7 copy-start.14

commit v2 on v0

v2 whole, which is shorter than its diff:
```python
import functools

import jax
import jax.numpy as jnp
from jax import lax
from jax.experimental import pallas as pl
from jax.experimental.pallas import tpu as pltpu
from jax.sharding import PartitionSpec as P

GUIDES = 8
SHIFT_MAX = 16
LANES = 128
HALF = LANES // 2
QUART = LANES // 4
F32 = jnp.float32
BF16 = jnp.bfloat16
DOT = functools.partial(jnp.dot, preferred_element_type=F32)

X_HALO, R_HALO, V_HALO, V_NEAR, Z_HALO, Y_HALO = 56, 24, 72, 40, 88, 40
DEPTH1, DEPTH2 = 24, 56


def lane_iota(shape=(1, LANES)):
    return lax.broadcasted_iota(jnp.int32, shape, len(shape) - 1)


def roll(x, amount):
    amount = amount % LANES if isinstance(amount, int) else amount & (LANES - 1)
    if isinstance(amount, int) and amount == 0:
        return x
    return pltpu.roll(x, amount, x.ndim - 1)


def spans(low, high, size):
    return [(r, min(size, high - r)) for r in range(low, high, size)]


class Meta:
    def __init__(self, ref):
        self.top_ok, self.bottom_ok, self.left_ok, self.right_ok = (ref[k].astype(F32) for k in range(4))
        self.layer, self.gx_odd, self.gy_odd = ref[4], ref[5], ref[6]


def exact_dot(values, matrix):
    high = values.astype(BF16)
    rest = values - high.astype(F32)
    mid = rest.astype(BF16)
    low = (rest - mid.astype(F32)).astype(BF16)
    return DOT(high, matrix) + (DOT(mid, matrix) + DOT(low, matrix))


def selection(shape, wanted_of):
    source = lax.broadcasted_iota(jnp.int32, shape, 0)
    target = lax.broadcasted_iota(jnp.int32, shape, 1)
    return wanted_of(source, target).astype(F32).astype(BF16)


def send_rows(meta, own_of, halo, rows, out_a, out_b, base):
    for r, n in spans(0, halo, 32):
        up, down = own_of(r, n), own_of(rows - halo + r, n)
        odd = meta.gx_odd == 1
        out_a[pl.ds(base + r, n), :] = jnp.where(odd, up, down)
        out_b[pl.ds(base + r, n), :] = jnp.where(odd, down, up)


def rows_with_halo(meta, own_of, a_of, b_of, skip, halo, rows, size=16):
    odd = meta.gx_odd == 1
    for r, n in spans(0, halo, size):
        yield r - halo, n, lambda t, r=r, n=n: jnp.where(odd, a_of(t, skip + r, n), b_of(t, skip + r, n)) * meta.top_ok
    for r, n in spans(0, rows, size):
        yield r, n, lambda t, r=r, n=n: own_of(t, r, n)
    for r, n in spans(0, halo, size):
        yield rows + r, n, lambda t, r=r, n=n: jnp.where(odd, b_of(t, r, n), a_of(t, r, n)) * meta.bottom_ok


def side_mask(meta):
    return ((lane_iota() >> 5) & 1) == meta.gy_odd


def send_columns(mask, even, odd):
    moved = roll(odd, -QUART)
    return jnp.where(mask, moved, even), jnp.where(mask, even, moved)


def with_columns(meta, mask, even, odd, from_a, from_b):
    lane = lane_iota()
    near = ((lane >> 5) & 1) == 0
    side_even = jnp.where(mask, from_a, from_b) * jnp.where(near, meta.right_ok, meta.left_ok)
    side_odd = jnp.where(mask, from_b, from_a) * jnp.where(near, meta.left_ok, meta.right_ok)
    side_even, side_odd = roll(side_even, HALF), roll(side_odd, -QUART)
    low = lane < HALF
    return (
        (jnp.where(low, even, side_even), jnp.where(low, odd, side_odd)),
        (jnp.where(low, side_even, even), jnp.where(low, side_odd, odd)),
    )


def merge(first, second):
    return jnp.where(lane_iota() < HALF, first, second)


def rows_of(ref, start):
    return lambda r, n: ref[pl.ds(start + r, n), :]


def five_point(ref, at, n):
    even, odd = ref[0, pl.ds(at, n), :], ref[1, pl.ds(at, n), :]
    sum_even = ref[0, pl.ds(at - 1, n), :] + ref[0, pl.ds(at + 1, n), :] + (odd + roll(odd, 1))
    sum_odd = ref[1, pl.ds(at - 1, n), :] + ref[1, pl.ds(at + 1, n), :] + (even + roll(even, -1))
    return sum_even - 4.0 * even, sum_odd - 4.0 * odd, even, odd


def five_coarse(ref, at, n, step):
    here = ref[pl.ds(at, n), :]
    sides = roll(here, step) + roll(here, -step)
    return ref[pl.ds(at - 1, n), :] + ref[pl.ds(at + 1, n), :] + sides - 4.0 * here, here


def mask_rows(meta, position, row_at, n, rows):
    row = row_at + lax.broadcasted_iota(jnp.int32, (n, LANES), 0)
    lane = (lane_iota((n, LANES)) - HALF * position) & (LANES - 1)
    by_row = jnp.where(row < 0, meta.top_ok, jnp.where(row >= rows, meta.bottom_ok, 1.0))
    return by_row * jnp.where(lane < HALF, 1.0, jnp.where(lane < 3 * QUART, meta.right_ok, meta.left_ok))


def guide_loop(meta, shifts_ref, frac_ref, x, valid, m, acc, p_rows, outs, slots, out_slots, square_ref=None, rows=None):
    (x_ref, x_base), (valid_ref, v_base), (m_ref, m_base), (acc_ref, acc_base) = x, valid, m, acc

    def coefficients(g, slot):
        layer = lax.rem(meta.layer - slot + slots, slots)
        at = (g * slots + layer) * 2
        return (
            shifts_ref[at],
            shifts_ref[at + 1],
            frac_ref[at].astype(F32) * (1.0 / 256.0),
            frac_ref[at + 1].astype(F32) * (1.0 / 256.0),
        )

    def between(ref, index, at, step, n, u):
        here = ref[index + (pl.ds(at, n), slice(None))]
        return here + u * (ref[index + (pl.ds(at + step, n), slice(None))] - here)

    def body(g, carry):
        home = HALF * (g & 1)
        fixed = []
        for slot in range(slots):
            a, b, u, v = coefficients(g, slot)
            amount = home - HALF * (slot & 1) - lax.shift_right_arithmetic(b, 1)
            fixed.append((a, u, v, b & 1, amount & (LANES - 1)))
        for r, n in spans(*p_rows, 16):
            even = odd = None
            for slot in range(slots):
                a, u, v, parity, amount = fixed[slot]
                c0, c1, c2 = (between(x_ref, (slot, parity + k), r + x_base + a, 1, n, u) for k in range(3))
                this_even = roll(c0 + v * (c1 - c0), amount)
                this_odd = roll(c1 + v * (c2 - c1), amount)
                even = this_even if even is None else even + this_even
                odd = this_odd if odd is None else odd + this_odd
            m_even = even * valid_ref[g, 0, pl.ds(r + v_base, n), :]
            m_odd = odd * valid_ref[g, 1, pl.ds(r + v_base, n), :]
            m_ref[0, pl.ds(r + m_base, n), :] = m_even
            m_ref[1, pl.ds(r + m_base, n), :] = m_odd
            if square_ref is not None:
                own = (((lane_iota() - home) & (LANES - 1)) < HALF).astype(F32)
                for k in range(0, n, 8):
                    if 0 <= r + k < rows:
                        sl = slice(k, k + 8)
                        square_ref[...] += own * (m_even[sl] * even[sl] + m_odd[sl] * odd[sl])
        for slot in range(out_slots):
            a, b, u, v = coefficients(g, slot)
            back = -b - 1
            parity = back & 1
            amount = HALF * (slot & 1) - home - lax.shift_right_arithmetic(back, 1)
            for r, n in spans(*outs, 16):
                at = r + m_base - a
                plane_a = between(m_ref, (parity,), at, -1, n, u)
                plane_b = between(m_ref, (1 - parity,), at, -1, n, u)
                q0, q1, q2 = roll(plane_a, amount), roll(plane_b, amount - parity), roll(plane_a, amount - 1)
                acc_ref[slot, 0, pl.ds(r + acc_base, n), :] += q1 + v * (q0 - q1)
                acc_ref[slot, 1, pl.ds(r + acc_base, n), :] += q2 + v * (q1 - q2)
        return carry

    lax.fori_loop(0, valid_ref.shape[0], body, 0)


def store_field(x_ref, slot, at, n, even, odd):
    for plane, value in enumerate((even, odd, roll(even, -1), roll(odd, -1))):
        x_ref[slot, plane, pl.ds(at, n), :] = value


def zero_rows(ref, index, ranges):
    for low, high in ranges:
        if high > low:
            ref[index + (pl.ds(low, high - low), slice(None))] = jnp.zeros((high - low, LANES), F32)


def clear_planes(ref, index):
    for plane in range(2):
        for r, n in spans(0, ref.shape[-2], 64):
            ref[index + (plane, pl.ds(r, n), slice(None))] = jnp.zeros((n, LANES), F32)


def vcycle(h_ref, out_ref, weight, depth, rows, masks, work):
    g_ref, w_ref, t_ref, h1, g1, w1, t1, h2, g2 = work
    mask0, mask1, mask2 = masks
    size0 = rows + 2 * depth
    size1, size2 = size0 // 2, size0 // 4
    lane = lane_iota()
    s0 = 0.5 / (4.0 + 20.0 * weight)
    weight1, weight2 = weight * (1.0 / 16.0), weight * (1.0 / 256.0)
    s1 = 0.5 / (4.0 + 20.0 * weight1)
    s2 = 0.5 / (4.0 + 20.0 * weight2)

    for r, n in spans(8, 8 + size0, 16):
        lap_even, lap_odd, _, _ = five_point(h_ref, r, n)
        mask = mask0[pl.ds(r, n), :]
        g_ref[0, pl.ds(r, n), :] = mask * lap_even
        g_ref[1, pl.ds(r, n), :] = mask * lap_odd
    for r, n in spans(8, 8 + size0, 16):
        bi_even, bi_odd, _, _ = five_point(g_ref, r, n)
        h_both = h_ref[0, pl.ds(r, n), :] + h_ref[1, pl.ds(r, n), :]
        t_ref[pl.ds(r, n), :] = mask0[pl.ds(r, n), :] * (
            h_both - s0 * (4.0 * h_both + weight * (bi_even + bi_odd))
        )
    h1[pl.ds(8, size1), :] = 0.25 * (t_ref[pl.ds(8, size1, stride=2), :] + t_ref[pl.ds(9, size1, stride=2), :])
    for r, n in spans(8, 8 + size1, 32):
        lap, _ = five_coarse(h1, r, n, 1)
        g1[pl.ds(r, n), :] = mask1[pl.ds(r, n), :] * lap
    for r, n in spans(8, 8 + size1, 32):
        bi, _ = five_coarse(g1, r, n, 1)
        here = h1[pl.ds(r, n), :]
        t1[pl.ds(r, n), :] = mask1[pl.ds(r, n), :] * (here - s1 * (4.0 * here + weight1 * bi))
    both = t1[pl.ds(8, size2, stride=2), :] + t1[pl.ds(9, size2, stride=2), :]
    h2[pl.ds(8, size2), :] = 0.25 * (both + jnp.where((lane & 1) == 0, roll(both, -1), roll(both, 1)))
    lap, _ = five_coarse(h2, 8, size2, 2)
    g2[pl.ds(8, size2), :] = mask2[pl.ds(8, size2), :] * lap
    bi, _ = five_coarse(g2, 8, size2, 2)
    here = h2[pl.ds(8, size2), :]
    e2 = mask2[pl.ds(8, size2), :] * (s2 * (2.0 * here - s2 * (4.0 * here + weight2 * bi)))
    t1[pl.ds(8, size2, stride=2), :] = e2
    t1[pl.ds(9, size2, stride=2), :] = e2
    for r, n in spans(8, 8 + size1, 32):
        w1[pl.ds(r, n), :] = s1 * h1[pl.ds(r, n), :] + t1[pl.ds(r, n), :]
    for r, n in spans(8, 8 + size1, 32):
        lap, _ = five_coarse(w1, r, n, 1)
        g1[pl.ds(r, n), :] = mask1[pl.ds(r, n), :] * lap
    for r, n in spans(8, 8 + size1, 32):
        bi, _ = five_coarse(g1, r, n, 1)
        here = w1[pl.ds(r, n), :]
        t1[pl.ds(r, n), :] = mask1[pl.ds(r, n), :] * (
            here + s1 * (h1[pl.ds(r, n), :] - 4.0 * here - weight1 * bi)
        )
    e1 = t1[pl.ds(8, size1), :]
    t_ref[pl.ds(8, size1, stride=2), :] = e1
    t_ref[pl.ds(9, size1, stride=2), :] = e1
    for r, n in spans(8, 8 + size0, 16):
        copied = t_ref[pl.ds(r, n), :]
        for plane in range(2):
            w_ref[plane, pl.ds(r, n), :] = s0 * h_ref[plane, pl.ds(r, n), :] + copied
    for r, n in spans(8, 8 + size0, 16):
        lap_even, lap_odd, _, _ = five_point(w_ref, r, n)
        mask = mask0[pl.ds(r, n), :]
        g_ref[0, pl.ds(r, n), :] = mask * lap_even
        g_ref[1, pl.ds(r, n), :] = mask * lap_odd
    for r, n in spans(8, 8 + size0, 16):
        bi = five_point(g_ref, r, n)[:2]
        mask = mask0[pl.ds(r, n), :]
        for plane in range(2):
            here = w_ref[plane, pl.ds(r, n), :]
            out_ref[plane, pl.ds(r, n), :] = mask * (
                here + s0 * (h_ref[plane, pl.ds(r, n), :] - 4.0 * here - weight * bi[plane])
            )


def vcycle_scratch(depth, rows, slots):
    size0 = rows + 2 * depth
    one = lambda size: pltpu.VMEM((size + 16, LANES), F32)
    two = pltpu.VMEM((2, size0 + 16, LANES), F32)
    size1, size2 = size0 // 2, size0 // 4
    work = [two, two, one(size0), one(size1), one(size1), one(size1), one(size1), one(size2), one(size2)]
    positions = min(slots, 2)
    return work + [pltpu.VMEM((positions, size + 16, LANES), F32) for size in (size0, size1, size2)]


def prepare_vcycle(meta, depth, rows, masks, work):
    size0 = rows + 2 * depth
    sizes = (size0, size0 // 2, size0 // 4)
    for level, (mask, size) in enumerate(zip(masks, sizes)):
        for position in range(mask.shape[0]):
            for r, n in spans(0, size + 16, 64):
                mask[position, pl.ds(r, n), :] = mask_rows(
                    meta, position, r - 8 - (depth >> level), n, rows >> level
                )
    g_ref, w_ref, t_ref, h1, g1, w1, t1, h2, g2 = work
    for plane in range(2):
        zero_rows(w_ref, (plane,), ((0, 8), (size0 + 8, size0 + 16)))
    for ref, size in ((h1, sizes[1]), (g1, sizes[1]), (w1, sizes[1]), (h2, sizes[2]), (g2, sizes[2])):
        zero_rows(ref, (), ((0, 8), (size + 8, size + 16)))


def bilaplace_into(x_ref, x_base, g_ref, low, high, mask_of):
    for r, n in spans(low - 8, high + 8, 16):
        lap_even, lap_odd, _, _ = five_point(x_ref, r + x_base, n)
        mask = mask_of(r, n)
        g_ref[0, pl.ds(r - low + 8, n), :] = mask * lap_even
        g_ref[1, pl.ds(r - low + 8, n), :] = mask * lap_odd


def fold(values):
    total = values[0:8]
    for k in range(8, values.shape[0], 8):
        total = total + values[k : k + 8]
    return total


def order_inputs(start_ref, rhs_ref, reg_ref, xr_ref):
    rows = start_ref.shape[1]
    matrix = selection(
        (LANES, LANES), lambda s, t: s == 2 * (t & (HALF - 1)) + (t >= HALF).astype(jnp.int32)
    )
    xr_ref[pl.ds(0, rows), :] = exact_dot(start_ref[0], matrix)
    xr_ref[pl.ds(rows, rows), :] = exact_dot(rhs_ref[0], matrix)
    xr_ref[pl.ds(2 * rows, 8), :] = jnp.full((8, LANES), reg_ref[0], F32)


def order_valid(meta_ref, valid_ref, own_ref, a_ref, b_ref):
    meta = Meta(meta_ref)
    guides, rows = valid_ref.shape[:2]
    matrix = selection(
        (2 * LANES, 2 * LANES),
        lambda s, t: s
        == ((t >> 6) & 1) * LANES + 2 * (t & (HALF - 1)) + (t >= LANES).astype(jnp.int32),
    )
    for q in range((guides + 1) // 2):
        pair = [valid_ref[min(2 * q + k, guides - 1)].astype(F32).astype(BF16) for k in range(2)]
        planes = DOT(jnp.concatenate(pair, axis=1), matrix)
        for t in range(2):
            own_ref[q, t] = planes[:, t * LANES : (t + 1) * LANES]
            send_rows(
                meta, lambda r, n: own_ref[q, t, pl.ds(r, n), :], V_HALO, rows, a_ref, b_ref, (2 * q + t) * V_HALO
            )


def pair_inputs(slots, rows, meta_ref, *refs):
    meta = Meta(meta_ref)
    xr_refs, (x_ref, r_ref, reg_ref, a_ref, b_ref) = refs[:slots], refs[slots:]
    low = lane_iota() < HALF
    for slot in range(slots):
        reg_ref[pl.ds(8 * slot, 8), :] = xr_refs[slot][pl.ds(2 * rows, 8), :]
    for q in range((slots + 1) // 2):
        first, second = xr_refs[2 * q], xr_refs[min(2 * q + 1, slots - 1)]
        for out, at in ((x_ref, 0), (r_ref, rows)):
            for r, n in spans(0, rows, 32):
                one, two = first[pl.ds(at + r, n), :], second[pl.ds(at + r, n), :]
                out[q, 0, pl.ds(r, n), :] = jnp.where(low, one, roll(two, HALF))
                out[q, 1, pl.ds(r, n), :] = jnp.where(low, roll(one, HALF), two)
        for t in range(2):
            base = (2 * q + t) * (X_HALO + R_HALO)
            send_rows(meta, lambda r, n: x_ref[q, t, pl.ds(r, n), :], X_HALO, rows, a_ref, b_ref, base)
            send_rows(meta, lambda r, n: r_ref[q, t, pl.ds(r, n), :], R_HALO, rows, a_ref, b_ref, base + X_HALO)


def pair_rows(meta, own_ref, a_ref, b_ref, q, stride, at, skip, halo, rows, size=16):
    return rows_with_halo(
        meta,
        lambda t, r, n: own_ref[q, t, pl.ds(r, n), :],
        lambda t, r, n: a_ref[pl.ds((2 * q + t) * stride + at + r, n), :],
        lambda t, r, n: b_ref[pl.ds((2 * q + t) * stride + at + r, n), :],
        skip, halo, rows, size,
    )


def pack_columns(meta, mask, groups, out_a, out_b):
    base = 0
    for halo, groups_rows in groups:
        low = None
        for r, n, get in groups_rows:
            low = r if low is None else low
            a, b = send_columns(mask, get(0), get(1))
            out_a[pl.ds(base + r - low, n), :] = a
            out_b[pl.ds(base + r - low, n), :] = b
            end = base + r - low + n
        base = end


def pack_first(meta_ref, x_ref, r_ref, v_ref, xa, xb, va, vb, a_ref, b_ref, far_a, far_b):
    meta = Meta(meta_ref)
    mask = side_mask(meta)
    pairs, _, rows, _ = x_ref.shape
    stride = X_HALO + R_HALO
    groups = [(X_HALO, pair_rows(meta, x_ref, xa, xb, q, stride, 0, 0, X_HALO, rows)) for q in range(pairs)]
    groups += [(R_HALO, pair_rows(meta, r_ref, xa, xb, q, stride, X_HALO, 0, R_HALO, rows)) for q in range(pairs)]
    groups += [
        (V_NEAR, pair_rows(meta, v_ref, va, vb, q, V_HALO, 0, V_HALO - V_NEAR, V_NEAR, rows))
        for q in range(v_ref.shape[0])
    ]
    pack_columns(meta, mask, groups, a_ref, b_ref)
    far = V_HALO - V_NEAR
    for q in range(v_ref.shape[0]):
        for r, n, get in pair_rows(meta, v_ref, va, vb, q, V_HALO, 0, 0, V_HALO, rows, 8):
            at = r + V_HALO if r < -V_NEAR else r - rows - V_NEAR + far
            if r < -V_NEAR or r >= rows + V_NEAR:
                a, b = send_columns(mask, get(0), get(1))
                far_a[pl.ds(2 * far * q + at, n), :] = a
                far_b[pl.ds(2 * far * q + at, n), :] = b


def spread_valid(meta_ref, v_ref, va, vb, near_a, near_b, far_a, far_b, out_ref, halo=V_HALO, near_base=0):
    meta = Meta(meta_ref)
    mask = side_mask(meta)
    pairs, _, rows, _ = v_ref.shape
    far = V_HALO - V_NEAR
    for q in range(pairs):
        for r, n, get in pair_rows(meta, v_ref, va, vb, q, V_HALO, 0, V_HALO - halo, halo, rows, 8):
            if r < -V_NEAR:
                a, b, at = far_a, far_b, 2 * far * q + r + V_HALO
            elif r >= rows + V_NEAR:
                a, b, at = far_a, far_b, 2 * far * q + r - rows - V_NEAR + far
            else:
                a, b, at = near_a, near_b, near_base + (rows + 2 * V_NEAR) * q + r + V_NEAR
            fields = with_columns(meta, mask, get(0), get(1), a[pl.ds(at, n), :], b[pl.ds(at, n), :])
            for k, planes in enumerate(fields):
                if 2 * q + k < out_ref.shape[0]:
                    for t in range(2):
                        out_ref[2 * q + k, t, pl.ds(r + halo, n), :] = planes[t]


def load_fields(meta, mask, slots, q, rows_iter, a_ref, b_ref, base, shift, x_ref, x_base):
    for r, n, get in rows_iter:
        at = base + r + shift
        fields = with_columns(meta, mask, get(0), get(1), a_ref[pl.ds(at, n), :], b_ref[pl.ds(at, n), :])
        for k, planes in enumerate(fields):
            if 2 * q + k < slots:
                store_field(x_ref, 2 * q + k, r + x_base, n, *planes)


def stage_first(slots, meta_ref, shifts_ref, frac_ref, own_ref, r_ref, v_ref, reg_ref, xa, xb, va, vb, ga, gb, *refs):
    z_ref, out_a, out_b, res_ref, dot_ref = refs[:5]
    x_ref, valid_ref, m_ref, acc_ref, z_planes, *rest = refs[5:]
    work, masks = rest[:9], rest[9:12]
    meta = Meta(meta_ref)
    mask = side_mask(meta)
    pairs, _, rows, _ = own_ref.shape
    x_base, m_base, acc_base = X_HALO + 8, V_NEAR + 8, DEPTH1 + 8
    prepare_vcycle(meta, DEPTH1, rows, masks, work)
    total = rows + 2 * X_HALO
    total_r = rows + 2 * R_HALO
    stride = X_HALO + R_HALO
    for q in range(pairs):
        load_fields(
            meta, mask, slots, q, pair_rows(meta, own_ref, xa, xb, q, stride, 0, 0, X_HALO, rows),
            ga, gb, q * total, X_HALO, x_ref, x_base,
        )
    for k in range(slots):
        for plane in range(4):
            zero_rows(x_ref, (k, plane), ((0, 8), (total + 8, total + 16)))
        clear_planes(acc_ref, (k,))
    for plane in range(2):
        zero_rows(m_ref, (plane,), ((0, 8), (rows + 2 * V_NEAR + 8, rows + 2 * V_NEAR + 16)))
    spread_valid(
        meta_ref, v_ref, va, vb, ga, gb, None, None, valid_ref, V_NEAR, pairs * (total + total_r)
    )
    guide_loop(
        meta, shifts_ref, frac_ref, (x_ref, x_base), (valid_ref, V_NEAR), (m_ref, m_base), (acc_ref, acc_base),
        (-V_NEAR, rows + V_NEAR), (-DEPTH1, rows + DEPTH1), slots, slots,
    )
    g_ref = work[0]
    dot_ref[...] = jnp.zeros((8, LANES), F32)
    for q in range(pairs):
        base = pairs * total + q * total_r + R_HALO
        for r, n, get in pair_rows(meta, r_ref, xa, xb, q, stride, X_HALO, 0, R_HALO, rows):
            fields = with_columns(
                meta, mask, get(0), get(1), ga[pl.ds(base + r, n), :], gb[pl.ds(base + r, n), :]
            )
            at = r + DEPTH1 + 8
            for k, planes in enumerate(fields):
                if 2 * q + k < slots:
                    for t in range(2):
                        acc_ref[2 * q + k, t, pl.ds(at, n), :] = planes[t] - (
                            acc_ref[2 * q + k, t, pl.ds(at, n), :] + 0.1 * x_ref[2 * q + k, t, pl.ds(r + x_base, n), :]
                        )
    for k in range(slots):
        weight = reg_ref[pl.ds(8 * k, 1), :]
        own_masks = [m.at[k & 1] for m in masks]
        bilaplace_into(
            x_ref.at[k], x_base, g_ref, -DEPTH1, rows + DEPTH1,
            lambda r, n: own_masks[0][pl.ds(r + DEPTH1 + 8, n), :],
        )
        h_ref = acc_ref.at[k]
        for at, n in spans(8, rows + 2 * DEPTH1 + 8, 16):
            bi = five_point(g_ref, at, n)[:2]
            inside = own_masks[0][pl.ds(at, n), :]
            for t in range(2):
                h_ref[t, pl.ds(at, n), :] = inside * (h_ref[t, pl.ds(at, n), :] - weight * bi[t])
        for t in range(2):
            zero_rows(g_ref, (t,), ((0, 8), (rows + 2 * DEPTH1 + 8, rows + 2 * DEPTH1 + 16)))
        vcycle(h_ref, z_planes.at[k], weight, DEPTH1, rows, own_masks, work)
    for q in range(pairs):
        one, two = 2 * q, min(2 * q + 1, slots - 1)
        for r, n in spans(0, rows, 16):
            rows_at = pl.ds(r + DEPTH1 + 8, n)
            for t in range(2):
                z = merge(z_planes[one, t, rows_at, :], z_planes[two, t, rows_at, :])
                res = merge(acc_ref[one, t, rows_at, :], acc_ref[two, t, rows_at, :])
                z_ref[q, t, pl.ds(r, n), :] = z
                if q == 0:
                    res_ref[t, pl.ds(r, n), :] = res
                dot_ref[...] += fold(own_lanes(slots, q) * (z * res))
        for t in range(2):
            send_rows(
                meta, lambda r, n: z_ref[q, t, pl.ds(r, n), :], Z_HALO, rows, out_a, out_b, (2 * q + t) * Z_HALO
            )


def own_lanes(slots, q):
    return 1.0 if 2 * q + 1 < slots else (lane_iota() < HALF).astype(F32)


def pack_second(meta_ref, z_ref, za, zb, a_ref, b_ref):
    meta = Meta(meta_ref)
    pairs, _, rows, _ = z_ref.shape
    groups = [(Z_HALO, pair_rows(meta, z_ref, za, zb, q, Z_HALO, 0, 0, Z_HALO, rows)) for q in range(pairs)]
    pack_columns(meta, side_mask(meta), groups, a_ref, b_ref)


def stage_second(slots, meta_ref, shifts_ref, frac_ref, z_ref, reg_ref, valid_ref, za, zb, ga, gb, *refs):
    y_ref, out_a, out_b, image_ref, dot_zq, dot_yq = refs[:6]
    x_ref, m_ref, acc_ref, y_planes, *rest = refs[6:]
    work, masks = rest[:9], rest[9:12]
    meta = Meta(meta_ref)
    mask = side_mask(meta)
    pairs, _, rows, _ = z_ref.shape
    x_base, m_base, acc_base = Z_HALO, V_HALO + 8, DEPTH2 + 8
    prepare_vcycle(meta, DEPTH2, rows, masks, work)
    total = rows + 2 * Z_HALO
    for q in range(pairs):
        load_fields(
            meta, mask, slots, q, pair_rows(meta, z_ref, za, zb, q, Z_HALO, 0, 0, Z_HALO, rows),
            ga, gb, q * total, Z_HALO, x_ref, x_base,
        )
    for k in range(slots):
        for plane in range(4):
            zero_rows(x_ref, (k, plane), ((total, total + 8),))
        clear_planes(acc_ref, (k,))
    for plane in range(2):
        zero_rows(m_ref, (plane,), ((0, 8), (rows + 2 * V_HALO + 8, rows + 2 * V_HALO + 16)))
    guide_loop(
        meta, shifts_ref, frac_ref, (x_ref, x_base), (valid_ref, V_HALO), (m_ref, m_base), (acc_ref, acc_base),
        (-V_HALO, rows + V_HALO), (-DEPTH2, rows + DEPTH2), slots, slots,
    )
    g_ref = work[0]
    for k in range(slots):
        weight = reg_ref[pl.ds(8 * k, 1), :]
        own_masks = [m.at[k & 1] for m in masks]
        bilaplace_into(
            x_ref.at[k], x_base, g_ref, -DEPTH2, rows + DEPTH2,
            lambda r, n: own_masks[0][pl.ds(r + DEPTH2 + 8, n), :],
        )
        h_ref = acc_ref.at[k]
        for r, n in spans(-DEPTH2, rows + DEPTH2, 16):
            at = r + DEPTH2 + 8
            bi = five_point(g_ref, at, n)[:2]
            inside = own_masks[0][pl.ds(at, n), :]
            for t in range(2):
                h_ref[t, pl.ds(at, n), :] = inside * (
                    h_ref[t, pl.ds(at, n), :] + weight * bi[t] + 0.1 * x_ref[k, t, pl.ds(r + x_base, n), :]
                )
        for t in range(2):
            zero_rows(g_ref, (t,), ((0, 8), (rows + 2 * DEPTH2 + 8, rows + 2 * DEPTH2 + 16)))
        vcycle(h_ref, y_planes.at[k], weight, DEPTH2, rows, own_masks, work)
    dot_zq[...] = jnp.zeros((8, LANES), F32)
    dot_yq[...] = jnp.zeros((8, LANES), F32)
    total_y = rows + 2 * Y_HALO
    for q in range(pairs):
        one, two = 2 * q, min(2 * q + 1, slots - 1)
        for r, n in spans(-Y_HALO, rows + Y_HALO, 8):
            rows_at = pl.ds(r + DEPTH2 + 8, n)
            y = [merge(y_planes[one, t, rows_at, :], y_planes[two, t, rows_at, :]) for t in range(2)]
            at = pl.ds(q * total_y + r + Y_HALO, n)
            out_a[at, :], out_b[at, :] = send_columns(mask, *y)
            for t in range(2):
                y_ref[q, t, pl.ds(r + Y_HALO, n), :] = y[t]
                if 0 <= r < rows:
                    image = merge(acc_ref[one, t, rows_at, :], acc_ref[two, t, rows_at, :])
                    z = z_ref[q, t, pl.ds(r, n), :]
                    own = own_lanes(slots, q)
                    dot_zq[...] += fold(own * (z * image))
                    dot_yq[...] += fold(own * (y[t] * image))
                    if q == 0:
                        image_ref[t, pl.ds(r, n), :] = image


def stage_third(slots, meta_ref, shifts_ref, frac_ref, y_ref, reg_ref, valid_ref, dot_rz, dot_zq, dot_yq, ga, gb, *refs):
    image_ref, sums_ref, x_ref, m_ref, acc_ref, g_ref, square_ref, mask_ref = refs
    meta = Meta(meta_ref)
    mask = side_mask(meta)
    pairs, _, total, _ = y_ref.shape
    rows = total - 2 * Y_HALO
    x_base, m_base = Y_HALO, 24
    for q in range(pairs):
        load_fields(
            meta, mask, slots, q,
            [(r, n, lambda t, r=r, n=n: y_ref[q, t, pl.ds(r, n), :]) for r, n in spans(0, total, 16)],
            ga, gb, q * total, 0, x_ref, 0,
        )
    for k in range(slots):
        for plane in range(4):
            zero_rows(x_ref, (k, plane), ((total, total + 8),))
    clear_planes(acc_ref, (0,))
    square_ref[...] = jnp.zeros((8, LANES), F32)
    for position in range(mask_ref.shape[0]):
        for r, n in spans(-8, rows + 8, 48):
            mask_ref[position, pl.ds(r + 8, n), :] = mask_rows(meta, position, r, n, rows)
    guide_loop(
        meta, shifts_ref, frac_ref, (x_ref, x_base), (valid_ref, V_HALO), (m_ref, m_base), (acc_ref, 0),
        (-24, rows + 24), (0, rows), slots, 1, square_ref, rows,
    )
    for k in reversed(range(slots)):
        weight = reg_ref[pl.ds(8 * k, 1), :]
        bilaplace_into(
            x_ref.at[k], x_base, g_ref, 0, rows, lambda r, n: mask_ref[k & 1, pl.ds(r + 8, n), :]
        )
        own = (((lane_iota() - HALF * (k & 1)) & (LANES - 1)) < HALF).astype(F32)
        for r, n in spans(0, rows, 16):
            x = x_ref[k, 0, pl.ds(r + x_base, n), :], x_ref[k, 1, pl.ds(r + x_base, n), :]
            if k == 0:
                bi_even, bi_odd, g_even, g_odd = five_point(g_ref, r + 8, n)
                image_ref[0, pl.ds(r, n), :] = acc_ref[0, 0, pl.ds(r, n), :] + weight * bi_even + 0.1 * x[0]
                image_ref[1, pl.ds(r, n), :] = acc_ref[0, 1, pl.ds(r, n), :] + weight * bi_odd + 0.1 * x[1]
            else:
                g_even, g_odd = g_ref[0, pl.ds(r + 8, n), :], g_ref[1, pl.ds(r + 8, n), :]
            square_ref[...] += own * fold(
                weight * (g_even * g_even + g_odd * g_odd) + 0.1 * (x[0] * x[0] + x[1] * x[1])
            )
    row = lax.broadcasted_iota(jnp.int32, (8, LANES), 0)
    packed = jnp.zeros((8, LANES), F32)
    for at, part in enumerate((dot_rz[...], dot_zq[...], dot_yq[...], square_ref[...])):
        packed = jnp.where(row == at, jnp.sum(part, axis=0, keepdims=True), packed)
    for d in range(sums_ref.shape[0]):
        sums_ref[d] = packed


def finish(start_ref, z_ref, res_ref, q_ref, y_ref, p_ref, sums_ref, solution_ref, residual_ref):
    rows = start_ref.shape[1]
    total = sums_ref[0]
    for d in range(1, sums_ref.shape[0]):
        total = total + sums_ref[d]
    total = jnp.sum(total, axis=1, keepdims=True)
    rz, zq, yq, yp = (total[k : k + 1] for k in range(4))
    alpha = rz / zq
    rz_next = alpha * alpha * yq - rz
    grown = 1.0 + rz_next / rz
    alpha_next = rz_next / (grown * grown * zq - 2.0 * alpha * grown * yq + alpha * alpha * yp)
    matrix = selection(
        (2 * LANES, LANES), lambda s, t: s == (t >> 1) + LANES * (t & 1)
    )
    c_z = alpha + alpha_next * grown
    c_y = alpha_next * alpha
    step, rest = [], []
    for t in range(2):
        step.append(c_z * z_ref[0, t] - c_y * y_ref[0, t, pl.ds(Y_HALO, rows), :])
        rest.append(res_ref[t] - (c_z * q_ref[t] - c_y * p_ref[t]))
    solution_ref[0] = start_ref[0] + exact_dot(jnp.concatenate(step, axis=1), matrix)
    residual_ref[0] = exact_dot(jnp.concatenate(rest, axis=1), matrix)


def call(kernel, outs, *args, scratch=(), scalars=0, fetched=0):
    n_in, n_out = len(args), len(outs)
    spaces = [pltpu.SMEM] * scalars + [pltpu.VMEM] * (n_in - scalars - fetched) + [pl.ANY] * fetched
    landing = [pltpu.VMEM(a.shape, a.dtype) for a in args[n_in - fetched :]] if fetched else []

    def run(*refs):
        ins, outputs, rest = refs[:n_in], refs[n_in : n_in + n_out], refs[n_in + n_out :]
        if fetched:
            held, sems, rest = rest[:fetched], rest[fetched], rest[fetched + 1 :]
            copies = [
                pltpu.make_async_copy(src, dst, sems.at[k])
                for k, (src, dst) in enumerate(zip(ins[n_in - fetched :], held))
            ]
            for copy in copies:
                copy.start()
            for copy in copies:
                copy.wait()
            ins = ins[: n_in - fetched] + held
        kernel(*ins, *outputs, *rest)

    return pl.pallas_call(
        run,
        out_shape=[jax.ShapeDtypeStruct(shape, F32) for shape in outs],
        in_specs=[pl.BlockSpec(memory_space=space) for space in spaces],
        out_specs=[pl.BlockSpec(memory_space=pltpu.VMEM)] * n_out,
        scratch_shapes=[*landing, *([pltpu.SemaphoreType.DMA((fetched,))] if fetched else []), *scratch],
    )(*args)


def swap(a, b, axis, closed):
    n = lax.axis_size(axis)
    first = [(i, i ^ 1 if i ^ 1 < n else i) for i in range(n)]
    last = lambda i: i - 1 if i % 2 == 0 else i + 1
    if closed and n % 2 == 0:
        second = [(i, last(i) % n) for i in range(n)]
    else:
        second = [(i, last(i) if 0 <= last(i) < n else i) for i in range(n)]
    return lax.ppermute(a, axis, first), lax.ppermute(b, axis, second)


def shards(rhs, start, valid, reg, shifts, frac):
    rows = rhs.shape[1]
    guides = valid.shape[0]
    slots = lax.axis_size("layer")
    gx, gy = lax.axis_index("gx"), lax.axis_index("gy")
    n_gx, n_gy = lax.axis_size("gx"), lax.axis_size("gy")
    at = jnp.arange(8, dtype=jnp.int32)
    meta = jnp.zeros((8,), jnp.int32)
    for k, value in enumerate(
        (gx > 0, gx < n_gx - 1, gy > 0, gy < n_gy - 1, lax.axis_index("layer"), gx & 1, gy & 1)
    ):
        meta = jnp.where(at == k, value.astype(jnp.int32), meta)
    shifts, frac = shifts.reshape(-1), frac.reshape(-1)
    pairs, maps = (slots + 1) // 2, (guides + 1) // 2
    vmem = lambda *shape: pltpu.VMEM((*shape, LANES), F32)

    xr = pl.pallas_call(
        order_inputs,
        out_shape=jax.ShapeDtypeStruct((2 * rows + 8, LANES), F32),
        in_specs=[pl.BlockSpec(memory_space=pltpu.VMEM)] * 2 + [pl.BlockSpec(memory_space=pltpu.SMEM)],
        out_specs=pl.BlockSpec(memory_space=pltpu.VMEM),
    )(start, rhs, reg)
    strip = (maps * 2 * V_HALO, LANES)
    v_own, va, vb = call(order_valid, ((maps, 2, rows, LANES), strip, strip), meta, valid, scalars=1)
    va, vb = swap(va, vb, "gx", False)
    others = [lax.ppermute(xr, "layer", [(i, (i + k) % slots) for i in range(slots)]) for k in range(1, slots)]
    tile = (pairs, 2, rows, LANES)
    strip = (pairs * 2 * (X_HALO + R_HALO), LANES)
    x_own, r_own, weights, xa, xb = call(
        functools.partial(pair_inputs, slots, rows),
        (tile, tile, (8 * slots, LANES), strip, strip),
        meta, xr, *others,
        scalars=1, fetched=len(others),
    )
    xa, xb = swap(xa, xb, "gx", False)
    near = (pairs * (2 * rows + 2 * X_HALO + 2 * R_HALO) + maps * (rows + 2 * V_NEAR), LANES)
    far = (maps * 2 * (V_HALO - V_NEAR), LANES)
    ga, gb, fa, fb = call(
        pack_first, (near, near, far, far), meta, x_own, r_own, v_own, xa, xb, va, vb, scalars=1, fetched=4
    )
    ga, gb = swap(ga, gb, "gy", False)
    fa, fb = swap(fa, fb, "gy", False)

    size = rows + 2 * DEPTH1 + 16
    strip = (pairs * 2 * Z_HALO, LANES)
    z, za, zb, res, dot_rz = call(
        functools.partial(stage_first, slots),
        (tile, strip, strip, (2, rows, LANES), (8, LANES)),
        meta, shifts, frac, x_own, r_own, v_own, weights, xa, xb, va, vb, ga, gb,
        scalars=3, fetched=6,
        scratch=[
            vmem(slots, 4, rows + 2 * X_HALO + 16),
            vmem(guides, 2, rows + 2 * V_NEAR),
            vmem(2, rows + 2 * V_NEAR + 16),
            vmem(slots, 2, size),
            vmem(slots, 2, size),
            *vcycle_scratch(DEPTH1, rows, slots),
        ],
    )
    za, zb = swap(za, zb, "gx", False)
    (spread,) = call(
        functools.partial(spread_valid, near_base=pairs * (2 * rows + 2 * X_HALO + 2 * R_HALO)),
        ((guides, 2, rows + 2 * V_HALO, LANES),),
        meta, v_own, va, vb, ga, gb, fa, fb,
        scalars=1, fetched=6,
    )
    strip = (pairs * (rows + 2 * Z_HALO), LANES)
    ka, kb = call(pack_second, (strip, strip), meta, z, za, zb, scalars=1, fetched=2)
    ka, kb = swap(ka, kb, "gy", True)

    size = rows + 2 * DEPTH2 + 16
    strip = (pairs * (rows + 2 * Y_HALO), LANES)
    y, ya, yb, image, dot_zq, dot_yq = call(
        functools.partial(stage_second, slots),
        ((pairs, 2, rows + 2 * Y_HALO, LANES), strip, strip, (2, rows, LANES), (8, LANES), (8, LANES)),
        meta, shifts, frac, z, weights, spread, za, zb, ka, kb,
        scalars=3, fetched=4,
        scratch=[
            vmem(slots, 4, rows + 2 * Z_HALO + 8),
            vmem(2, rows + 2 * V_HALO + 16),
            vmem(slots, 2, size),
            vmem(slots, 2, size),
            *vcycle_scratch(DEPTH2, rows, slots),
        ],
    )
    ya, yb = swap(ya, yb, "gy", True)

    image_y, sums = call(
        functools.partial(stage_third, slots),
        ((2, rows, LANES), (n_gx * n_gy, 8, LANES)),
        meta, shifts, frac, y, weights, spread, dot_rz, dot_zq, dot_yq, ya, yb,
        scalars=3, fetched=2,
        scratch=[
            vmem(slots, 4, rows + 2 * Y_HALO + 8),
            vmem(2, rows + 48),
            vmem(1, 2, rows),
            vmem(2, rows + 16),
            vmem(8),
            vmem(min(slots, 2), rows + 16),
        ],
    )
    sums = lax.all_to_all(sums, ("gx", "gy"), 0, 0)
    return call(finish, ((1, rows, LANES), (1, rows, LANES)), start, z, res, image, y, image_y, sums)


def solution(mesh):
    in_specs = (
        P("layer", "gx", "gy"),
        P("layer", "gx", "gy"),
        P(None, "gx", "gy"),
        P("layer"),
        P(),
        P(),
    )
    out_specs = (P("layer", "gx", "gy"), P("layer", "gx", "gy"))

    def run(*args):
        return tuple(jax.shard_map(shards, mesh=mesh, in_specs=in_specs, out_specs=out_specs, check_vma=False)(*args))

    return run
```

time: 624 us -> 118 us (0.19)
  blocking collectives: 171 us -> 12.6 us
  waiting for transfers between devices: 134 us -> 10.6 us
  starting transfers between devices: 157 us -> 35.5 us
  between operations: 90.7 us -> 1.49 us
  Pallas kernels: 0 us -> 47.9 us
  local copies, waits for them, and re-layouts: 41.1 us -> 8.03 us
  other arithmetic: 26.1 us -> 0.51 us
    ppermute x76 -> x15, waiting for transfers between devices: 133 us -> 10.6 us  [the longest x14 6.91 us: swap(): return (lax.ppermute(a, axis, first), lax.ppermute(b, axis, second))]
    ppermute x76 -> x15, starting transfers between devices: 157 us -> 35.5 us  [the longest x14 34 us: swap(): return (lax.ppermute(a, axis, first), lax.ppermute(b, axis, second))]
    psum x3 -> x0, blocking collectives: 120 us -> none  [global_sum(): return lax.psum(jnp.sum(values), ('layer', 'gx', 'gy'))]
    all_gather x3 -> x0, blocking collectives: 50.2 us -> none  [operator_a(): lax.all_gather(padded_m, 'layer', axis=0, tiled=True)]
    pallas_call x0 -> x10, Pallas kernels: none -> 47.9 us  [the longest x9 46.2 us: call(): pl.pallas_call(run, out_shape=[jax.ShapeDtypeStruct(shape, F32) for shape...]
    all_to_all x0 -> x1, blocking collectives: none -> 12.6 us  [shards(): sums = lax.all_to_all(sums, ('gx', 'gy'), 0, 0)]
    reshape x10 -> x2, local copies, waits for them, and re-layouts: 13.6 us -> 1.36 us  [shards(): shifts, frac = (shifts.reshape(-1), frac.reshape(-1))]
    unnamed x111 -> x40, local copies, waits for them, and re-layouts: 17 us -> 6.67 us
  transfers between devices with their start and end apart: 79 -> 15, of which waited for: 44 -> 5; matrix products, arithmetic and copies ran while one was open for 1% -> 1% of each run, Pallas kernels for 0% -> 8%
where the time goes in v2:
time: 118 us; the launch traced here: 117 us
  Pallas kernels  47.9 us (41%)
  starting transfers between devices  35.5 us (30%)
  blocking collectives  12.6 us (11%)
  waiting for transfers between devices  10.6 us (9%)
  local copies, waits for them, and re-layouts  8.03 us (7%)
  between operations  1.49 us (1%)
    pallas_call x9, Pallas kernels, call(): pl.pallas_call(run, out_shape=[jax.ShapeDtypeStruct(shape, F32) for shape...  46.2 us
    ppermute x14, starting transfers between devices, swap(): return (lax.ppermute(a, axis, first), lax.ppermute(b, axis, second))  34 us
    all_to_all x1, blocking collectives, shards(): sums = lax.all_to_all(sums, ('gx', 'gy'), 0, 0)  12.6 us
    ppermute x14, waiting for transfers between devices, swap(): return (lax.ppermute(a, axis, first), lax.ppermute(b, axis, second))  6.91 us
    unnamed x40, local copies, waits for them, and re-layouts  6.67 us
    ppermute x1, waiting for transfers between devices, shards(): lax.ppermute(xr, 'layer', [(i, (i + k) % slots) for i in range(slots)])  3.74 us
  transfers between devices with their start and end apart: 15, of which 5 were waited for; matrix products, arithmetic and copies ran while one was open for 1% of the time, Pallas kernels for 8%

profile of v2, /device:TPU:0, one launch (start us, length us, event | category | flops | bytes accessed | tf_op | source)
XLA Modules:
  0.0 116.8 jit_solution(17009697587084411825)
XLA Ops:
  1.2 2.4 %shard_map.79 = (f32[4,2,128,128]{3,2,1,0:T(8,128)}, f32[576,128]{1,0:T(8,128)}, f32[576,128]{1,0:T(8,128)}) custom-call(s32[8]{0:T(128)} %compare_select_fusion.6.refs_0_, s32[8,128,128]{2,1,0:T(8,128)} %refs_1_.1), custom_call_target="tpu_custom_call" | custom-call | tf_op jit(solution)/shard_map/pallas_call | solution.py:687
  3.5 3.0 %collective-permute-start.3 = (f32[576,128]{1,0:T(8,128)}, f32[576,128]{1,0:T(8,128)S(1)}, u32[]{:S(2)}, u32[]{:S(2)}) collective-permute-start(f32[576,128]{1,0:T(8,128)} %get-tuple-element.35), channel_id=1, source_target_pairs={{0,4},{4,0},{8,12},{12,8},{1,5},{5,1},{9,13},{13,9},{2,6},{6,2},{1... | collective-permute-start | bytes 884744 | tf_op jit(solution)/shard_map/ppermute | solution.py:704
  6.6 1.6 %collective-permute-start.4 = (f32[576,128]{1,0:T(8,128)}, f32[576,128]{1,0:T(8,128)S(1)}, u32[]{:S(2)}, u32[]{:S(2)}) collective-permute-start(f32[576,128]{1,0:T(8,128)} %get-tuple-element.36), channel_id=1, source_target_pairs={{0,0},{4,8},{8,4},{12,12},{1,1},{5,9},{9,5},{13,13},{2,2},{6,10},{... | collective-permute-start | bytes 884744 | tf_op jit(solution)/shard_map/ppermute | solution.py:704
  8.8 1.7 %shard_map.77.refs_1_ = f32[264,128]{1,0:T(8,128)} custom-call(f32[1,128,128]{2,1,0:T(8,128)} %refs_0_.1, f32[1,128,128]{2,1,0:T(8,128)} %rhs_ref.1, f32[1]{0:T(128)S(6)} %copy.12.reg_ref), custom_call_target="tpu_custom_call" | custom-call | tf_op jit(solution)/shard_map/pallas_call | solution.py:723
  10.5 1.5 %collective-permute-start = (f32[264,128]{1,0:T(8,128)}, f32[264,128]{1,0:T(8,128)S(1)}, u32[]{:S(2)}, u32[]{:S(2)}) collective-permute-start(f32[264,128]{1,0:T(8,128)} %shard_map.77.refs_1_), channel_id=1, source_target_pairs={{0,16},{16,0},{1,17},{17,1},{2,18},{18,2},{3,19},{19,3},{4,20},{20... | collective-permute-start | bytes 405512 | tf_op jit(solution)/shard_map/ppermute | solution.py:732
  12.1 3.7 %collective-permute-done.refs_2_ = f32[264,128]{1,0:T(8,128)S(1)} collective-permute-done((f32[264,128]{1,0:T(8,128)}, f32[264,128]{1,0:T(8,128)S(1)}, u32[]{:S(2)}, u32[]{:S(2)}) %collective-permute-start) | collective-permute-done | bytes 135200 | tf_op jit(solution)/shard_map/ppermute | solution.py:732
  16.4 2.7 %shard_map.78 = (f32[1,2,128,128]{3,2,1,0:T(8,128)}, f32[1,2,128,128]{3,2,1,0:T(8,128)}, f32[16,128]{1,0:T(8,128)}, f32[160,128]{1,0:T(8,128)}, f32[160,128]{1,0:T(8,128)}) custom-call(s32[8]{0:T(128)} %compare_select_fusion.6.refs_0_, f32[264,128]{1,0:T(8,128)} %shard_map.77.refs_1_, f32[264,128]{1,0:T(8,128)} %copy-done.10), custom_call_target="tpu_custom_call" | custom-call | tf_op jit(solution)/shard_map/pallas_call | solution.py:687
  19.2 3.5 %collective-permute-start.1 = (f32[160,128]{1,0:T(8,128)}, f32[160,128]{1,0:T(8,128)S(1)}, u32[]{:S(2)}, u32[]{:S(2)}) collective-permute-start(f32[160,128]{1,0:T(8,128)} %get-tuple-element.33), channel_id=1, source_target_pairs={{0,4},{4,0},{8,12},{12,8},{1,5},{5,1},{9,13},{13,9},{2,6},{6,2},{1... | collective-permute-start | bytes 245768 | tf_op jit(solution)/shard_map/ppermute | solution.py:704
  22.7 1.5 %collective-permute-start.2 = (f32[160,128]{1,0:T(8,128)}, f32[160,128]{1,0:T(8,128)S(1)}, u32[]{:S(2)}, u32[]{:S(2)}) collective-permute-start(f32[160,128]{1,0:T(8,128)} %get-tuple-element.34), channel_id=1, source_target_pairs={{0,0},{4,8},{8,4},{12,12},{1,1},{5,9},{9,5},{13,13},{2,2},{6,10},{... | collective-permute-start | bytes 245768 | tf_op jit(solution)/shard_map/ppermute | solution.py:704
  24.2 1.1 collective-permute-done.1.refs_4_.refs_7_
  26.2 3.8 %shard_map.80 = (f32[1248,128]{1,0:T(8,128)}, f32[1248,128]{1,0:T(8,128)}, f32[256,128]{1,0:T(8,128)}, f32[256,128]{1,0:T(8,128)}) custom-call(s32[8]{0:T(128)} %compare_select_fusion.6.refs_0_, f32[1,2,128,128]{3,2,1,0:T(8,128)} %get-tuple-element.29.refs_1_.refs_3_, f32[1,2,128,128]{3,2,1,0:T(8,128)} %get-tuple-element.30.refs_2_.refs_4_, ...), custom_call_target="tpu_custom_call" | custom-call | tf_op jit(solution)/shard_map/pallas_call | solution.py:687
  30.1 1.9 %collective-permute-start.6 = (f32[1248,128]{1,0:T(8,128)}, f32[1248,128]{1,0:T(8,128)S(1)}, u32[]{:S(2)}, u32[]{:S(2)}) collective-permute-start(f32[1248,128]{1,0:T(8,128)} %get-tuple-element.38), channel_id=1, source_target_pairs={{0,0},{1,2},{2,1},{3,3},{4,4},{5,6},{6,5},{7,7},{8,8},{9,10},{10,9... | collective-permute-start | bytes 1916936 | tf_op jit(solution)/shard_map/ppermute | solution.py:704
  32.0 0.7 reshape.10.refs_1_
  32.8 0.7 reshape.11.refs_2_
  33.5 0.8 copy-done.2
  34.5 10.2 %shard_map.81 = (f32[1,2,128,128]{3,2,1,0:T(8,128)}, f32[176,128]{1,0:T(8,128)}, f32[176,128]{1,0:T(8,128)}, f32[2,128,128]{2,1,0:T(8,128)}, f32[8,128]{1,0:T(8,128)}) custom-call(s32[8]{0:T(128)} %compare_select_fusion.6.refs_0_, s32[32]{0:T(128)} %reshape.10.refs_1_, s32[32]{0:T(128)} %reshape.11.refs_2_, ...), custom_call_target="tpu_custom_call" | custom-call | tf_op jit(solution)/shard_map/pallas_call | solution.py:687
  44.8 4.0 %collective-permute-start.9 = (f32[176,128]{1,0:T(8,128)}, f32[176,128]{1,0:T(8,128)S(1)}, u32[]{:S(2)}, u32[]{:S(2)}) collective-permute-start(f32[176,128]{1,0:T(8,128)} %get-tuple-element.43), channel_id=1, source_target_pairs={{0,4},{4,0},{8,12},{12,8},{1,5},{5,1},{9,13},{13,9},{2,6},{6,2},{1... | collective-permute-start | bytes 270344 | tf_op jit(solution)/shard_map/ppermute | solution.py:704
  48.7 1.5 %collective-permute-start.10 = (f32[176,128]{1,0:T(8,128)}, f32[176,128]{1,0:T(8,128)S(1)}, u32[]{:S(2)}, u32[]{:S(2)}) collective-permute-start(f32[176,128]{1,0:T(8,128)} %get-tuple-element.44), channel_id=1, source_target_pairs={{0,0},{4,8},{8,4},{12,12},{1,1},{5,9},{9,5},{13,13},{2,2},{6,10},{... | collective-permute-start | bytes 270344 | tf_op jit(solution)/shard_map/ppermute | solution.py:704
  50.3 1.2 %collective-permute-done.9.refs_2_.refs_6_ = f32[176,128]{1,0:T(8,128)S(1)} collective-permute-done((f32[176,128]{1,0:T(8,128)}, f32[176,128]{1,0:T(8,128)S(1)}, u32[]{:S(2)}, u32[]{:S(2)}) %collective-permute-start.9) | collective-permute-done | bytes 90144 | tf_op jit(solution)/shard_map/ppermute | solution.py:704
  52.1 2.7 %shard_map.83 = (f32[304,128]{1,0:T(8,128)}, f32[304,128]{1,0:T(8,128)}) custom-call(s32[8]{0:T(128)} %compare_select_fusion.6.refs_0_, f32[1,2,128,128]{3,2,1,0:T(8,128)} %get-tuple-element.39.refs_1_.refs_3_, f32[176,128]{1,0:T(8,128)} %copy-done.4, f32[176,128]{1,0:T(8,128)} %copy-done.5), custom_call_target="tpu_custom_call" | custom-call | tf_op jit(solution)/shard_map/pallas_call | solution.py:687
  54.8 8.0 %collective-permute-start.11 = (f32[304,128]{1,0:T(8,128)}, f32[304,128]{1,0:T(8,128)S(1)}, u32[]{:S(2)}, u32[]{:S(2)}) collective-permute-start(f32[304,128]{1,0:T(8,128)} %get-tuple-element.45), channel_id=1, source_target_pairs={{0,1},{1,0},{2,3},{3,2},{4,5},{5,4},{6,7},{7,6},{8,9},{9,8},{10,11... | collective-permute-start | bytes 466952 | tf_op jit(solution)/shard_map/ppermute | solution.py:704
  62.8 2.1 %collective-permute-start.12 = (f32[304,128]{1,0:T(8,128)}, f32[304,128]{1,0:T(8,128)S(1)}, u32[]{:S(2)}, u32[]{:S(2)}) collective-permute-start(f32[304,128]{1,0:T(8,128)} %get-tuple-element.46), channel_id=1, source_target_pairs={{0,3},{1,2},{2,1},{3,0},{4,7},{5,6},{6,5},{7,4},{8,11},{9,10},{10,... | collective-permute-start | bytes 466952 | tf_op jit(solution)/shard_map/ppermute | solution.py:704
  65.0 0.7 collective-permute-start.8
  66.3 0.7 copy-done.11
  67.6 4.3 %shard_map.82.refs_5_ = f32[8,2,272,128]{3,2,1,0:T(8,128)} custom-call(s32[8]{0:T(128)} %compare_select_fusion.6.refs_0_, f32[4,2,128,128]{3,2,1,0:T(8,128)} %get-tuple-element.31.refs_3_.refs_5_.refs_1_, f32[576,128]{1,0:T(8,128)} %copy-done, f32[576,128]{1,0:T(8,128)} %copy-done.1, f32[1248,128]{1,0:T(8,128)} %copy-done.2, f32[1248,128]{1,0:T(8,128)} %copy-done.3, ...), custom_call_target="tpu_custom_call" | custom-call | tf_op jit(solution)/shard_map/pallas_call | solution.py:687
  73.3 11.3 %shard_map.84 = (f32[1,2,208,128]{3,2,1,0:T(8,128)}, f32[208,128]{1,0:T(8,128)}, f32[208,128]{1,0:T(8,128)}, f32[2,128,128]{2,1,0:T(8,128)}, f32[8,128]{1,0:T(8,128)}, /*index=5*/f32[8,128]{1,0:T(8,128)}) custom-call(s32[8]{0:T(128)} %compare_select_fusion.6.refs_0_, s32[32]{0:T(128)} %reshape.10.refs_1_, s32[32]{0:T(128)} %reshape.11.refs_2_, ...), custom_call_target="tpu_custom_call" | custom-call | tf_op jit(solution)/shard_map/pallas_call | solution.py:687
  84.6 4.8 %collective-permute-start.13 = (f32[208,128]{1,0:T(8,128)}, f32[208,128]{1,0:T(8,128)S(1)}, u32[]{:S(2)}, u32[]{:S(2)}) collective-permute-start(f32[208,128]{1,0:T(8,128)} %get-tuple-element.52), channel_id=1, source_target_pairs={{0,1},{1,0},{2,3},{3,2},{4,5},{5,4},{6,7},{7,6},{8,9},{9,8},{10,11... | collective-permute-start | bytes 319496 | tf_op jit(solution)/shard_map/ppermute | solution.py:704
  89.5 1.2 %collective-permute-start.14 = (f32[208,128]{1,0:T(8,128)}, f32[208,128]{1,0:T(8,128)S(1)}, u32[]{:S(2)}, u32[]{:S(2)}) collective-permute-start(f32[208,128]{1,0:T(8,128)} %get-tuple-element.53), channel_id=1, source_target_pairs={{0,3},{1,2},{2,1},{3,0},{4,7},{5,6},{6,5},{7,4},{8,11},{9,10},{10,... | collective-permute-start | bytes 319496 | tf_op jit(solution)/shard_map/ppermute | solution.py:704
  90.7 4.0 %collective-permute-done.14.refs_10_ = f32[208,128]{1,0:T(8,128)S(1)} collective-permute-done((f32[208,128]{1,0:T(8,128)}, f32[208,128]{1,0:T(8,128)S(1)}, u32[]{:S(2)}, u32[]{:S(2)}) %collective-permute-start.14) | collective-permute-done | bytes 106528 | tf_op jit(solution)/shard_map/ppermute | solution.py:704
  95.3 6.6 %shard_map.85 = (f32[2,128,128]{2,1,0:T(8,128)}, f32[16,8,128]{2,1,0:T(8,128)}) custom-call(s32[8]{0:T(128)} %compare_select_fusion.6.refs_0_, s32[32]{0:T(128)} %reshape.10.refs_1_, s32[32]{0:T(128)} %reshape.11.refs_2_, f32[1,2,208,128]{3,2,1,0:T(8,128)} %get-tuple-element.48.refs_3_.refs_4_, f32[16,128]{1,0:T(8,128)} %get-tuple-element.32.refs_6_.refs_4_, ...), custom_call_target="tpu_custom_call" | custom-call | tf_op jit(solution)/shard_map/pallas_call | solution.py:687
  101.9 12.6 %all_to_all.5.refs_6_ = f32[16,8,128]{2,1,0:T(8,128)} all-to-all(f32[16,8,128]{2,1,0:T(8,128)} %get-tuple-element.55), channel_id=1, replica_groups=mesh['layer'=2,'gx'=4,'gy'=4] {'gx','gy'}, dimensions={0} | all-to-all | bytes 131072 | tf_op jit(solution)/shard_map/all_to_all | solution.py:808
  114.5 2.3 %shard_map.86 = (f32[1,128,128]{2,1,0:T(8,128)}, f32[1,128,128]{2,1,0:T(8,128)}) custom-call(f32[1,128,128]{2,1,0:T(8,128)} %refs_0_.1, f32[1,2,128,128]{3,2,1,0:T(8,128)} %get-tuple-element.39.refs_1_.refs_3_, f32[2,128,128]{2,1,0:T(8,128)} %get-tuple-element.40.refs_2_, f32[2,128,128]{2,1,0:T(8,128)} %get-tuple-element.47.refs_3_, ...), custom_call_target="tpu_custom_call" | custom-call | tf_op jit(solution)/shard_map/pallas_call | solution.py:687
  (52 shorter events, 6.5 us)
Async XLA Ops:
  0.6 31.3 %copy-start.15 = (s32[8,2,2]{0,2,1:T(2,128)S(1)}, s32[8,2,2]{0,2,1:T(2,128)}, u32[]{:S(2)}) copy-start(s32[8,2,2]{0,2,1:T(2,128)} %param.10) | copy-start | bytes 388
  0.6 32.1 %copy-start.16 = (s32[8,2,2]{0,2,1:T(2,128)S(1)}, s32[8,2,2]{0,2,1:T(2,128)}, u32[]{:S(2)}) copy-start(s32[8,2,2]{0,2,1:T(2,128)} %param.11) | copy-start | bytes 388
  3.5 21.8 %collective-permute-start.3 = (f32[576,128]{1,0:T(8,128)}, f32[576,128]{1,0:T(8,128)S(1)}, u32[]{:S(2)}, u32[]{:S(2)}) collective-permute-start(f32[576,128]{1,0:T(8,128)} %get-tuple-element.35), channel_id=1, source_target_pairs={{0,4},{4,0},{8,12},{12,8},{1,5},{5,1},{9,13},{13,9},{2,6},{6,2},{1... | collective-permute-start | bytes 884744 | tf_op jit(solution)/shard_map/ppermute | solution.py:704
  6.6 18.8 %collective-permute-start.4 = (f32[576,128]{1,0:T(8,128)}, f32[576,128]{1,0:T(8,128)S(1)}, u32[]{:S(2)}, u32[]{:S(2)}) collective-permute-start(f32[576,128]{1,0:T(8,128)} %get-tuple-element.36), channel_id=1, source_target_pairs={{0,0},{4,8},{8,4},{12,12},{1,1},{5,9},{9,5},{13,13},{2,2},{6,10},{... | collective-permute-start | bytes 884744 | tf_op jit(solution)/shard_map/ppermute | solution.py:704
  10.5 5.3 %collective-permute-start = (f32[264,128]{1,0:T(8,128)}, f32[264,128]{1,0:T(8,128)S(1)}, u32[]{:S(2)}, u32[]{:S(2)}) collective-permute-start(f32[264,128]{1,0:T(8,128)} %shard_map.77.refs_1_), channel_id=1, source_target_pairs={{0,16},{16,0},{1,17},{17,1},{2,18},{18,2},{3,19},{19,3},{4,20},{20... | collective-permute-start | bytes 405512 | tf_op jit(solution)/shard_map/ppermute | solution.py:732
  15.8 0.7 copy-start.10
  19.2 6.1 %collective-permute-start.1 = (f32[160,128]{1,0:T(8,128)}, f32[160,128]{1,0:T(8,128)S(1)}, u32[]{:S(2)}, u32[]{:S(2)}) collective-permute-start(f32[160,128]{1,0:T(8,128)} %get-tuple-element.33), channel_id=1, source_target_pairs={{0,4},{4,0},{8,12},{12,8},{1,5},{5,1},{9,13},{13,9},{2,6},{6,2},{1... | collective-permute-start | bytes 245768 | tf_op jit(solution)/shard_map/ppermute | solution.py:704
  22.7 2.6 %collective-permute-start.2 = (f32[160,128]{1,0:T(8,128)}, f32[160,128]{1,0:T(8,128)S(1)}, u32[]{:S(2)}, u32[]{:S(2)}) collective-permute-start(f32[160,128]{1,0:T(8,128)} %get-tuple-element.34), channel_id=1, source_target_pairs={{0,0},{4,8},{8,4},{12,12},{1,1},{5,9},{9,5},{13,13},{2,2},{6,10},{... | collective-permute-start | bytes 245768 | tf_op jit(solution)/shard_map/ppermute | solution.py:704
  25.3 0.7 copy-start.7
  25.3 0.8 copy-start
  25.3 0.9 copy-start.1
  30.0 35.0 %copy-start.18 = (f32[256,128]{1,0:T(8,128)S(1)}, f32[256,128]{1,0:T(8,128)}, u32[]{:S(2)}) copy-start(f32[256,128]{1,0:T(8,128)} %get-tuple-element.41) | copy-start | bytes 393220
  30.0 35.0 %copy-start.17 = (f32[256,128]{1,0:T(8,128)S(1)}, f32[256,128]{1,0:T(8,128)}, u32[]{:S(2)}) copy-start(f32[256,128]{1,0:T(8,128)} %get-tuple-element.42) | copy-start | bytes 393220
  30.0 3.5 %collective-permute-start.5 = (f32[1248,128]{1,0:T(8,128)}, f32[1248,128]{1,0:T(8,128)S(1)}, u32[]{:S(2)}, u32[]{:S(2)}) collective-permute-start(f32[1248,128]{1,0:T(8,128)} %get-tuple-element.37), channel_id=1, source_target_pairs={{0,1},{1,0},{2,3},{3,2},{4,5},{5,4},{6,7},{7,6},{8,9},{9,8},{10,11... | collective-permute-start | bytes 1916936 | tf_op jit(solution)/shard_map/ppermute | solution.py:704
  30.1 3.4 %collective-permute-start.6 = (f32[1248,128]{1,0:T(8,128)}, f32[1248,128]{1,0:T(8,128)S(1)}, u32[]{:S(2)}, u32[]{:S(2)}) collective-permute-start(f32[1248,128]{1,0:T(8,128)} %get-tuple-element.38), channel_id=1, source_target_pairs={{0,0},{1,2},{2,1},{3,3},{4,4},{5,6},{6,5},{7,7},{8,8},{9,10},{10,9... | collective-permute-start | bytes 1916936 | tf_op jit(solution)/shard_map/ppermute | solution.py:704
  33.5 0.8 copy-start.2
  33.5 1.0 copy-start.3
  44.8 6.7 %collective-permute-start.9 = (f32[176,128]{1,0:T(8,128)}, f32[176,128]{1,0:T(8,128)S(1)}, u32[]{:S(2)}, u32[]{:S(2)}) collective-permute-start(f32[176,128]{1,0:T(8,128)} %get-tuple-element.43), channel_id=1, source_target_pairs={{0,4},{4,0},{8,12},{12,8},{1,5},{5,1},{9,13},{13,9},{2,6},{6,2},{1... | collective-permute-start | bytes 270344 | tf_op jit(solution)/shard_map/ppermute | solution.py:704
  48.7 2.7 %collective-permute-start.10 = (f32[176,128]{1,0:T(8,128)}, f32[176,128]{1,0:T(8,128)S(1)}, u32[]{:S(2)}, u32[]{:S(2)}) collective-permute-start(f32[176,128]{1,0:T(8,128)} %get-tuple-element.44), channel_id=1, source_target_pairs={{0,0},{4,8},{8,4},{12,12},{1,1},{5,9},{9,5},{13,13},{2,2},{6,10},{... | collective-permute-start | bytes 270344 | tf_op jit(solution)/shard_map/ppermute | solution.py:704
  51.5 0.7 copy-start.4
  51.5 0.7 copy-start.5
  54.8 17.2 %collective-permute-start.11 = (f32[304,128]{1,0:T(8,128)}, f32[304,128]{1,0:T(8,128)S(1)}, u32[]{:S(2)}, u32[]{:S(2)}) collective-permute-start(f32[304,128]{1,0:T(8,128)} %get-tuple-element.45), channel_id=1, source_target_pairs={{0,1},{1,0},{2,3},{3,2},{4,5},{5,4},{6,7},{7,6},{8,9},{9,8},{10,11... | collective-permute-start | bytes 466952 | tf_op jit(solution)/shard_map/ppermute | solution.py:704
  62.8 9.2 %collective-permute-start.12 = (f32[304,128]{1,0:T(8,128)}, f32[304,128]{1,0:T(8,128)S(1)}, u32[]{:S(2)}, u32[]{:S(2)}) collective-permute-start(f32[304,128]{1,0:T(8,128)} %get-tuple-element.46), channel_id=1, source_target_pairs={{0,3},{1,2},{2,1},{3,0},{4,7},{5,6},{6,5},{7,4},{8,11},{9,10},{10,... | collective-permute-start | bytes 466952 | tf_op jit(solution)/shard_map/ppermute | solution.py:704
  65.0 1.3 %collective-permute-start.7 = (f32[256,128]{1,0:T(8,128)S(1)}, f32[256,128]{1,0:T(8,128)S(1)}, u32[]{:S(2)}, u32[]{:S(2)}) collective-permute-start(f32[256,128]{1,0:T(8,128)S(1)} %copy-done.18), channel_id=1, source_target_pairs={{0,1},{1,0},{2,3},{3,2},{4,5},{5,4},{6,7},{7,6},{8,9},{9,8},{10,11... | collective-permute-start | bytes 393224 | tf_op jit(solution)/shard_map/ppermute | solution.py:704
  65.0 1.3 %collective-permute-start.8 = (f32[256,128]{1,0:T(8,128)S(1)}, f32[256,128]{1,0:T(8,128)S(1)}, u32[]{:S(2)}, u32[]{:S(2)}) collective-permute-start(f32[256,128]{1,0:T(8,128)S(1)} %copy-done.17), channel_id=1, source_target_pairs={{0,0},{1,2},{2,1},{3,3},{4,4},{5,6},{6,5},{7,7},{8,8},{9,10},{10,9... | collective-permute-start | bytes 393224 | tf_op jit(solution)/shard_map/ppermute | solution.py:704
  66.3 0.7 copy-start.11
  67.0 0.7 copy-start.12
  72.0 0.7 copy-start.8
  72.7 0.7 copy-start.9
  84.6 6.1 %collective-permute-start.13 = (f32[208,128]{1,0:T(8,128)}, f32[208,128]{1,0:T(8,128)S(1)}, u32[]{:S(2)}, u32[]{:S(2)}) collective-permute-start(f32[208,128]{1,0:T(8,128)} %get-tuple-element.52), channel_id=1, source_target_pairs={{0,1},{1,0},{2,3},{3,2},{4,5},{5,4},{6,7},{7,6},{8,9},{9,8},{10,11... | collective-permute-start | bytes 319496 | tf_op jit(solution)/shard_map/ppermute | solution.py:704
  89.5 5.2 %collective-permute-start.14 = (f32[208,128]{1,0:T(8,128)}, f32[208,128]{1,0:T(8,128)S(1)}, u32[]{:S(2)}, u32[]{:S(2)}) collective-permute-start(f32[208,128]{1,0:T(8,128)} %get-tuple-element.53), channel_id=1, source_target_pairs={{0,3},{1,2},{2,1},{3,0},{4,7},{5,6},{6,5},{7,4},{8,11},{9,10},{10,... | collective-permute-start | bytes 319496 | tf_op jit(solution)/shard_map/ppermute | solution.py:704
  90.7 4.0 %copy-start.13 = (f32[208,128]{1,0:T(8,128)}, f32[208,128]{1,0:T(8,128)S(1)}, u32[]{:S(2)}) copy-start(f32[208,128]{1,0:T(8,128)S(1)} %collective-permute-done.13.refs_9_) | copy-start | bytes 319492
  (2 other events, 1.3 us)

commit v3 on v2

--- a/solution.py
+++ b/solution.py
@@ -18,6 +18,8 @@
 
 X_HALO, R_HALO, V_HALO, V_NEAR, Z_HALO, Y_HALO = 56, 24, 72, 40, 88, 40
 DEPTH1, DEPTH2 = 24, 56
+VMEM_LIMIT = 16 << 20
+V_CLOSED = True
 
 
 def lane_iota(shape=(1, LANES)):
@@ -123,30 +125,31 @@
     return by_row * jnp.where(lane < HALF, 1.0, jnp.where(lane < 3 * QUART, meta.right_ok, meta.left_ok))
 
 
-def guide_loop(meta, shifts_ref, frac_ref, x, valid, m, acc, p_rows, outs, slots, out_slots, square_ref=None, rows=None):
-    (x_ref, x_base), (valid_ref, v_base), (m_ref, m_base), (acc_ref, acc_base) = x, valid, m, acc
-
+def guide_loop(meta, table_ref, guides, slots, x=None, valid=None, m=None, acc=None, p_rows=None, outs=None, out_slots=None, footprints=None, square_ref=None, rows=None):
     def coefficients(g, slot):
         layer = lax.rem(meta.layer - slot + slots, slots)
         at = (g * slots + layer) * 2
+        there = guides * slots * 2
         return (
-            shifts_ref[at],
-            shifts_ref[at + 1],
-            frac_ref[at].astype(F32) * (1.0 / 256.0),
-            frac_ref[at + 1].astype(F32) * (1.0 / 256.0),
+            table_ref[at],
+            table_ref[at + 1],
+            table_ref[there + at].astype(F32) * (1.0 / 256.0),
+            table_ref[there + at + 1].astype(F32) * (1.0 / 256.0),
         )
 
     def between(ref, index, at, step, n, u):
         here = ref[index + (pl.ds(at, n), slice(None))]
         return here + u * (ref[index + (pl.ds(at + step, n), slice(None))] - here)
 
-    def body(g, carry):
+    def forward(g):
         home = HALF * (g & 1)
+        x_ref, x_base = x
         fixed = []
         for slot in range(slots):
             a, b, u, v = coefficients(g, slot)
             amount = home - HALF * (slot & 1) - lax.shift_right_arithmetic(b, 1)
             fixed.append((a, u, v, b & 1, amount & (LANES - 1)))
+        squares = []
         for r, n in spans(*p_rows, 16):
             even = odd = None
             for slot in range(slots):
@@ -156,16 +159,29 @@
                 this_odd = roll(c1 + v * (c2 - c1), amount)
                 even = this_even if even is None else even + this_even
                 odd = this_odd if odd is None else odd + this_odd
+            if footprints is not None:
+                out_ref, out_base = footprints
+                out_ref[g, 0, pl.ds(r + out_base, n), :] = even
+                out_ref[g, 1, pl.ds(r + out_base, n), :] = odd
+                continue
+            (valid_ref, v_base), (m_ref, m_base) = valid, m
             m_even = even * valid_ref[g, 0, pl.ds(r + v_base, n), :]
             m_odd = odd * valid_ref[g, 1, pl.ds(r + v_base, n), :]
             m_ref[0, pl.ds(r + m_base, n), :] = m_even
             m_ref[1, pl.ds(r + m_base, n), :] = m_odd
             if square_ref is not None:
-                own = (((lane_iota() - home) & (LANES - 1)) < HALF).astype(F32)
                 for k in range(0, n, 8):
                     if 0 <= r + k < rows:
                         sl = slice(k, k + 8)
-                        square_ref[...] += own * (m_even[sl] * even[sl] + m_odd[sl] * odd[sl])
+                        squares.append(m_even[sl] * even[sl] + m_odd[sl] * odd[sl])
+        if squares:
+            own = (((lane_iota() - home) & (LANES - 1)) < HALF).astype(F32)
+            square_ref[...] += own * total_of(squares)
+
+    def backward(g):
+        home = HALF * (g & 1)
+        (m_ref, m_base), (acc_ref, acc_base) = m, acc
+        lead = () if x is not None else (g,)
         for slot in range(out_slots):
             a, b, u, v = coefficients(g, slot)
             back = -b - 1
@@ -173,14 +189,20 @@
             amount = HALF * (slot & 1) - home - lax.shift_right_arithmetic(back, 1)
             for r, n in spans(*outs, 16):
                 at = r + m_base - a
-                plane_a = between(m_ref, (parity,), at, -1, n, u)
-                plane_b = between(m_ref, (1 - parity,), at, -1, n, u)
+                plane_a = between(m_ref, (*lead, parity), at, -1, n, u)
+                plane_b = between(m_ref, (*lead, 1 - parity), at, -1, n, u)
                 q0, q1, q2 = roll(plane_a, amount), roll(plane_b, amount - parity), roll(plane_a, amount - 1)
                 acc_ref[slot, 0, pl.ds(r + acc_base, n), :] += q1 + v * (q0 - q1)
                 acc_ref[slot, 1, pl.ds(r + acc_base, n), :] += q2 + v * (q1 - q2)
+
+    def body(g, carry):
+        if x is not None:
+            forward(g)
+        if acc is not None:
+            backward(g)
         return carry
 
-    lax.fori_loop(0, valid_ref.shape[0], body, 0)
+    lax.fori_loop(0, guides, body, 0)
 
 
 def store_field(x_ref, slot, at, n, even, odd):
@@ -216,6 +238,7 @@
         mask = mask0[pl.ds(r, n), :]
         g_ref[0, pl.ds(r, n), :] = mask * lap_even
         g_ref[1, pl.ds(r, n), :] = mask * lap_odd
+    yield
     for r, n in spans(8, 8 + size0, 16):
         bi_even, bi_odd, _, _ = five_point(g_ref, r, n)
         h_both = h_ref[0, pl.ds(r, n), :] + h_ref[1, pl.ds(r, n), :]
@@ -223,27 +246,35 @@
             h_both - s0 * (4.0 * h_both + weight * (bi_even + bi_odd))
         )
     h1[pl.ds(8, size1), :] = 0.25 * (t_ref[pl.ds(8, size1, stride=2), :] + t_ref[pl.ds(9, size1, stride=2), :])
+    yield
     for r, n in spans(8, 8 + size1, 32):
         lap, _ = five_coarse(h1, r, n, 1)
         g1[pl.ds(r, n), :] = mask1[pl.ds(r, n), :] * lap
+    yield
     for r, n in spans(8, 8 + size1, 32):
         bi, _ = five_coarse(g1, r, n, 1)
         here = h1[pl.ds(r, n), :]
         t1[pl.ds(r, n), :] = mask1[pl.ds(r, n), :] * (here - s1 * (4.0 * here + weight1 * bi))
     both = t1[pl.ds(8, size2, stride=2), :] + t1[pl.ds(9, size2, stride=2), :]
     h2[pl.ds(8, size2), :] = 0.25 * (both + jnp.where((lane & 1) == 0, roll(both, -1), roll(both, 1)))
+    yield
     lap, _ = five_coarse(h2, 8, size2, 2)
     g2[pl.ds(8, size2), :] = mask2[pl.ds(8, size2), :] * lap
+    yield
     bi, _ = five_coarse(g2, 8, size2, 2)
     here = h2[pl.ds(8, size2), :]
     e2 = mask2[pl.ds(8, size2), :] * (s2 * (2.0 * here - s2 * (4.0 * here + weight2 * bi)))
+    yield
     t1[pl.ds(8, size2, stride=2), :] = e2
     t1[pl.ds(9, size2, stride=2), :] = e2
+    yield
     for r, n in spans(8, 8 + size1, 32):
         w1[pl.ds(r, n), :] = s1 * h1[pl.ds(r, n), :] + t1[pl.ds(r, n), :]
+    yield
     for r, n in spans(8, 8 + size1, 32):
         lap, _ = five_coarse(w1, r, n, 1)
         g1[pl.ds(r, n), :] = mask1[pl.ds(r, n), :] * lap
+    yield
     for r, n in spans(8, 8 + size1, 32):
         bi, _ = five_coarse(g1, r, n, 1)
         here = w1[pl.ds(r, n), :]
@@ -251,17 +282,21 @@
             here + s1 * (h1[pl.ds(r, n), :] - 4.0 * here - weight1 * bi)
         )
     e1 = t1[pl.ds(8, size1), :]
+    yield
     t_ref[pl.ds(8, size1, stride=2), :] = e1
     t_ref[pl.ds(9, size1, stride=2), :] = e1
+    yield
     for r, n in spans(8, 8 + size0, 16):
         copied = t_ref[pl.ds(r, n), :]
         for plane in range(2):
             w_ref[plane, pl.ds(r, n), :] = s0 * h_ref[plane, pl.ds(r, n), :] + copied
+    yield
     for r, n in spans(8, 8 + size0, 16):
         lap_even, lap_odd, _, _ = five_point(w_ref, r, n)
         mask = mask0[pl.ds(r, n), :]
         g_ref[0, pl.ds(r, n), :] = mask * lap_even
         g_ref[1, pl.ds(r, n), :] = mask * lap_odd
+    yield
     for r, n in spans(8, 8 + size0, 16):
         bi = five_point(g_ref, r, n)[:2]
         mask = mask0[pl.ds(r, n), :]
@@ -272,6 +307,12 @@
             )
 
 
+def in_step(runs):
+    runs = list(runs)
+    while runs:
+        runs = [run for run in runs if next(run, runs) is not runs]
+
+
 def vcycle_scratch(depth, rows, slots):
     size0 = rows + 2 * depth
     one = lambda size: pltpu.VMEM((size + 16, LANES), F32)
@@ -279,7 +320,7 @@
     size1, size2 = size0 // 2, size0 // 4
     work = [two, two, one(size0), one(size1), one(size1), one(size1), one(size1), one(size2), one(size2)]
     positions = min(slots, 2)
-    return work + [pltpu.VMEM((positions, size + 16, LANES), F32) for size in (size0, size1, size2)]
+    return work * positions + [pltpu.VMEM((positions, size + 16, LANES), F32) for size in (size0, size1, size2)]
 
 
 def prepare_vcycle(meta, depth, rows, masks, work):
@@ -291,11 +332,12 @@
                 mask[position, pl.ds(r, n), :] = mask_rows(
                     meta, position, r - 8 - (depth >> level), n, rows >> level
                 )
-    g_ref, w_ref, t_ref, h1, g1, w1, t1, h2, g2 = work
-    for plane in range(2):
-        zero_rows(w_ref, (plane,), ((0, 8), (size0 + 8, size0 + 16)))
-    for ref, size in ((h1, sizes[1]), (g1, sizes[1]), (w1, sizes[1]), (h2, sizes[2]), (g2, sizes[2])):
-        zero_rows(ref, (), ((0, 8), (size + 8, size + 16)))
+    for k in range(0, len(work), 9):
+        g_ref, w_ref, t_ref, h1, g1, w1, t1, h2, g2 = work[k : k + 9]
+        for plane in range(2):
+            zero_rows(w_ref, (plane,), ((0, 8), (size0 + 8, size0 + 16)))
+        for ref, size in ((h1, sizes[1]), (g1, sizes[1]), (w1, sizes[1]), (h2, sizes[2]), (g2, sizes[2])):
+            zero_rows(ref, (), ((0, 8), (size + 8, size + 16)))
 
 
 def bilaplace_into(x_ref, x_base, g_ref, low, high, mask_of):
@@ -306,14 +348,18 @@
         g_ref[1, pl.ds(r - low + 8, n), :] = mask * lap_odd
 
 
+def total_of(parts):
+    while len(parts) > 1:
+        parts = [sum(parts[k : k + 2][1:], parts[k]) for k in range(0, len(parts), 2)]
+    return parts[0]
+
+
 def fold(values):
-    total = values[0:8]
-    for k in range(8, values.shape[0], 8):
-        total = total + values[k : k + 8]
-    return total
-
-
-def order_inputs(start_ref, rhs_ref, reg_ref, xr_ref):
+    return total_of([values[k : k + 8] for k in range(0, values.shape[0], 8)])
+
+
+def order_inputs(meta_ref, reg_ref, start_ref, rhs_ref, xr_ref, a_ref, b_ref):
+    meta = Meta(meta_ref)
     rows = start_ref.shape[1]
     matrix = selection(
         (LANES, LANES), lambda s, t: s == 2 * (t & (HALF - 1)) + (t >= HALF).astype(jnp.int32)
@@ -321,9 +367,11 @@
     xr_ref[pl.ds(0, rows), :] = exact_dot(start_ref[0], matrix)
     xr_ref[pl.ds(rows, rows), :] = exact_dot(rhs_ref[0], matrix)
     xr_ref[pl.ds(2 * rows, 8), :] = jnp.full((8, LANES), reg_ref[0], F32)
-
-
-def order_valid(meta_ref, valid_ref, own_ref, a_ref, b_ref):
+    send_rows(meta, lambda r, n: xr_ref[pl.ds(r, n), :], X_HALO, rows, a_ref, b_ref, 0)
+    send_rows(meta, lambda r, n: xr_ref[pl.ds(rows + r, n), :], R_HALO, rows, a_ref, b_ref, X_HALO)
+
+
+def order_valid(meta_ref, valid_ref, _, __, own_ref, a_ref, b_ref):
     meta = Meta(meta_ref)
     guides, rows = valid_ref.shape[:2]
     matrix = selection(
@@ -336,28 +384,21 @@
         planes = DOT(jnp.concatenate(pair, axis=1), matrix)
         for t in range(2):
             own_ref[q, t] = planes[:, t * LANES : (t + 1) * LANES]
-            send_rows(
-                meta, lambda r, n: own_ref[q, t, pl.ds(r, n), :], V_HALO, rows, a_ref, b_ref, (2 * q + t) * V_HALO
-            )
-
-
-def pair_inputs(slots, rows, meta_ref, *refs):
-    meta = Meta(meta_ref)
-    xr_refs, (x_ref, r_ref, reg_ref, a_ref, b_ref) = refs[:slots], refs[slots:]
-    low = lane_iota() < HALF
-    for slot in range(slots):
-        reg_ref[pl.ds(8 * slot, 8), :] = xr_refs[slot][pl.ds(2 * rows, 8), :]
-    for q in range((slots + 1) // 2):
-        first, second = xr_refs[2 * q], xr_refs[min(2 * q + 1, slots - 1)]
-        for out, at in ((x_ref, 0), (r_ref, rows)):
-            for r, n in spans(0, rows, 32):
-                one, two = first[pl.ds(at + r, n), :], second[pl.ds(at + r, n), :]
-                out[q, 0, pl.ds(r, n), :] = jnp.where(low, one, roll(two, HALF))
-                out[q, 1, pl.ds(r, n), :] = jnp.where(low, roll(one, HALF), two)
-        for t in range(2):
-            base = (2 * q + t) * (X_HALO + R_HALO)
-            send_rows(meta, lambda r, n: x_ref[q, t, pl.ds(r, n), :], X_HALO, rows, a_ref, b_ref, base)
-            send_rows(meta, lambda r, n: r_ref[q, t, pl.ds(r, n), :], R_HALO, rows, a_ref, b_ref, base + X_HALO)
+            own = lambda r, n: own_ref[q, t, pl.ds(r, n), :]
+            send_rows(meta, own, V_NEAR, rows, a_ref, b_ref, (2 * q + t) * V_NEAR)
+
+
+def input_rows(meta, slots, xrs, a_refs, b_refs, q, own_at, at, halo, rows):
+    one, two = 2 * q, min(2 * q + 1, slots - 1)
+
+    def of(refs, start):
+        def get(t, r, n):
+            first, second = refs[one][pl.ds(start + r, n), :], refs[two][pl.ds(start + r, n), :]
+            return merge(first, roll(second, HALF)) if t == 0 else merge(roll(first, HALF), second)
+
+        return get
+
+    return rows_with_halo(meta, of(xrs, own_at), of(a_refs, at), of(b_refs, at), 0, halo, rows)
 
 
 def pair_rows(meta, own_ref, a_ref, b_ref, q, stride, at, skip, halo, rows, size=16):
@@ -383,46 +424,94 @@
         base = end
 
 
-def pack_first(meta_ref, x_ref, r_ref, v_ref, xa, xb, va, vb, a_ref, b_ref, far_a, far_b):
+def pack_inputs(slots, meta_ref, *refs):
+    xrs, xa, xb = refs[:slots], refs[slots : 2 * slots], refs[2 * slots : 3 * slots]
+    _, _, out_a, out_b = refs[3 * slots :]
     meta = Meta(meta_ref)
     mask = side_mask(meta)
-    pairs, _, rows, _ = x_ref.shape
-    stride = X_HALO + R_HALO
-    groups = [(X_HALO, pair_rows(meta, x_ref, xa, xb, q, stride, 0, 0, X_HALO, rows)) for q in range(pairs)]
-    groups += [(R_HALO, pair_rows(meta, r_ref, xa, xb, q, stride, X_HALO, 0, R_HALO, rows)) for q in range(pairs)]
-    groups += [
-        (V_NEAR, pair_rows(meta, v_ref, va, vb, q, V_HALO, 0, V_HALO - V_NEAR, V_NEAR, rows))
-        for q in range(v_ref.shape[0])
-    ]
-    pack_columns(meta, mask, groups, a_ref, b_ref)
-    far = V_HALO - V_NEAR
-    for q in range(v_ref.shape[0]):
-        for r, n, get in pair_rows(meta, v_ref, va, vb, q, V_HALO, 0, 0, V_HALO, rows, 8):
-            at = r + V_HALO if r < -V_NEAR else r - rows - V_NEAR + far
-            if r < -V_NEAR or r >= rows + V_NEAR:
-                a, b = send_columns(mask, get(0), get(1))
-                far_a[pl.ds(2 * far * q + at, n), :] = a
-                far_b[pl.ds(2 * far * q + at, n), :] = b
-
-
-def spread_valid(meta_ref, v_ref, va, vb, near_a, near_b, far_a, far_b, out_ref, halo=V_HALO, near_base=0):
+    rows = (xrs[0].shape[0] - 8) // 2
+    pairs = range((slots + 1) // 2)
+    groups = [(X_HALO, input_rows(meta, slots, xrs, xa, xb, q, 0, 0, X_HALO, rows)) for q in pairs]
+    groups += [(R_HALO, input_rows(meta, slots, xrs, xa, xb, q, rows, X_HALO, R_HALO, rows)) for q in pairs]
+    pack_columns(meta, mask, groups, out_a, out_b)
+
+
+def pack_valid(meta_ref, v_ref, va, vb, _, __, v_a, v_b, far_a, far_b):
     meta = Meta(meta_ref)
     mask = side_mask(meta)
-    pairs, _, rows, _ = v_ref.shape
-    far = V_HALO - V_NEAR
-    for q in range(pairs):
-        for r, n, get in pair_rows(meta, v_ref, va, vb, q, V_HALO, 0, V_HALO - halo, halo, rows, 8):
-            if r < -V_NEAR:
-                a, b, at = far_a, far_b, 2 * far * q + r + V_HALO
-            elif r >= rows + V_NEAR:
-                a, b, at = far_a, far_b, 2 * far * q + r - rows - V_NEAR + far
-            else:
-                a, b, at = near_a, near_b, near_base + (rows + 2 * V_NEAR) * q + r + V_NEAR
-            fields = with_columns(meta, mask, get(0), get(1), a[pl.ds(at, n), :], b[pl.ds(at, n), :])
-            for k, planes in enumerate(fields):
-                if 2 * q + k < out_ref.shape[0]:
-                    for t in range(2):
-                        out_ref[2 * q + k, t, pl.ds(r + halo, n), :] = planes[t]
+    maps, _, rows, _ = v_ref.shape
+    pack_columns(
+        meta, mask,
+        [(V_NEAR, pair_rows(meta, v_ref, va, vb, q, V_NEAR, 0, 0, V_NEAR, rows)) for q in range(maps)],
+        v_a, v_b,
+    )
+    gap = V_HALO - V_NEAR
+    odd = meta.gx_odd == 1
+    for q in range(maps):
+        for t in range(2):
+            for r, n in spans(0, gap, 32):
+                up = v_ref[q, t, pl.ds(V_NEAR + r, n), :]
+                down = v_ref[q, t, pl.ds(rows - V_HALO + r, n), :]
+                far_a[pl.ds((2 * q + t) * gap + r, n), :] = jnp.where(odd, up, down)
+                far_b[pl.ds((2 * q + t) * gap + r, n), :] = jnp.where(odd, down, up)
+
+
+def far_rows(meta, fa, fb, q):
+    gap = V_HALO - V_NEAR
+    odd = meta.gx_odd == 1
+    for below in range(2):
+        scale = meta.bottom_ok if below else meta.top_ok
+        for r, n in spans(0, gap, 16):
+
+            def get(t, r=r, n=n):
+                rows_at = pl.ds((2 * q + t) * gap + r, n)
+                first, second = (fa, fb) if below == 0 else (fb, fa)
+                return jnp.where(odd, first[rows_at, :], second[rows_at, :]) * scale
+
+            yield below * gap + r, n, get
+
+
+def pack_far(meta_ref, fa, fb, _, __, out_a, out_b):
+    meta = Meta(meta_ref)
+    mask = side_mask(meta)
+    gap = V_HALO - V_NEAR
+    for q in range(out_a.shape[0] // (2 * gap)):
+        for at, n, get in far_rows(meta, fa, fb, q):
+            a, b = send_columns(mask, get(0), get(1))
+            out_a[pl.ds(2 * gap * q + at, n), :] = a
+            out_b[pl.ds(2 * gap * q + at, n), :] = b
+
+
+def spread_valid(meta, mask, v_ref, va, vb, near_a, near_b, guides, halo, put):
+    maps, _, rows, _ = v_ref.shape
+    for q in range(maps):
+        for r, n, get in pair_rows(meta, v_ref, va, vb, q, V_NEAR, 0, 0, V_NEAR, rows):
+            at = pl.ds((rows + 2 * V_NEAR) * q + r + V_NEAR, n)
+            fields = with_columns(meta, mask, get(0), get(1), near_a[at, :], near_b[at, :])
+            for k, planes in enumerate(fields[: guides - 2 * q]):
+                for t in range(2):
+                    put(2 * q + k, t, r + halo, n, planes[t])
+
+
+def spread_all(meta_ref, v_ref, va, vb, near_a, near_b, fa, fb, far_a, far_b, out_ref):
+    meta = Meta(meta_ref)
+    mask = side_mask(meta)
+    guides = out_ref.shape[0]
+
+    def put(g, t, at, n, value):
+        out_ref[g, t, pl.ds(at, n), :] = value
+
+    spread_valid(meta, mask, v_ref, va, vb, near_a, near_b, guides, V_HALO, put)
+    maps, _, rows, _ = v_ref.shape
+    gap = V_HALO - V_NEAR
+    for q in range(maps):
+        for at, n, get in far_rows(meta, fa, fb, q):
+            rows_at = pl.ds(2 * gap * q + at, n)
+            where = at if at < gap else at - gap + V_HALO + rows + V_NEAR
+            fields = with_columns(meta, mask, get(0), get(1), far_a[rows_at, :], far_b[rows_at, :])
+            for k, planes in enumerate(fields[: guides - 2 * q]):
+                for t in range(2):
+                    put(2 * q + k, t, where, n, planes[t])
 
 
 def load_fields(meta, mask, slots, q, rows_iter, a_ref, b_ref, base, shift, x_ref, x_base):
@@ -434,67 +523,99 @@
                 store_field(x_ref, 2 * q + k, r + x_base, n, *planes)
 
 
-def stage_first(slots, meta_ref, shifts_ref, frac_ref, own_ref, r_ref, v_ref, reg_ref, xa, xb, va, vb, ga, gb, *refs):
-    z_ref, out_a, out_b, res_ref, dot_ref = refs[:5]
-    x_ref, valid_ref, m_ref, acc_ref, z_planes, *rest = refs[5:]
-    work, masks = rest[:9], rest[9:12]
+def stage_inputs(slots, meta_ref, table_ref, ga, gb, *refs):
+    xrs, xa, xb = refs[:slots], refs[slots : 2 * slots], refs[2 * slots : 3 * slots]
+    foot_ref, part_ref, reg_ref, x_ref, g_all, mask_ref = refs[3 * slots :]
     meta = Meta(meta_ref)
     mask = side_mask(meta)
-    pairs, _, rows, _ = own_ref.shape
-    x_base, m_base, acc_base = X_HALO + 8, V_NEAR + 8, DEPTH1 + 8
-    prepare_vcycle(meta, DEPTH1, rows, masks, work)
+    rows = (xrs[0].shape[0] - 8) // 2
+    pairs = (slots + 1) // 2
+    x_base = X_HALO + 8
     total = rows + 2 * X_HALO
     total_r = rows + 2 * R_HALO
-    stride = X_HALO + R_HALO
+    for k in range(slots):
+        reg_ref[pl.ds(8 * k, 8), :] = xrs[k][pl.ds(2 * rows, 8), :]
+        for plane in range(4):
+            zero_rows(x_ref, (k, plane), ((0, 8), (total + 8, total + 16)))
     for q in range(pairs):
         load_fields(
-            meta, mask, slots, q, pair_rows(meta, own_ref, xa, xb, q, stride, 0, 0, X_HALO, rows),
+            meta, mask, slots, q, input_rows(meta, slots, xrs, xa, xb, q, 0, 0, X_HALO, rows),
             ga, gb, q * total, X_HALO, x_ref, x_base,
         )
+    for position in range(mask_ref.shape[0]):
+        for r, n in spans(0, rows + 2 * DEPTH1 + 16, 32):
+            mask_ref[position, pl.ds(r, n), :] = mask_rows(meta, position, r - DEPTH1 - 8, n, rows)
+    guide_loop(
+        meta, table_ref, foot_ref.shape[0], slots, (x_ref, x_base),
+        p_rows=(-V_NEAR, rows + V_NEAR), footprints=(foot_ref, V_NEAR),
+    )
     for k in range(slots):
-        for plane in range(4):
-            zero_rows(x_ref, (k, plane), ((0, 8), (total + 8, total + 16)))
-        clear_planes(acc_ref, (k,))
-    for plane in range(2):
-        zero_rows(m_ref, (plane,), ((0, 8), (rows + 2 * V_NEAR + 8, rows + 2 * V_NEAR + 16)))
-    spread_valid(
-        meta_ref, v_ref, va, vb, ga, gb, None, None, valid_ref, V_NEAR, pairs * (total + total_r)
-    )
-    guide_loop(
-        meta, shifts_ref, frac_ref, (x_ref, x_base), (valid_ref, V_NEAR), (m_ref, m_base), (acc_ref, acc_base),
-        (-V_NEAR, rows + V_NEAR), (-DEPTH1, rows + DEPTH1), slots, slots,
-    )
-    g_ref = work[0]
-    dot_ref[...] = jnp.zeros((8, LANES), F32)
+        bilaplace_into(
+            x_ref.at[k], x_base, g_all.at[k], -DEPTH1, rows + DEPTH1,
+            lambda r, n: mask_ref[k & 1, pl.ds(r + DEPTH1 + 8, n), :],
+        )
     for q in range(pairs):
         base = pairs * total + q * total_r + R_HALO
-        for r, n, get in pair_rows(meta, r_ref, xa, xb, q, stride, X_HALO, 0, R_HALO, rows):
+        for r, n, get in input_rows(meta, slots, xrs, xa, xb, q, rows, X_HALO, R_HALO, rows):
             fields = with_columns(
                 meta, mask, get(0), get(1), ga[pl.ds(base + r, n), :], gb[pl.ds(base + r, n), :]
             )
             at = r + DEPTH1 + 8
-            for k, planes in enumerate(fields):
-                if 2 * q + k < slots:
-                    for t in range(2):
-                        acc_ref[2 * q + k, t, pl.ds(at, n), :] = planes[t] - (
-                            acc_ref[2 * q + k, t, pl.ds(at, n), :] + 0.1 * x_ref[2 * q + k, t, pl.ds(r + x_base, n), :]
-                        )
+            for k, planes in enumerate(fields[: slots - 2 * q]):
+                slot = 2 * q + k
+                weight = reg_ref[pl.ds(8 * slot, 1), :]
+                bi = five_point(g_all.at[slot], at, n)[:2]
+                for t in range(2):
+                    part_ref[slot, t, pl.ds(r + DEPTH1, n), :] = (
+                        planes[t] - weight * bi[t] - 0.1 * x_ref[slot, t, pl.ds(r + x_base, n), :]
+                    )
+
+
+def stage_first(slots, meta_ref, table_ref, v_ref, va, vb, na, nb, foot_ref, part_ref, reg_ref, _, *refs):
+    z_ref, out_a, out_b, res_ref, dot_ref = refs[:5]
+    m_ref, acc_ref, z_planes, *rest = refs[5:]
+    work, masks = rest[:-3], rest[-3:]
+    meta = Meta(meta_ref)
+    mask = side_mask(meta)
+    maps, _, rows, _ = v_ref.shape
+    guides = foot_ref.shape[0]
+    pairs = (slots + 1) // 2
+    m_base, acc_base = V_NEAR + 8, DEPTH1 + 8
+    prepare_vcycle(meta, DEPTH1, rows, masks, work)
     for k in range(slots):
+        clear_planes(acc_ref, (k,))
+    for g in range(guides):
+        for plane in range(2):
+            zero_rows(m_ref, (g, plane), ((0, 8), (rows + 2 * V_NEAR + 8, rows + 2 * V_NEAR + 16)))
+
+    def put(g, t, at, n, value):
+        m_ref[g, t, pl.ds(at + 8, n), :] = value * foot_ref[g, t, pl.ds(at, n), :]
+
+    spread_valid(meta, mask, v_ref, va, vb, na, nb, guides, V_NEAR, put)
+    guide_loop(
+        meta, table_ref, guides, slots, m=(m_ref, m_base), acc=(acc_ref, acc_base),
+        outs=(-DEPTH1, rows + DEPTH1), out_slots=slots,
+    )
+
+    def finish_slot(k):
         weight = reg_ref[pl.ds(8 * k, 1), :]
         own_masks = [m.at[k & 1] for m in masks]
-        bilaplace_into(
-            x_ref.at[k], x_base, g_ref, -DEPTH1, rows + DEPTH1,
-            lambda r, n: own_masks[0][pl.ds(r + DEPTH1 + 8, n), :],
-        )
+        own_work = work[9 * (k & 1) :][:9]
         h_ref = acc_ref.at[k]
         for at, n in spans(8, rows + 2 * DEPTH1 + 8, 16):
-            bi = five_point(g_ref, at, n)[:2]
             inside = own_masks[0][pl.ds(at, n), :]
             for t in range(2):
-                h_ref[t, pl.ds(at, n), :] = inside * (h_ref[t, pl.ds(at, n), :] - weight * bi[t])
+                h_ref[t, pl.ds(at, n), :] = inside * (
+                    part_ref[k, t, pl.ds(at - 8, n), :] - h_ref[t, pl.ds(at, n), :]
+                )
         for t in range(2):
-            zero_rows(g_ref, (t,), ((0, 8), (rows + 2 * DEPTH1 + 8, rows + 2 * DEPTH1 + 16)))
-        vcycle(h_ref, z_planes.at[k], weight, DEPTH1, rows, own_masks, work)
+            zero_rows(own_work[0], (t,), ((0, 8), (rows + 2 * DEPTH1 + 8, rows + 2 * DEPTH1 + 16)))
+        yield
+        yield from vcycle(h_ref, z_planes.at[k], weight, DEPTH1, rows, own_masks, own_work)
+
+    for q in range(pairs):
+        in_step(finish_slot(k) for k in range(2 * q, min(2 * q + 2, slots)))
+    dots = []
     for q in range(pairs):
         one, two = 2 * q, min(2 * q + 1, slots - 1)
         for r, n in spans(0, rows, 16):
@@ -505,28 +626,29 @@
                 z_ref[q, t, pl.ds(r, n), :] = z
                 if q == 0:
                     res_ref[t, pl.ds(r, n), :] = res
-                dot_ref[...] += fold(own_lanes(slots, q) * (z * res))
+                dots.append(fold(own_lanes(slots, q) * (z * res)))
         for t in range(2):
             send_rows(
                 meta, lambda r, n: z_ref[q, t, pl.ds(r, n), :], Z_HALO, rows, out_a, out_b, (2 * q + t) * Z_HALO
             )
+    dot_ref[...] = total_of(dots)
 
 
 def own_lanes(slots, q):
     return 1.0 if 2 * q + 1 < slots else (lane_iota() < HALF).astype(F32)
 
 
-def pack_second(meta_ref, z_ref, za, zb, a_ref, b_ref):
+def pack_second(meta_ref, z_ref, za, zb, _, __, a_ref, b_ref):
     meta = Meta(meta_ref)
     pairs, _, rows, _ = z_ref.shape
     groups = [(Z_HALO, pair_rows(meta, z_ref, za, zb, q, Z_HALO, 0, 0, Z_HALO, rows)) for q in range(pairs)]
     pack_columns(meta, side_mask(meta), groups, a_ref, b_ref)
 
 
-def stage_second(slots, meta_ref, shifts_ref, frac_ref, z_ref, reg_ref, valid_ref, za, zb, ga, gb, *refs):
+def stage_second(slots, meta_ref, table_ref, z_ref, reg_ref, valid_ref, za, zb, ga, gb, *refs):
     y_ref, out_a, out_b, image_ref, dot_zq, dot_yq = refs[:6]
     x_ref, m_ref, acc_ref, y_planes, *rest = refs[6:]
-    work, masks = rest[:9], rest[9:12]
+    work, masks = rest[:-3], rest[-3:]
     meta = Meta(meta_ref)
     mask = side_mask(meta)
     pairs, _, rows, _ = z_ref.shape
@@ -545,17 +667,21 @@
     for plane in range(2):
         zero_rows(m_ref, (plane,), ((0, 8), (rows + 2 * V_HALO + 8, rows + 2 * V_HALO + 16)))
     guide_loop(
-        meta, shifts_ref, frac_ref, (x_ref, x_base), (valid_ref, V_HALO), (m_ref, m_base), (acc_ref, acc_base),
-        (-V_HALO, rows + V_HALO), (-DEPTH2, rows + DEPTH2), slots, slots,
-    )
-    g_ref = work[0]
-    for k in range(slots):
+        meta, table_ref, valid_ref.shape[0], slots,
+        (x_ref, x_base), (valid_ref, V_HALO), (m_ref, m_base), (acc_ref, acc_base),
+        (-V_HALO, rows + V_HALO), (-DEPTH2, rows + DEPTH2), slots,
+    )
+
+    def finish_slot(k):
         weight = reg_ref[pl.ds(8 * k, 1), :]
         own_masks = [m.at[k & 1] for m in masks]
+        own_work = work[9 * (k & 1) :][:9]
+        g_ref = own_work[0]
         bilaplace_into(
             x_ref.at[k], x_base, g_ref, -DEPTH2, rows + DEPTH2,
             lambda r, n: own_masks[0][pl.ds(r + DEPTH2 + 8, n), :],
         )
+        yield
         h_ref = acc_ref.at[k]
         for r, n in spans(-DEPTH2, rows + DEPTH2, 16):
             at = r + DEPTH2 + 8
@@ -567,9 +693,12 @@
                 )
         for t in range(2):
             zero_rows(g_ref, (t,), ((0, 8), (rows + 2 * DEPTH2 + 8, rows + 2 * DEPTH2 + 16)))
-        vcycle(h_ref, y_planes.at[k], weight, DEPTH2, rows, own_masks, work)
-    dot_zq[...] = jnp.zeros((8, LANES), F32)
-    dot_yq[...] = jnp.zeros((8, LANES), F32)
+        yield
+        yield from vcycle(h_ref, y_planes.at[k], weight, DEPTH2, rows, own_masks, own_work)
+
+    for q in range(pairs):
+        in_step(finish_slot(k) for k in range(2 * q, min(2 * q + 2, slots)))
+    zq, yq = [], []
     total_y = rows + 2 * Y_HALO
     for q in range(pairs):
         one, two = 2 * q, min(2 * q + 1, slots - 1)
@@ -584,13 +713,14 @@
                     image = merge(acc_ref[one, t, rows_at, :], acc_ref[two, t, rows_at, :])
                     z = z_ref[q, t, pl.ds(r, n), :]
                     own = own_lanes(slots, q)
-                    dot_zq[...] += fold(own * (z * image))
-                    dot_yq[...] += fold(own * (y[t] * image))
+                    zq.append(own * (z * image))
+                    yq.append(own * (y[t] * image))
                     if q == 0:
                         image_ref[t, pl.ds(r, n), :] = image
-
-
-def stage_third(slots, meta_ref, shifts_ref, frac_ref, y_ref, reg_ref, valid_ref, dot_rz, dot_zq, dot_yq, ga, gb, *refs):
+    dot_zq[...], dot_yq[...] = total_of(zq), total_of(yq)
+
+
+def stage_third(slots, meta_ref, table_ref, y_ref, reg_ref, valid_ref, dot_rz, dot_zq, dot_yq, ga, gb, *refs):
     image_ref, sums_ref, x_ref, m_ref, acc_ref, g_ref, square_ref, mask_ref = refs
     meta = Meta(meta_ref)
     mask = side_mask(meta)
@@ -612,9 +742,11 @@
         for r, n in spans(-8, rows + 8, 48):
             mask_ref[position, pl.ds(r + 8, n), :] = mask_rows(meta, position, r, n, rows)
     guide_loop(
-        meta, shifts_ref, frac_ref, (x_ref, x_base), (valid_ref, V_HALO), (m_ref, m_base), (acc_ref, 0),
-        (-24, rows + 24), (0, rows), slots, 1, square_ref, rows,
-    )
+        meta, table_ref, valid_ref.shape[0], slots,
+        (x_ref, x_base), (valid_ref, V_HALO), (m_ref, m_base), (acc_ref, 0),
+        (-24, rows + 24), (0, rows), 1, square_ref=square_ref, rows=rows,
+    )
+    squares = []
     for k in reversed(range(slots)):
         weight = reg_ref[pl.ds(8 * k, 1), :]
         bilaplace_into(
@@ -629,9 +761,10 @@
                 image_ref[1, pl.ds(r, n), :] = acc_ref[0, 1, pl.ds(r, n), :] + weight * bi_odd + 0.1 * x[1]
             else:
                 g_even, g_odd = g_ref[0, pl.ds(r + 8, n), :], g_ref[1, pl.ds(r + 8, n), :]
-            square_ref[...] += own * fold(
-                weight * (g_even * g_even + g_odd * g_odd) + 0.1 * (x[0] * x[0] + x[1] * x[1])
+            squares.append(
+                own * fold(weight * (g_even * g_even + g_odd * g_odd) + 0.1 * (x[0] * x[0] + x[1] * x[1]))
             )
+    square_ref[...] += total_of(squares)
     row = lax.broadcasted_iota(jnp.int32, (8, LANES), 0)
     packed = jnp.zeros((8, LANES), F32)
     for at, part in enumerate((dot_rz[...], dot_zq[...], dot_yq[...], square_ref[...])):
@@ -664,32 +797,16 @@
     residual_ref[0] = exact_dot(jnp.concatenate(rest, axis=1), matrix)
 
 
-def call(kernel, outs, *args, scratch=(), scalars=0, fetched=0):
+def call(kernel, outs, *args, scratch=(), scalars=0, unread=0):
     n_in, n_out = len(args), len(outs)
-    spaces = [pltpu.SMEM] * scalars + [pltpu.VMEM] * (n_in - scalars - fetched) + [pl.ANY] * fetched
-    landing = [pltpu.VMEM(a.shape, a.dtype) for a in args[n_in - fetched :]] if fetched else []
-
-    def run(*refs):
-        ins, outputs, rest = refs[:n_in], refs[n_in : n_in + n_out], refs[n_in + n_out :]
-        if fetched:
-            held, sems, rest = rest[:fetched], rest[fetched], rest[fetched + 1 :]
-            copies = [
-                pltpu.make_async_copy(src, dst, sems.at[k])
-                for k, (src, dst) in enumerate(zip(ins[n_in - fetched :], held))
-            ]
-            for copy in copies:
-                copy.start()
-            for copy in copies:
-                copy.wait()
-            ins = ins[: n_in - fetched] + held
-        kernel(*ins, *outputs, *rest)
-
+    spaces = [pltpu.SMEM] * scalars + [pltpu.VMEM] * (n_in - scalars - unread) + [pl.ANY] * unread
     return pl.pallas_call(
-        run,
+        kernel,
         out_shape=[jax.ShapeDtypeStruct(shape, F32) for shape in outs],
         in_specs=[pl.BlockSpec(memory_space=space) for space in spaces],
         out_specs=[pl.BlockSpec(memory_space=pltpu.VMEM)] * n_out,
-        scratch_shapes=[*landing, *([pltpu.SemaphoreType.DMA((fetched,))] if fetched else []), *scratch],
+        scratch_shapes=list(scratch),
+        compiler_params=pltpu.CompilerParams(vmem_limit_bytes=VMEM_LIMIT),
     )(*args)
 
 
@@ -716,62 +833,72 @@
         (gx > 0, gx < n_gx - 1, gy > 0, gy < n_gy - 1, lax.axis_index("layer"), gx & 1, gy & 1)
     ):
         meta = jnp.where(at == k, value.astype(jnp.int32), meta)
-    shifts, frac = shifts.reshape(-1), frac.reshape(-1)
+    table = jnp.concatenate([shifts.reshape(-1), frac.reshape(-1)])
     pairs, maps = (slots + 1) // 2, (guides + 1) // 2
     vmem = lambda *shape: pltpu.VMEM((*shape, LANES), F32)
 
-    xr = pl.pallas_call(
-        order_inputs,
-        out_shape=jax.ShapeDtypeStruct((2 * rows + 8, LANES), F32),
-        in_specs=[pl.BlockSpec(memory_space=pltpu.VMEM)] * 2 + [pl.BlockSpec(memory_space=pltpu.SMEM)],
-        out_specs=pl.BlockSpec(memory_space=pltpu.VMEM),
-    )(start, rhs, reg)
-    strip = (maps * 2 * V_HALO, LANES)
-    v_own, va, vb = call(order_valid, ((maps, 2, rows, LANES), strip, strip), meta, valid, scalars=1)
-    va, vb = swap(va, vb, "gx", False)
-    others = [lax.ppermute(xr, "layer", [(i, (i + k) % slots) for i in range(slots)]) for k in range(1, slots)]
+    strip = (X_HALO + R_HALO, LANES)
+    xr, xa, xb = call(order_inputs, ((2 * rows + 8, LANES), strip, strip), meta, reg, start, rhs, scalars=2)
+    round_layers = lambda x: [x] + [
+        lax.ppermute(x, "layer", [(i, (i + k) % slots) for i in range(slots)]) for k in range(1, slots)
+    ]
+    xa, xb = swap(xa, xb, "gx", True)
+    xrs = round_layers(xr)
+    near, far = (maps * 2 * V_NEAR, LANES), (maps * 2 * (V_HALO - V_NEAR), LANES)
+    v_own, va, vb = call(
+        order_valid, ((maps, 2, rows, LANES), near, near), meta, valid, xa, xb, scalars=1, unread=2
+    )
+    va, vb = swap(va, vb, "gx", True)
+    xas, xbs = round_layers(xa), round_layers(xb)
+    strip = (2 * pairs * (rows + X_HALO + R_HALO), LANES)
+    v_strip = (maps * (rows + 2 * V_NEAR), LANES)
+    ga, gb = call(
+        functools.partial(pack_inputs, slots), (strip, strip),
+        meta, *xrs, *xas, *xbs, table, v_own,
+        scalars=1, unread=2,
+    )
+    ga, gb = swap(ga, gb, "gy", True)
+    na, nb, fa, fb = call(
+        pack_valid, (v_strip, v_strip, far, far), meta, v_own, va, vb, ga, gb, scalars=1, unread=2
+    )
+    na, nb = swap(na, nb, "gy", V_CLOSED)
+    fa, fb = swap(fa, fb, "gx", True)
+
     tile = (pairs, 2, rows, LANES)
-    strip = (pairs * 2 * (X_HALO + R_HALO), LANES)
-    x_own, r_own, weights, xa, xb = call(
-        functools.partial(pair_inputs, slots, rows),
-        (tile, tile, (8 * slots, LANES), strip, strip),
-        meta, xr, *others,
-        scalars=1, fetched=len(others),
-    )
-    xa, xb = swap(xa, xb, "gx", False)
-    near = (pairs * (2 * rows + 2 * X_HALO + 2 * R_HALO) + maps * (rows + 2 * V_NEAR), LANES)
-    far = (maps * 2 * (V_HALO - V_NEAR), LANES)
-    ga, gb, fa, fb = call(
-        pack_first, (near, near, far, far), meta, x_own, r_own, v_own, xa, xb, va, vb, scalars=1, fetched=4
-    )
-    ga, gb = swap(ga, gb, "gy", False)
-    fa, fb = swap(fa, fb, "gy", False)
-
     size = rows + 2 * DEPTH1 + 16
+    positions = min(slots, 2)
+    footprints, part, weights = call(
+        functools.partial(stage_inputs, slots),
+        ((guides, 2, rows + 2 * V_NEAR, LANES), (slots, 2, rows + 2 * DEPTH1, LANES), (8 * slots, LANES)),
+        meta, table, ga, gb, *xrs, *xas, *xbs,
+        scalars=2,
+        scratch=[vmem(slots, 4, rows + 2 * X_HALO + 16), vmem(slots, 2, size), vmem(positions, size)],
+    )
+    ha, hb = call(pack_far, (far, far), meta, fa, fb, na, weights, scalars=1, unread=2)
+    packed_far = ha
+    ha, hb = swap(ha, hb, "gy", True)
     strip = (pairs * 2 * Z_HALO, LANES)
     z, za, zb, res, dot_rz = call(
         functools.partial(stage_first, slots),
         (tile, strip, strip, (2, rows, LANES), (8, LANES)),
-        meta, shifts, frac, x_own, r_own, v_own, weights, xa, xb, va, vb, ga, gb,
-        scalars=3, fetched=6,
+        meta, table, v_own, va, vb, na, nb, footprints, part, weights, packed_far,
+        scalars=2, unread=1,
         scratch=[
-            vmem(slots, 4, rows + 2 * X_HALO + 16),
-            vmem(guides, 2, rows + 2 * V_NEAR),
-            vmem(2, rows + 2 * V_NEAR + 16),
+            vmem(guides, 2, rows + 2 * V_NEAR + 16),
             vmem(slots, 2, size),
             vmem(slots, 2, size),
             *vcycle_scratch(DEPTH1, rows, slots),
         ],
     )
-    za, zb = swap(za, zb, "gx", False)
+    za, zb = swap(za, zb, "gx", True)
     (spread,) = call(
-        functools.partial(spread_valid, near_base=pairs * (2 * rows + 2 * X_HALO + 2 * R_HALO)),
+        spread_all,
         ((guides, 2, rows + 2 * V_HALO, LANES),),
-        meta, v_own, va, vb, ga, gb, fa, fb,
-        scalars=1, fetched=6,
+        meta, v_own, va, vb, na, nb, fa, fb, ha, hb,
+        scalars=1,
     )
     strip = (pairs * (rows + 2 * Z_HALO), LANES)
-    ka, kb = call(pack_second, (strip, strip), meta, z, za, zb, scalars=1, fetched=2)
+    ka, kb = call(pack_second, (strip, strip), meta, z, za, zb, ha, hb, scalars=1, unread=2)
     ka, kb = swap(ka, kb, "gy", True)
 
     size = rows + 2 * DEPTH2 + 16
@@ -779,8 +906,8 @@
     y, ya, yb, image, dot_zq, dot_yq = call(
         functools.partial(stage_second, slots),
         ((pairs, 2, rows + 2 * Y_HALO, LANES), strip, strip, (2, rows, LANES), (8, LANES), (8, LANES)),
-        meta, shifts, frac, z, weights, spread, za, zb, ka, kb,
-        scalars=3, fetched=4,
+        meta, table, z, weights, spread, za, zb, ka, kb,
+        scalars=2,
         scratch=[
             vmem(slots, 4, rows + 2 * Z_HALO + 8),
             vmem(2, rows + 2 * V_HALO + 16),
@@ -794,8 +921,8 @@
     image_y, sums = call(
         functools.partial(stage_third, slots),
         ((2, rows, LANES), (n_gx * n_gy, 8, LANES)),
-        meta, shifts, frac, y, weights, spread, dot_rz, dot_zq, dot_yq, ya, yb,
-        scalars=3, fetched=2,
+        meta, table, y, weights, spread, dot_rz, dot_zq, dot_yq, ya, yb,
+        scalars=2,
         scratch=[
             vmem(slots, 4, rows + 2 * Y_HALO + 8),
             vmem(2, rows + 48),

time: 118 us -> 90.3 us (0.77)
  Pallas kernels: 47.9 us -> 25.8 us
  waiting for transfers between devices: 10.6 us -> 25.8 us
  starting transfers between devices: 35.5 us -> 22.4 us
  local copies, waits for them, and re-layouts: 8.03 us -> 4.44 us
  blocking collectives: 12.6 us -> 10 us
    pallas_call x10 -> x12, Pallas kernels: 47.9 us -> 25.8 us  [call(): pl.pallas_call(kernel, out_shape=[jax.ShapeDtypeStruct(shape, F32) for sh...]
    ppermute x14 -> x18, waiting for transfers between devices: 6.91 us -> 25.2 us  [swap(): return (lax.ppermute(a, axis, first), lax.ppermute(b, axis, second))]
    ppermute x14 -> x18, starting transfers between devices: 34 us -> 18.8 us  [swap(): return (lax.ppermute(a, axis, first), lax.ppermute(b, axis, second))]
    ppermute x1 -> x3, waiting for transfers between devices: 3.74 us -> 0.57 us  [shards(): lax.ppermute(x, 'layer', [(i, (i + k) % slots) for i in range(slots)])]
    all_to_all x1, blocking collectives: 12.6 us -> 10 us  [shards(): sums = lax.all_to_all(sums, ('gx', 'gy'), 0, 0)]
    unnamed x40 -> x10, local copies, waits for them, and re-layouts: 6.67 us -> 4.26 us
    ppermute x1 -> x3, starting transfers between devices: 1.52 us -> 3.61 us  [shards(): lax.ppermute(x, 'layer', [(i, (i + k) % slots) for i in range(slots)])]
  transfers between devices with their start and end apart: 15 -> 21, of which waited for: 5 -> 11; matrix products, arithmetic and copies ran while one was open for 1% -> 2% of each run, Pallas kernels for 8% -> 11%
where the time goes in v3:
time: 90.3 us; the launch traced here: 90 us
  Pallas kernels  25.8 us (29%)
  waiting for transfers between devices  25.8 us (29%)
  starting transfers between devices  22.4 us (25%)
  blocking collectives  10 us (11%)
  local copies, waits for them, and re-layouts  4.44 us (5%)
  between operations  1.45 us (2%)
    pallas_call x12, Pallas kernels, call(): pl.pallas_call(kernel, out_shape=[jax.ShapeDtypeStruct(shape, F32) for sh...  25.8 us
    ppermute x18, waiting for transfers between devices, swap(): return (lax.ppermute(a, axis, first), lax.ppermute(b, axis, second))  25.2 us
    ppermute x18, starting transfers between devices, swap(): return (lax.ppermute(a, axis, first), lax.ppermute(b, axis, second))  18.8 us
    all_to_all x1, blocking collectives, shards(): sums = lax.all_to_all(sums, ('gx', 'gy'), 0, 0)  10 us
    unnamed x10, local copies, waits for them, and re-layouts  4.26 us
    ppermute x3, starting transfers between devices, shards(): lax.ppermute(x, 'layer', [(i, (i + k) % slots) for i in range(slots)])  3.61 us
  transfers between devices with their start and end apart: 21, of which 11 were waited for; matrix products, arithmetic and copies ran while one was open for 2% of the time, Pallas kernels for 11%

profile of v3, /device:TPU:0, one launch (start us, length us, event | category | flops | bytes accessed | tf_op | source)
XLA Modules:
  0.0 90.0 jit_solution(816668698544877372)
XLA Ops:
  1.3 0.8 copy-done.1
  2.2 0.8 copy-done.3
  3.7 3.1 %collective-permute-start = (f32[80,128]{1,0:T(8,128)S(1)}, f32[80,128]{1,0:T(8,128)S(1)}, u32[]{:S(2)}, u32[]{:S(2)}) collective-permute-start(f32[80,128]{1,0:T(8,128)S(1)} %get-tuple-element.34), channel_id=1, source_target_pairs={{0,4},{4,0},{8,12},{12,8},{1,5},{5,1},{9,13},{13,9},{2,6},{6,2},{1... | collective-permute-start | bytes 122888 | tf_op jit(solution)/shard_map/ppermute | solution.py:821
  6.8 2.5 %collective-permute-start.1 = (f32[80,128]{1,0:T(8,128)S(1)}, f32[80,128]{1,0:T(8,128)S(1)}, u32[]{:S(2)}, u32[]{:S(2)}) collective-permute-start(f32[80,128]{1,0:T(8,128)S(1)} %get-tuple-element.35), channel_id=1, source_target_pairs={{0,12},{4,8},{8,4},{12,0},{1,13},{5,9},{9,5},{13,1},{2,14},{6,10},... | collective-permute-start | bytes 122888 | tf_op jit(solution)/shard_map/ppermute | solution.py:821
  9.3 1.5 %collective-permute-start.4 = (f32[264,128]{1,0:T(8,128)S(1)}, f32[264,128]{1,0:T(8,128)S(1)}, u32[]{:S(2)}, u32[]{:S(2)}) collective-permute-start(f32[264,128]{1,0:T(8,128)S(1)} %get-tuple-element.39.refs_0_), channel_id=1, source_target_pairs={{0,16},{16,0},{1,17},{17,1},{2,18},{18,2},{3,19},{19,3},{4,20},{20... | collective-permute-start | bytes 405512 | tf_op jit(solution)/shard_map/ppermute | solution.py:843
  10.8 0.8 copy.10
  11.7 0.8 copy.11
  13.1 1.5 %collective-permute-start.6 = (f32[80,128]{1,0:T(8,128)S(1)}, f32[80,128]{1,0:T(8,128)S(1)}, u32[]{:S(2)}, u32[]{:S(2)}) collective-permute-start(f32[80,128]{1,0:T(8,128)S(1)} %collective-permute-done.1.__.refs_4_), channel_id=1, source_target_pairs={{0,16},{16,0},{1,17},{17,1},{2,18},{18,2},{3,19},{19,3},{4,20},{20... | collective-permute-start | bytes 122888 | tf_op jit(solution)/shard_map/ppermute | solution.py:843
  14.7 1.0 %copy-done = s32[8,128,128]{2,1,0:T(8,128)S(1)} copy-done((s32[8,128,128]{2,1,0:T(8,128)S(1)}, s32[8,128,128]{2,1,0:T(8,128)}, u32[]{:S(2)}) %copy-start) | copy-done | bytes 524312
  15.8 0.8 shard_map.78
  17.1 1.5 %shard_map.79 = (f32[416,128]{1,0:T(8,128)S(1)}, f32[416,128]{1,0:T(8,128)S(1)}) custom-call(s32[8]{0:T(128)S(1)} %compare_select_fusion.6.meta_ref, f32[264,128]{1,0:T(8,128)S(1)} %get-tuple-element.39.refs_0_, f32[264,128]{1,0:T(8,128)S(1)} %collective-permute-done.4.refs_1_, f32[80,128]{1,0:T(8,128)S(1)} %collective-permute-done._.refs_2_, ...), custom_call_target="tpu_custom_call" | custom-call | tf_op jit(solution)/shard_map/pallas_call | solution.py:803
  18.7 1.6 %collective-permute-start.8 = (f32[416,128]{1,0:T(8,128)S(1)}, f32[416,128]{1,0:T(8,128)S(1)}, u32[]{:S(2)}, u32[]{:S(2)}) collective-permute-start(f32[416,128]{1,0:T(8,128)S(1)} %get-tuple-element.41), channel_id=1, source_target_pairs={{0,3},{1,2},{2,1},{3,0},{4,7},{5,6},{6,5},{7,4},{8,11},{9,10},{10,... | collective-permute-start | bytes 638984 | tf_op jit(solution)/shard_map/ppermute | solution.py:821
  21.0 1.4 %collective-permute-start.3 = (f32[320,128]{1,0:T(8,128)S(1)}, f32[320,128]{1,0:T(8,128)S(1)}, u32[]{:S(2)}, u32[]{:S(2)}) collective-permute-start(f32[320,128]{1,0:T(8,128)S(1)} %get-tuple-element.38), channel_id=1, source_target_pairs={{0,12},{4,8},{8,4},{12,0},{1,13},{5,9},{9,5},{13,1},{2,14},{6,10},... | collective-permute-start | bytes 491528 | tf_op jit(solution)/shard_map/ppermute | solution.py:821
  22.4 4.5 %collective-permute-done.2.va = f32[320,128]{1,0:T(8,128)S(1)} collective-permute-done((f32[320,128]{1,0:T(8,128)S(1)}, f32[320,128]{1,0:T(8,128)S(1)}, u32[]{:S(2)}, u32[]{:S(2)}) %collective-permute-start.2) | collective-permute-done | bytes 163872 | tf_op jit(solution)/shard_map/ppermute | solution.py:821
  26.9 3.4 %collective-permute-done.3.vb = f32[320,128]{1,0:T(8,128)S(1)} collective-permute-done((f32[320,128]{1,0:T(8,128)S(1)}, f32[320,128]{1,0:T(8,128)S(1)}, u32[]{:S(2)}, u32[]{:S(2)}) %collective-permute-start.3) | collective-permute-done | bytes 163872 | tf_op jit(solution)/shard_map/ppermute | solution.py:821
  31.8 1.4 %collective-permute-start.11 = (f32[256,128]{1,0:T(8,128)S(1)}, f32[256,128]{1,0:T(8,128)S(1)}, u32[]{:S(2)}, u32[]{:S(2)}) collective-permute-start(f32[256,128]{1,0:T(8,128)S(1)} %get-tuple-element.47), channel_id=1, source_target_pairs={{0,4},{4,0},{8,12},{12,8},{1,5},{5,1},{9,13},{13,9},{2,6},{6,2},{1... | collective-permute-start | bytes 393224 | tf_op jit(solution)/shard_map/ppermute | solution.py:821
  33.2 2.0 %collective-permute-start.12 = (f32[256,128]{1,0:T(8,128)S(1)}, f32[256,128]{1,0:T(8,128)S(1)}, u32[]{:S(2)}, u32[]{:S(2)}) collective-permute-start(f32[256,128]{1,0:T(8,128)S(1)} %get-tuple-element.48), channel_id=1, source_target_pairs={{0,12},{4,8},{8,4},{12,0},{1,13},{5,9},{9,5},{13,1},{2,14},{6,10},... | collective-permute-start | bytes 393224 | tf_op jit(solution)/shard_map/ppermute | solution.py:821
  35.2 3.5 %shard_map.81 = (f32[8,2,208,128]{3,2,1,0:T(8,128)S(1)}, f32[2,2,176,128]{3,2,1,0:T(8,128)S(1)}, f32[16,128]{1,0:T(8,128)S(1)}) custom-call(s32[8]{0:T(128)S(1)} %compare_select_fusion.6.meta_ref, s32[64]{0:T(128)S(1)} %pad_add_fusion.refs_6_.table_ref, f32[416,128]{1,0:T(8,128)S(1)} %collective-permute-done.7._.ga, ...), custom_call_target="tpu_custom_call" | custom-call | tf_op jit(solution)/shard_map/pallas_call | solution.py:803
  38.7 2.7 %collective-permute-done.12.fb = f32[256,128]{1,0:T(8,128)S(1)} collective-permute-done((f32[256,128]{1,0:T(8,128)S(1)}, f32[256,128]{1,0:T(8,128)S(1)}, u32[]{:S(2)}, u32[]{:S(2)}) %collective-permute-start.12) | collective-permute-done | bytes 131104 | tf_op jit(solution)/shard_map/ppermute | solution.py:821
  42.4 1.3 %collective-permute-start.13 = (f32[256,128]{1,0:T(8,128)S(1)}, f32[256,128]{1,0:T(8,128)S(1)}, u32[]{:S(2)}, u32[]{:S(2)}) collective-permute-start(f32[256,128]{1,0:T(8,128)S(1)} %get-tuple-element.49._), channel_id=1, source_target_pairs={{0,1},{1,0},{2,3},{3,2},{4,5},{5,4},{6,7},{7,6},{8,9},{9,8},{10,11... | collective-permute-start | bytes 393224 | tf_op jit(solution)/shard_map/ppermute | solution.py:821
  43.7 4.0 %shard_map.83 = (f32[1,2,128,128]{3,2,1,0:T(8,128)S(1)}, f32[176,128]{1,0:T(8,128)S(1)}, f32[176,128]{1,0:T(8,128)S(1)}, f32[2,128,128]{2,1,0:T(8,128)S(1)}, f32[8,128]{1,0:T(8,128)S(1)}) custom-call(s32[8]{0:T(128)S(1)} %compare_select_fusion.6.meta_ref, s32[64]{0:T(128)S(1)} %pad_add_fusion.refs_6_.table_ref, ...), custom_call_target="tpu_custom_call" | custom-call | tf_op jit(solution)/shard_map/pallas_call | solution.py:803
  48.2 2.2 %collective-permute-start.16 = (f32[176,128]{1,0:T(8,128)S(1)}, f32[176,128]{1,0:T(8,128)S(1)}, u32[]{:S(2)}, u32[]{:S(2)}) collective-permute-start(f32[176,128]{1,0:T(8,128)S(1)} %get-tuple-element.54), channel_id=1, source_target_pairs={{0,12},{4,8},{8,4},{12,0},{1,13},{5,9},{9,5},{13,1},{2,14},{6,10},... | collective-permute-start | bytes 270344 | tf_op jit(solution)/shard_map/ppermute | solution.py:821
  50.5 1.9 %collective-permute-done.15.za = f32[176,128]{1,0:T(8,128)S(1)} collective-permute-done((f32[176,128]{1,0:T(8,128)S(1)}, f32[176,128]{1,0:T(8,128)S(1)}, u32[]{:S(2)}, u32[]{:S(2)}) %collective-permute-start.15) | collective-permute-done | bytes 90144 | tf_op jit(solution)/shard_map/ppermute | solution.py:821
  52.3 3.3 %collective-permute-done.16.zb = f32[176,128]{1,0:T(8,128)S(1)} collective-permute-done((f32[176,128]{1,0:T(8,128)S(1)}, f32[176,128]{1,0:T(8,128)S(1)}, u32[]{:S(2)}, u32[]{:S(2)}) %collective-permute-start.16) | collective-permute-done | bytes 90144 | tf_op jit(solution)/shard_map/ppermute | solution.py:821
  56.7 0.9 %shard_map.84.valid_ref = f32[8,2,272,128]{3,2,1,0:T(8,128)S(1)} custom-call(s32[8]{0:T(128)S(1)} %compare_select_fusion.6.meta_ref, f32[4,2,128,128]{3,2,1,0:T(8,128)S(1)} %get-tuple-element.36.refs_7_.v_ref, f32[320,128]{1,0:T(8,128)S(1)} %collective-permute-done.2.va, f32[320,128]{1,0:T(8,128)S(1)} %collective-permute-done.3.vb, ...), custom_call_target="tpu_custom_call" | custom-call | tf_op jit(solution)/shard_map/pallas_call | solution.py:803
  57.7 4.4 %collective-permute-done.18.gb = f32[304,128]{1,0:T(8,128)S(1)} collective-permute-done((f32[304,128]{1,0:T(8,128)S(1)}, f32[304,128]{1,0:T(8,128)S(1)}, u32[]{:S(2)}, u32[]{:S(2)}) %collective-permute-start.18) | collective-permute-done | bytes 155680 | tf_op jit(solution)/shard_map/ppermute | solution.py:821
  62.2 7.6 %shard_map.86 = (f32[1,2,208,128]{3,2,1,0:T(8,128)S(1)}, f32[208,128]{1,0:T(8,128)S(1)}, f32[208,128]{1,0:T(8,128)S(1)}, f32[2,128,128]{2,1,0:T(8,128)S(1)}, f32[8,128]{1,0:T(8,128)S(1)}, /*index=5*/f32[8,128]{1,0:T(8,128)S(1)}) custom-call(s32[8]{0:T(128)S(1)} %compare_select_fusion.6.meta_ref, s32[64]{0:T(128)S(1)} %pad_add_fusion.refs_6_.table_ref, ...), custom_call_target="tpu_custom_call" | custom-call | tf_op jit(solution)/shard_map/pallas_call | solution.py:803
  70.3 0.9 collective-permute-done.19.ga
  71.2 4.0 %collective-permute-done.20.gb = f32[208,128]{1,0:T(8,128)S(1)} collective-permute-done((f32[208,128]{1,0:T(8,128)S(1)}, f32[208,128]{1,0:T(8,128)S(1)}, u32[]{:S(2)}, u32[]{:S(2)}) %collective-permute-start.20) | collective-permute-done | bytes 106528 | tf_op jit(solution)/shard_map/ppermute | solution.py:821
  75.2 3.7 %shard_map.87 = (f32[2,128,128]{2,1,0:T(8,128)S(1)}, f32[16,8,128]{2,1,0:T(8,128)S(1)}) custom-call(s32[8]{0:T(128)S(1)} %compare_select_fusion.6.meta_ref, s32[64]{0:T(128)S(1)} %pad_add_fusion.refs_6_.table_ref, f32[1,2,208,128]{3,2,1,0:T(8,128)S(1)} %get-tuple-element.58.y_ref, f32[16,128]{1,0:T(8,128)S(1)} %get-tuple-element.46.__.reg_ref, ...), custom_call_target="tpu_custom_call" | custom-call | tf_op jit(solution)/shard_map/pallas_call | solution.py:803
  78.9 10.0 %all_to_all.5.sums_ref = f32[16,8,128]{2,1,0:T(8,128)S(1)} all-to-all(f32[16,8,128]{2,1,0:T(8,128)S(1)} %get-tuple-element.65), channel_id=1, replica_groups=mesh['layer'=2,'gx'=4,'gy'=4] {'gx','gy'}, dimensions={0} | all-to-all | bytes 131072 | tf_op jit(solution)/shard_map/all_to_all | solution.py:935
  88.9 1.0 %shard_map.88 = (f32[1,128,128]{2,1,0:T(8,128)}, f32[1,128,128]{2,1,0:T(8,128)}) custom-call(f32[1,128,128]{2,1,0:T(8,128)S(1)} %copy-done.2, f32[1,2,128,128]{3,2,1,0:T(8,128)S(1)} %get-tuple-element.50.z_ref, f32[2,128,128]{2,1,0:T(8,128)S(1)} %get-tuple-element.51.res_ref, f32[2,128,128]{2,1,0:T(8,128)S(1)} %get-tuple-element.57.q_ref, ...), custom_call_target="tpu_custom_call" | custom-call | tf_op jit(solution)/shard_map/pallas_call | solution.py:803
  (37 shorter events, 7.6 us)
Async XLA Ops:
  1.3 0.8 copy-start.1
  2.1 0.8 copy-start.3
  3.7 8.8 %collective-permute-start = (f32[80,128]{1,0:T(8,128)S(1)}, f32[80,128]{1,0:T(8,128)S(1)}, u32[]{:S(2)}, u32[]{:S(2)}) collective-permute-start(f32[80,128]{1,0:T(8,128)S(1)} %get-tuple-element.34), channel_id=1, source_target_pairs={{0,4},{4,0},{8,12},{12,8},{1,5},{5,1},{9,13},{13,9},{2,6},{6,2},{1... | collective-permute-start | bytes 122888 | tf_op jit(solution)/shard_map/ppermute | solution.py:821
  6.8 6.3 %collective-permute-start.1 = (f32[80,128]{1,0:T(8,128)S(1)}, f32[80,128]{1,0:T(8,128)S(1)}, u32[]{:S(2)}, u32[]{:S(2)}) collective-permute-start(f32[80,128]{1,0:T(8,128)S(1)} %get-tuple-element.35), channel_id=1, source_target_pairs={{0,12},{4,8},{8,4},{12,0},{1,13},{5,9},{9,5},{13,1},{2,14},{6,10},... | collective-permute-start | bytes 122888 | tf_op jit(solution)/shard_map/ppermute | solution.py:821
  9.3 7.8 %collective-permute-start.4 = (f32[264,128]{1,0:T(8,128)S(1)}, f32[264,128]{1,0:T(8,128)S(1)}, u32[]{:S(2)}, u32[]{:S(2)}) collective-permute-start(f32[264,128]{1,0:T(8,128)S(1)} %get-tuple-element.39.refs_0_), channel_id=1, source_target_pairs={{0,16},{16,0},{1,17},{17,1},{2,18},{18,2},{3,19},{19,3},{4,20},{20... | collective-permute-start | bytes 405512 | tf_op jit(solution)/shard_map/ppermute | solution.py:843
  12.6 4.1 %collective-permute-start.5 = (f32[80,128]{1,0:T(8,128)S(1)}, f32[80,128]{1,0:T(8,128)S(1)}, u32[]{:S(2)}, u32[]{:S(2)}) collective-permute-start(f32[80,128]{1,0:T(8,128)S(1)} %collective-permute-done._.refs_2_), channel_id=1, source_target_pairs={{0,16},{16,0},{1,17},{17,1},{2,18},{18,2},{3,19},{19,3},{4,20},{20... | collective-permute-start | bytes 122888 | tf_op jit(solution)/shard_map/ppermute | solution.py:843
  13.1 4.0 %collective-permute-start.6 = (f32[80,128]{1,0:T(8,128)S(1)}, f32[80,128]{1,0:T(8,128)S(1)}, u32[]{:S(2)}, u32[]{:S(2)}) collective-permute-start(f32[80,128]{1,0:T(8,128)S(1)} %collective-permute-done.1.__.refs_4_), channel_id=1, source_target_pairs={{0,16},{16,0},{1,17},{17,1},{2,18},{18,2},{3,19},{19,3},{4,20},{20... | collective-permute-start | bytes 122888 | tf_op jit(solution)/shard_map/ppermute | solution.py:843
  14.7 1.0 %copy-start = (s32[8,128,128]{2,1,0:T(8,128)S(1)}, s32[8,128,128]{2,1,0:T(8,128)}, u32[]{:S(2)}) copy-start(s32[8,128,128]{2,1,0:T(8,128)} %valid_ref.1) | copy-start | bytes 1572868
  18.6 11.7 %collective-permute-start.7 = (f32[416,128]{1,0:T(8,128)S(1)}, f32[416,128]{1,0:T(8,128)S(1)}, u32[]{:S(2)}, u32[]{:S(2)}) collective-permute-start(f32[416,128]{1,0:T(8,128)S(1)} %get-tuple-element.40), channel_id=1, source_target_pairs={{0,1},{1,0},{2,3},{3,2},{4,5},{5,4},{6,7},{7,6},{8,9},{9,8},{10,11... | collective-permute-start | bytes 638984 | tf_op jit(solution)/shard_map/ppermute | solution.py:821
  18.7 11.6 %collective-permute-start.8 = (f32[416,128]{1,0:T(8,128)S(1)}, f32[416,128]{1,0:T(8,128)S(1)}, u32[]{:S(2)}, u32[]{:S(2)}) collective-permute-start(f32[416,128]{1,0:T(8,128)S(1)} %get-tuple-element.41), channel_id=1, source_target_pairs={{0,3},{1,2},{2,1},{3,0},{4,7},{5,6},{6,5},{7,4},{8,11},{9,10},{10,... | collective-permute-start | bytes 638984 | tf_op jit(solution)/shard_map/ppermute | solution.py:821
  20.3 6.6 %collective-permute-start.2 = (f32[320,128]{1,0:T(8,128)S(1)}, f32[320,128]{1,0:T(8,128)S(1)}, u32[]{:S(2)}, u32[]{:S(2)}) collective-permute-start(f32[320,128]{1,0:T(8,128)S(1)} %get-tuple-element.37), channel_id=1, source_target_pairs={{0,4},{4,0},{8,12},{12,8},{1,5},{5,1},{9,13},{13,9},{2,6},{6,2},{1... | collective-permute-start | bytes 491528 | tf_op jit(solution)/shard_map/ppermute | solution.py:821
  21.0 9.3 %collective-permute-start.3 = (f32[320,128]{1,0:T(8,128)S(1)}, f32[320,128]{1,0:T(8,128)S(1)}, u32[]{:S(2)}, u32[]{:S(2)}) collective-permute-start(f32[320,128]{1,0:T(8,128)S(1)} %get-tuple-element.38), channel_id=1, source_target_pairs={{0,12},{4,8},{8,4},{12,0},{1,13},{5,9},{9,5},{13,1},{2,14},{6,10},... | collective-permute-start | bytes 491528 | tf_op jit(solution)/shard_map/ppermute | solution.py:821
  31.0 10.4 %collective-permute-start.9 = (f32[832,128]{1,0:T(8,128)S(1)}, f32[832,128]{1,0:T(8,128)S(1)}, u32[]{:S(2)}, u32[]{:S(2)}) collective-permute-start(f32[832,128]{1,0:T(8,128)S(1)} %get-tuple-element.42), channel_id=1, source_target_pairs={{0,1},{1,0},{2,3},{3,2},{4,5},{5,4},{6,7},{7,6},{8,9},{9,8},{10,11... | collective-permute-start | bytes 1277960 | tf_op jit(solution)/shard_map/ppermute | solution.py:821
  31.1 12.6 %collective-permute-start.10 = (f32[832,128]{1,0:T(8,128)S(1)}, f32[832,128]{1,0:T(8,128)S(1)}, u32[]{:S(2)}, u32[]{:S(2)}) collective-permute-start(f32[832,128]{1,0:T(8,128)S(1)} %get-tuple-element.43), channel_id=1, source_target_pairs={{0,3},{1,2},{2,1},{3,0},{4,7},{5,6},{6,5},{7,4},{8,11},{9,10},{10,... | collective-permute-start | bytes 1277960 | tf_op jit(solution)/shard_map/ppermute | solution.py:821
  31.8 6.9 %collective-permute-start.11 = (f32[256,128]{1,0:T(8,128)S(1)}, f32[256,128]{1,0:T(8,128)S(1)}, u32[]{:S(2)}, u32[]{:S(2)}) collective-permute-start(f32[256,128]{1,0:T(8,128)S(1)} %get-tuple-element.47), channel_id=1, source_target_pairs={{0,4},{4,0},{8,12},{12,8},{1,5},{5,1},{9,13},{13,9},{2,6},{6,2},{1... | collective-permute-start | bytes 393224 | tf_op jit(solution)/shard_map/ppermute | solution.py:821
  33.2 8.2 %collective-permute-start.12 = (f32[256,128]{1,0:T(8,128)S(1)}, f32[256,128]{1,0:T(8,128)S(1)}, u32[]{:S(2)}, u32[]{:S(2)}) collective-permute-start(f32[256,128]{1,0:T(8,128)S(1)} %get-tuple-element.48), channel_id=1, source_target_pairs={{0,12},{4,8},{8,4},{12,0},{1,13},{5,9},{9,5},{13,1},{2,14},{6,10},... | collective-permute-start | bytes 393224 | tf_op jit(solution)/shard_map/ppermute | solution.py:821
  42.1 13.6 %collective-permute-start.14 = (f32[256,128]{1,0:T(8,128)S(1)}, f32[256,128]{1,0:T(8,128)S(1)}, u32[]{:S(2)}, u32[]{:S(2)}) collective-permute-start(f32[256,128]{1,0:T(8,128)S(1)} %get-tuple-element.52), channel_id=1, source_target_pairs={{0,3},{1,2},{2,1},{3,0},{4,7},{5,6},{6,5},{7,4},{8,11},{9,10},{10,... | collective-permute-start | bytes 393224 | tf_op jit(solution)/shard_map/ppermute | solution.py:821
  42.4 13.2 %collective-permute-start.13 = (f32[256,128]{1,0:T(8,128)S(1)}, f32[256,128]{1,0:T(8,128)S(1)}, u32[]{:S(2)}, u32[]{:S(2)}) collective-permute-start(f32[256,128]{1,0:T(8,128)S(1)} %get-tuple-element.49._), channel_id=1, source_target_pairs={{0,1},{1,0},{2,3},{3,2},{4,5},{5,4},{6,7},{7,6},{8,9},{9,8},{10,11... | collective-permute-start | bytes 393224 | tf_op jit(solution)/shard_map/ppermute | solution.py:821
  47.8 4.6 %collective-permute-start.15 = (f32[176,128]{1,0:T(8,128)S(1)}, f32[176,128]{1,0:T(8,128)S(1)}, u32[]{:S(2)}, u32[]{:S(2)}) collective-permute-start(f32[176,128]{1,0:T(8,128)S(1)} %get-tuple-element.53), channel_id=1, source_target_pairs={{0,4},{4,0},{8,12},{12,8},{1,5},{5,1},{9,13},{13,9},{2,6},{6,2},{1... | collective-permute-start | bytes 270344 | tf_op jit(solution)/shard_map/ppermute | solution.py:821
  48.2 7.4 %collective-permute-start.16 = (f32[176,128]{1,0:T(8,128)S(1)}, f32[176,128]{1,0:T(8,128)S(1)}, u32[]{:S(2)}, u32[]{:S(2)}) collective-permute-start(f32[176,128]{1,0:T(8,128)S(1)} %get-tuple-element.54), channel_id=1, source_target_pairs={{0,12},{4,8},{8,4},{12,0},{1,13},{5,9},{9,5},{13,1},{2,14},{6,10},... | collective-permute-start | bytes 270344 | tf_op jit(solution)/shard_map/ppermute | solution.py:821
  56.3 1.4 %collective-permute-start.17 = (f32[304,128]{1,0:T(8,128)S(1)}, f32[304,128]{1,0:T(8,128)S(1)}, u32[]{:S(2)}, u32[]{:S(2)}) collective-permute-start(f32[304,128]{1,0:T(8,128)S(1)} %get-tuple-element.55), channel_id=1, source_target_pairs={{0,1},{1,0},{2,3},{3,2},{4,5},{5,4},{6,7},{7,6},{8,9},{9,8},{10,11... | collective-permute-start | bytes 466952 | tf_op jit(solution)/shard_map/ppermute | solution.py:821
  56.4 5.8 %collective-permute-start.18 = (f32[304,128]{1,0:T(8,128)S(1)}, f32[304,128]{1,0:T(8,128)S(1)}, u32[]{:S(2)}, u32[]{:S(2)}) collective-permute-start(f32[304,128]{1,0:T(8,128)S(1)} %get-tuple-element.56), channel_id=1, source_target_pairs={{0,3},{1,2},{2,1},{3,0},{4,7},{5,6},{6,5},{7,4},{8,11},{9,10},{10,... | collective-permute-start | bytes 466952 | tf_op jit(solution)/shard_map/ppermute | solution.py:821
  57.7 31.3 %copy-start.2 = (f32[1,128,128]{2,1,0:T(8,128)S(1)}, f32[1,128,128]{2,1,0:T(8,128)}, u32[]{:S(2)}) copy-start(f32[1,128,128]{2,1,0:T(8,128)} %start_ref.3) | copy-start | bytes 196612
  69.8 1.4 %collective-permute-start.19 = (f32[208,128]{1,0:T(8,128)S(1)}, f32[208,128]{1,0:T(8,128)S(1)}, u32[]{:S(2)}, u32[]{:S(2)}) collective-permute-start(f32[208,128]{1,0:T(8,128)S(1)} %get-tuple-element.62), channel_id=1, source_target_pairs={{0,1},{1,0},{2,3},{3,2},{4,5},{5,4},{6,7},{7,6},{8,9},{9,8},{10,11... | collective-permute-start | bytes 319496 | tf_op jit(solution)/shard_map/ppermute | solution.py:821
  70.2 5.0 %collective-permute-start.20 = (f32[208,128]{1,0:T(8,128)S(1)}, f32[208,128]{1,0:T(8,128)S(1)}, u32[]{:S(2)}, u32[]{:S(2)}) collective-permute-start(f32[208,128]{1,0:T(8,128)S(1)} %get-tuple-element.63), channel_id=1, source_target_pairs={{0,3},{1,2},{2,1},{3,0},{4,7},{5,6},{6,5},{7,4},{8,11},{9,10},{10,... | collective-permute-start | bytes 319496 | tf_op jit(solution)/shard_map/ppermute | solution.py:821

commit v4 on v3

--- a/solution.py
+++ b/solution.py
@@ -2,6 +2,7 @@
 
 import jax
 import jax.numpy as jnp
+import numpy as np
 from jax import lax
 from jax.experimental import pallas as pl
 from jax.experimental.pallas import tpu as pltpu
@@ -19,7 +20,6 @@
 X_HALO, R_HALO, V_HALO, V_NEAR, Z_HALO, Y_HALO = 56, 24, 72, 40, 88, 40
 DEPTH1, DEPTH2 = 24, 56
 VMEM_LIMIT = 16 << 20
-V_CLOSED = True
 
 
 def lane_iota(shape=(1, LANES)):
@@ -571,7 +571,7 @@
                     )
 
 
-def stage_first(slots, meta_ref, table_ref, v_ref, va, vb, na, nb, foot_ref, part_ref, reg_ref, _, *refs):
+def stage_first(slots, meta_ref, table_ref, v_ref, va, vb, na, nb, foot_ref, part_ref, reg_ref, *refs):
     z_ref, out_a, out_b, res_ref, dot_ref = refs[:5]
     m_ref, acc_ref, z_planes, *rest = refs[5:]
     work, masks = rest[:-3], rest[-3:]
@@ -810,15 +810,28 @@
     )(*args)
 
 
-def swap(a, b, axis, closed):
-    n = lax.axis_size(axis)
-    first = [(i, i ^ 1 if i ^ 1 < n else i) for i in range(n)]
-    last = lambda i: i - 1 if i % 2 == 0 else i + 1
-    if closed and n % 2 == 0:
-        second = [(i, last(i) % n) for i in range(n)]
-    else:
-        second = [(i, last(i) if 0 <= last(i) < n else i) for i in range(n)]
-    return lax.ppermute(a, axis, first), lax.ppermute(b, axis, second)
+def swap(a, b, axis):
+    axes = ("layer", "gx", "gy")
+    sizes = [lax.axis_size(name) for name in axes]
+    moved = axes.index(axis)
+    n = sizes[moved]
+
+    def pairs(partner):
+        found = []
+        for source in np.ndindex(*sizes):
+            target = list(source)
+            other = partner(source[moved])
+            if 0 <= other < n:
+                target[moved] = other
+            elif source[0] ^ 1 < sizes[0]:
+                target[0] ^= 1
+            found.append(tuple(int(np.ravel_multi_index(place, sizes)) for place in (source, tuple(target))))
+        return found
+
+    return (
+        lax.ppermute(a, axes, pairs(lambda i: i ^ 1)),
+        lax.ppermute(b, axes, pairs(lambda i: i - 1 if i % 2 == 0 else i + 1)),
+    )
 
 
 def shards(rhs, start, valid, reg, shifts, frac):
@@ -842,13 +855,13 @@
     round_layers = lambda x: [x] + [
         lax.ppermute(x, "layer", [(i, (i + k) % slots) for i in range(slots)]) for k in range(1, slots)
     ]
-    xa, xb = swap(xa, xb, "gx", True)
+    xa, xb = swap(xa, xb, "gx")
     xrs = round_layers(xr)
     near, far = (maps * 2 * V_NEAR, LANES), (maps * 2 * (V_HALO - V_NEAR), LANES)
     v_own, va, vb = call(
         order_valid, ((maps, 2, rows, LANES), near, near), meta, valid, xa, xb, scalars=1, unread=2
     )
-    va, vb = swap(va, vb, "gx", True)
+    va, vb = swap(va, vb, "gx")
     xas, xbs = round_layers(xa), round_layers(xb)
     strip = (2 * pairs * (rows + X_HALO + R_HALO), LANES)
     v_strip = (maps * (rows + 2 * V_NEAR), LANES)
@@ -857,12 +870,12 @@
         meta, *xrs, *xas, *xbs, table, v_own,
         scalars=1, unread=2,
     )
-    ga, gb = swap(ga, gb, "gy", True)
+    ga, gb = swap(ga, gb, "gy")
     na, nb, fa, fb = call(
         pack_valid, (v_strip, v_strip, far, far), meta, v_own, va, vb, ga, gb, scalars=1, unread=2
     )
-    na, nb = swap(na, nb, "gy", V_CLOSED)
-    fa, fb = swap(fa, fb, "gx", True)
+    na, nb = swap(na, nb, "gy")
+    fa, fb = swap(fa, fb, "gx")
 
     tile = (pairs, 2, rows, LANES)
     size = rows + 2 * DEPTH1 + 16
@@ -874,15 +887,12 @@
         scalars=2,
         scratch=[vmem(slots, 4, rows + 2 * X_HALO + 16), vmem(slots, 2, size), vmem(positions, size)],
     )
-    ha, hb = call(pack_far, (far, far), meta, fa, fb, na, weights, scalars=1, unread=2)
-    packed_far = ha
-    ha, hb = swap(ha, hb, "gy", True)
     strip = (pairs * 2 * Z_HALO, LANES)
     z, za, zb, res, dot_rz = call(
         functools.partial(stage_first, slots),
         (tile, strip, strip, (2, rows, LANES), (8, LANES)),
-        meta, table, v_own, va, vb, na, nb, footprints, part, weights, packed_far,
-        scalars=2, unread=1,
+        meta, table, v_own, va, vb, na, nb, footprints, part, weights,
+        scalars=2,
         scratch=[
             vmem(guides, 2, rows + 2 * V_NEAR + 16),
             vmem(slots, 2, size),
@@ -890,7 +900,9 @@
             *vcycle_scratch(DEPTH1, rows, slots),
         ],
     )
-    za, zb = swap(za, zb, "gx", True)
+    ha, hb = call(pack_far, (far, far), meta, fa, fb, z, weights, scalars=1, unread=2)
+    za, zb = swap(za, zb, "gx")
+    ha, hb = swap(ha, hb, "gy")
     (spread,) = call(
         spread_all,
         ((guides, 2, rows + 2 * V_HALO, LANES),),
@@ -899,7 +911,7 @@
     )
     strip = (pairs * (rows + 2 * Z_HALO), LANES)
     ka, kb = call(pack_second, (strip, strip), meta, z, za, zb, ha, hb, scalars=1, unread=2)
-    ka, kb = swap(ka, kb, "gy", True)
+    ka, kb = swap(ka, kb, "gy")
 
     size = rows + 2 * DEPTH2 + 16
     strip = (pairs * (rows + 2 * Y_HALO), LANES)
@@ -916,7 +928,7 @@
             *vcycle_scratch(DEPTH2, rows, slots),
         ],
     )
-    ya, yb = swap(ya, yb, "gy", True)
+    ya, yb = swap(ya, yb, "gy")
 
     image_y, sums = call(
         functools.partial(stage_third, slots),

time: 90.3 us -> 82.8 us (0.917)
  starting transfers between devices: 22.4 us -> 17.6 us
  waiting for transfers between devices: 25.8 us -> 22.8 us
    ppermute x18, waiting for transfers between devices: 25.2 us -> 21.3 us  [the longest x9 13.4 us: swap(): lax.ppermute(b, axes, pairs(lambda i: i - 1 if i % 2 == 0 else i + 1))]
    ppermute x18, starting transfers between devices: 18.8 us -> 14.9 us  [the longest x9 8.56 us: swap(): lax.ppermute(b, axes, pairs(lambda i: i - 1 if i % 2 == 0 else i + 1))]
  transfers between devices with their start and end apart: 21 -> 21, of which waited for: 11 -> 10; matrix products, arithmetic and copies ran while one was open for 2% -> 2% of each run, Pallas kernels for 11% -> 11%
where the time goes in v4:
time: 82.8 us; the launch traced here: 82.4 us
  Pallas kernels  25.7 us (31%)
  waiting for transfers between devices  22.8 us (28%)
  starting transfers between devices  17.6 us (21%)
  blocking collectives  10.2 us (12%)
  local copies, waits for them, and re-layouts  4.44 us (5%)
  between operations  1.49 us (2%)
    pallas_call x12, Pallas kernels, call(): pl.pallas_call(kernel, out_shape=[jax.ShapeDtypeStruct(shape, F32) for sh...  25.7 us
    ppermute x9, waiting for transfers between devices, swap(): lax.ppermute(b, axes, pairs(lambda i: i - 1 if i % 2 == 0 else i + 1))  13.4 us
    all_to_all x1, blocking collectives, shards(): sums = lax.all_to_all(sums, ('gx', 'gy'), 0, 0)  10.2 us
    ppermute x9, starting transfers between devices, swap(): lax.ppermute(b, axes, pairs(lambda i: i - 1 if i % 2 == 0 else i + 1))  8.56 us
    ppermute x9, waiting for transfers between devices, swap(): lax.ppermute(a, axes, pairs(lambda i: i ^ 1))  7.92 us
    ppermute x9, starting transfers between devices, swap(): lax.ppermute(a, axes, pairs(lambda i: i ^ 1))  6.35 us
    unnamed x10, local copies, waits for them, and re-layouts  4.26 us
    ppermute x3, starting transfers between devices, shards(): lax.ppermute(x, 'layer', [(i, (i + k) % slots) for i in range(slots)])  2.73 us
  transfers between devices with their start and end apart: 21, of which 10 were waited for; matrix products, arithmetic and copies ran while one was open for 2% of the time, Pallas kernels for 11%

profile of v4, /device:TPU:0, one launch (start us, length us, event | category | flops | bytes accessed | tf_op | source)
XLA Modules:
  0.0 82.4 jit_solution(15466729659286037739)
XLA Ops:
  1.3 0.8 %copy-done.1 = f32[1,128,128]{2,1,0:T(8,128)S(1)} copy-done((f32[1,128,128]{2,1,0:T(8,128)S(1)}, f32[1,128,128]{2,1,0:T(8,128)}, u32[]{:S(2)}) %copy-start.1) | copy-done | bytes 65560
  2.2 0.8 %copy-done.3 = f32[1,128,128]{2,1,0:T(8,128)S(1)} copy-done((f32[1,128,128]{2,1,0:T(8,128)S(1)}, f32[1,128,128]{2,1,0:T(8,128)}, u32[]{:S(2)}) %copy-start.3) | copy-done | bytes 65560
  3.0 0.7 shard_map.77
  3.7 3.1 %collective-permute-start = (f32[80,128]{1,0:T(8,128)S(1)}, f32[80,128]{1,0:T(8,128)S(1)}, u32[]{:S(2)}, u32[]{:S(2)}) collective-permute-start(f32[80,128]{1,0:T(8,128)S(1)} %get-tuple-element.34), channel_id=1, source_target_pairs={{0,4},{1,5},{2,6},{3,7},{4,0},{5,1},{6,2},{7,3},{8,12},{9,13},{10,... | collective-permute-start | bytes 122888 | tf_op jit(solution)/shard_map/ppermute | solution.py:832
  6.8 1.5 %collective-permute-start.1 = (f32[80,128]{1,0:T(8,128)S(1)}, f32[80,128]{1,0:T(8,128)S(1)}, u32[]{:S(2)}, u32[]{:S(2)}) collective-permute-start(f32[80,128]{1,0:T(8,128)S(1)} %get-tuple-element.35), channel_id=1, source_target_pairs={{0,16},{1,17},{2,18},{3,19},{4,8},{5,9},{6,10},{7,11},{8,4},{9,5},... | collective-permute-start | bytes 122888 | tf_op jit(solution)/shard_map/ppermute | solution.py:833
  8.9 0.8 copy.10
  9.7 0.8 copy.11
  10.6 1.6 %collective-permute-start.5 = (f32[80,128]{1,0:T(8,128)S(1)}, f32[80,128]{1,0:T(8,128)S(1)}, u32[]{:S(2)}, u32[]{:S(2)}) collective-permute-start(f32[80,128]{1,0:T(8,128)S(1)} %collective-permute-done._.refs_2_), channel_id=1, source_target_pairs={{0,16},{16,0},{1,17},{17,1},{2,18},{18,2},{3,19},{19,3},{4,20},{20... | collective-permute-start | bytes 122888 | tf_op jit(solution)/shard_map/ppermute | solution.py:856
  12.9 1.0 %copy-done = s32[8,128,128]{2,1,0:T(8,128)S(1)} copy-done((s32[8,128,128]{2,1,0:T(8,128)S(1)}, s32[8,128,128]{2,1,0:T(8,128)}, u32[]{:S(2)}) %copy-start) | copy-done | bytes 524312
  13.9 0.8 shard_map.78
  14.9 1.3 %collective-permute-done.6.refs_5_ = f32[80,128]{1,0:T(8,128)S(1)} collective-permute-done((f32[80,128]{1,0:T(8,128)S(1)}, f32[80,128]{1,0:T(8,128)S(1)}, u32[]{:S(2)}, u32[]{:S(2)}) %collective-permute-start.6) | collective-permute-done | bytes 40992 | tf_op jit(solution)/shard_map/ppermute | solution.py:856
  16.2 1.5 %shard_map.79 = (f32[416,128]{1,0:T(8,128)S(1)}, f32[416,128]{1,0:T(8,128)S(1)}) custom-call(s32[8]{0:T(128)S(1)} %compare_select_fusion.6.meta_ref, f32[264,128]{1,0:T(8,128)S(1)} %get-tuple-element.39.refs_0_, f32[264,128]{1,0:T(8,128)S(1)} %collective-permute-done.4.refs_1_, f32[80,128]{1,0:T(8,128)S(1)} %collective-permute-done._.refs_2_, ...), custom_call_target="tpu_custom_call" | custom-call | tf_op jit(solution)/shard_map/pallas_call | solution.py:803
  18.4 2.5 %collective-permute-start.2 = (f32[320,128]{1,0:T(8,128)S(1)}, f32[320,128]{1,0:T(8,128)S(1)}, u32[]{:S(2)}, u32[]{:S(2)}) collective-permute-start(f32[320,128]{1,0:T(8,128)S(1)} %get-tuple-element.37), channel_id=1, source_target_pairs={{0,4},{1,5},{2,6},{3,7},{4,0},{5,1},{6,2},{7,3},{8,12},{9,13},{10,... | collective-permute-start | bytes 491528 | tf_op jit(solution)/shard_map/ppermute | solution.py:832
  21.5 4.1 %collective-permute-done.2.va = f32[320,128]{1,0:T(8,128)S(1)} collective-permute-done((f32[320,128]{1,0:T(8,128)S(1)}, f32[320,128]{1,0:T(8,128)S(1)}, u32[]{:S(2)}, u32[]{:S(2)}) %collective-permute-start.2) | collective-permute-done | bytes 163872 | tf_op jit(solution)/shard_map/ppermute | solution.py:832
  25.5 1.6 %collective-permute-done.3.vb = f32[320,128]{1,0:T(8,128)S(1)} collective-permute-done((f32[320,128]{1,0:T(8,128)S(1)}, f32[320,128]{1,0:T(8,128)S(1)}, u32[]{:S(2)}, u32[]{:S(2)}) %collective-permute-start.3) | collective-permute-done | bytes 163872 | tf_op jit(solution)/shard_map/ppermute | solution.py:833
  28.0 1.3 %collective-permute-start.10 = (f32[832,128]{1,0:T(8,128)S(1)}, f32[832,128]{1,0:T(8,128)S(1)}, u32[]{:S(2)}, u32[]{:S(2)}) collective-permute-start(f32[832,128]{1,0:T(8,128)S(1)} %get-tuple-element.43), channel_id=1, source_target_pairs={{0,16},{1,2},{2,1},{3,19},{4,20},{5,6},{6,5},{7,23},{8,24},{9,10},... | collective-permute-start | bytes 1277960 | tf_op jit(solution)/shard_map/ppermute | solution.py:833
  30.2 3.5 %shard_map.81 = (f32[8,2,208,128]{3,2,1,0:T(8,128)S(1)}, f32[2,2,176,128]{3,2,1,0:T(8,128)S(1)}, f32[16,128]{1,0:T(8,128)S(1)}) custom-call(s32[8]{0:T(128)S(1)} %compare_select_fusion.6.meta_ref, s32[64]{0:T(128)S(1)} %pad_add_fusion.refs_6_.table_ref, f32[416,128]{1,0:T(8,128)S(1)} %collective-permute-done.7._.ga, ...), custom_call_target="tpu_custom_call" | custom-call | tf_op jit(solution)/shard_map/pallas_call | solution.py:803
  33.7 3.9 %collective-permute-done.10.nb.near_b = f32[832,128]{1,0:T(8,128)S(1)} collective-permute-done((f32[832,128]{1,0:T(8,128)S(1)}, f32[832,128]{1,0:T(8,128)S(1)}, u32[]{:S(2)}, u32[]{:S(2)}) %collective-permute-start.10) | collective-permute-done | bytes 426016 | tf_op jit(solution)/shard_map/ppermute | solution.py:833
  37.6 4.0 %shard_map.82 = (f32[1,2,128,128]{3,2,1,0:T(8,128)S(1)}, f32[176,128]{1,0:T(8,128)S(1)}, f32[176,128]{1,0:T(8,128)S(1)}, f32[2,128,128]{2,1,0:T(8,128)S(1)}, f32[8,128]{1,0:T(8,128)S(1)}) custom-call(s32[8]{0:T(128)S(1)} %compare_select_fusion.6.meta_ref, s32[64]{0:T(128)S(1)} %pad_add_fusion.refs_6_.table_ref, ...), custom_call_target="tpu_custom_call" | custom-call | tf_op jit(solution)/shard_map/pallas_call | solution.py:803
  42.3 1.1 %collective-permute-start.14 = (f32[256,128]{1,0:T(8,128)S(1)}, f32[256,128]{1,0:T(8,128)S(1)}, u32[]{:S(2)}, u32[]{:S(2)}) collective-permute-start(f32[256,128]{1,0:T(8,128)S(1)} %get-tuple-element.52), channel_id=1, source_target_pairs={{0,16},{1,2},{2,1},{3,19},{4,20},{5,6},{6,5},{7,23},{8,24},{9,10},... | collective-permute-start | bytes 393224 | tf_op jit(solution)/shard_map/ppermute | solution.py:833
  43.4 1.0 %collective-permute-start.16 = (f32[176,128]{1,0:T(8,128)S(1)}, f32[176,128]{1,0:T(8,128)S(1)}, u32[]{:S(2)}, u32[]{:S(2)}) collective-permute-start(f32[176,128]{1,0:T(8,128)S(1)} %get-tuple-element.54), channel_id=1, source_target_pairs={{0,16},{1,17},{2,18},{3,19},{4,8},{5,9},{6,10},{7,11},{8,4},{9,5},... | collective-permute-start | bytes 270344 | tf_op jit(solution)/shard_map/ppermute | solution.py:833
  44.4 3.5 %collective-permute-done.15.za = f32[176,128]{1,0:T(8,128)S(1)} collective-permute-done((f32[176,128]{1,0:T(8,128)S(1)}, f32[176,128]{1,0:T(8,128)S(1)}, u32[]{:S(2)}, u32[]{:S(2)}) %collective-permute-start.15) | collective-permute-done | bytes 90144 | tf_op jit(solution)/shard_map/ppermute | solution.py:832
  48.0 1.0 %collective-permute-done.16.zb = f32[176,128]{1,0:T(8,128)S(1)} collective-permute-done((f32[176,128]{1,0:T(8,128)S(1)}, f32[176,128]{1,0:T(8,128)S(1)}, u32[]{:S(2)}, u32[]{:S(2)}) %collective-permute-start.16) | collective-permute-done | bytes 90144 | tf_op jit(solution)/shard_map/ppermute | solution.py:833
  49.7 0.9 %collective-permute-start.18 = (f32[304,128]{1,0:T(8,128)S(1)}, f32[304,128]{1,0:T(8,128)S(1)}, u32[]{:S(2)}, u32[]{:S(2)}) collective-permute-start(f32[304,128]{1,0:T(8,128)S(1)} %get-tuple-element.56), channel_id=1, source_target_pairs={{0,16},{1,2},{2,1},{3,19},{4,20},{5,6},{6,5},{7,23},{8,24},{9,10},... | collective-permute-start | bytes 466952 | tf_op jit(solution)/shard_map/ppermute | solution.py:833
  50.6 0.9 %shard_map.84.valid_ref = f32[8,2,272,128]{3,2,1,0:T(8,128)S(1)} custom-call(s32[8]{0:T(128)S(1)} %compare_select_fusion.6.meta_ref, f32[4,2,128,128]{3,2,1,0:T(8,128)S(1)} %get-tuple-element.36.refs_7_.v_ref, f32[320,128]{1,0:T(8,128)S(1)} %collective-permute-done.2.va, f32[320,128]{1,0:T(8,128)S(1)} %collective-permute-done.3.vb, ...), custom_call_target="tpu_custom_call" | custom-call | tf_op jit(solution)/shard_map/pallas_call | solution.py:803
  51.5 3.4 %collective-permute-done.18.gb = f32[304,128]{1,0:T(8,128)S(1)} collective-permute-done((f32[304,128]{1,0:T(8,128)S(1)}, f32[304,128]{1,0:T(8,128)S(1)}, u32[]{:S(2)}, u32[]{:S(2)}) %collective-permute-start.18) | collective-permute-done | bytes 155680 | tf_op jit(solution)/shard_map/ppermute | solution.py:833
  54.9 7.5 %shard_map.86 = (f32[1,2,208,128]{3,2,1,0:T(8,128)S(1)}, f32[208,128]{1,0:T(8,128)S(1)}, f32[208,128]{1,0:T(8,128)S(1)}, f32[2,128,128]{2,1,0:T(8,128)S(1)}, f32[8,128]{1,0:T(8,128)S(1)}, /*index=5*/f32[8,128]{1,0:T(8,128)S(1)}) custom-call(s32[8]{0:T(128)S(1)} %compare_select_fusion.6.meta_ref, s32[64]{0:T(128)S(1)} %pad_add_fusion.refs_6_.table_ref, ...), custom_call_target="tpu_custom_call" | custom-call | tf_op jit(solution)/shard_map/pallas_call | solution.py:803
  62.7 0.9 %collective-permute-start.20 = (f32[208,128]{1,0:T(8,128)S(1)}, f32[208,128]{1,0:T(8,128)S(1)}, u32[]{:S(2)}, u32[]{:S(2)}) collective-permute-start(f32[208,128]{1,0:T(8,128)S(1)} %get-tuple-element.63), channel_id=1, source_target_pairs={{0,16},{1,2},{2,1},{3,19},{4,20},{5,6},{6,5},{7,23},{8,24},{9,10},... | collective-permute-start | bytes 319496 | tf_op jit(solution)/shard_map/ppermute | solution.py:833
  63.9 3.5 %collective-permute-done.20.gb = f32[208,128]{1,0:T(8,128)S(1)} collective-permute-done((f32[208,128]{1,0:T(8,128)S(1)}, f32[208,128]{1,0:T(8,128)S(1)}, u32[]{:S(2)}, u32[]{:S(2)}) %collective-permute-start.20) | collective-permute-done | bytes 106528 | tf_op jit(solution)/shard_map/ppermute | solution.py:833
  67.4 3.7 %shard_map.87 = (f32[2,128,128]{2,1,0:T(8,128)S(1)}, f32[16,8,128]{2,1,0:T(8,128)S(1)}) custom-call(s32[8]{0:T(128)S(1)} %compare_select_fusion.6.meta_ref, s32[64]{0:T(128)S(1)} %pad_add_fusion.refs_6_.table_ref, f32[1,2,208,128]{3,2,1,0:T(8,128)S(1)} %get-tuple-element.58.y_ref, f32[16,128]{1,0:T(8,128)S(1)} %get-tuple-element.46.reg_ref.__, ...), custom_call_target="tpu_custom_call" | custom-call | tf_op jit(solution)/shard_map/pallas_call | solution.py:803
  71.1 10.2 %all_to_all.5.sums_ref = f32[16,8,128]{2,1,0:T(8,128)S(1)} all-to-all(f32[16,8,128]{2,1,0:T(8,128)S(1)} %get-tuple-element.65), channel_id=1, replica_groups=mesh['layer'=2,'gx'=4,'gy'=4] {'gx','gy'}, dimensions={0} | all-to-all | bytes 131072 | tf_op jit(solution)/shard_map/all_to_all | solution.py:947
  81.3 1.0 %shard_map.88 = (f32[1,128,128]{2,1,0:T(8,128)}, f32[1,128,128]{2,1,0:T(8,128)}) custom-call(f32[1,128,128]{2,1,0:T(8,128)S(1)} %copy-done.2, f32[1,2,128,128]{3,2,1,0:T(8,128)S(1)} %get-tuple-element.47._.z_ref, f32[2,128,128]{2,1,0:T(8,128)S(1)} %get-tuple-element.48.res_ref, f32[2,128,128]{2,1,0:T(8,128)S(1)} %get-tuple-element.57.q_ref, ...), custom_call_target="tpu_custom_call" | custom-call | tf_op jit(solution)/shard_map/pallas_call | solution.py:803
  (37 shorter events, 6.5 us)
Async XLA Ops:
  1.3 0.8 %copy-start.1 = (f32[1,128,128]{2,1,0:T(8,128)S(1)}, f32[1,128,128]{2,1,0:T(8,128)}, u32[]{:S(2)}) copy-start(f32[1,128,128]{2,1,0:T(8,128)} %start_ref.3) | copy-start | bytes 196612
  2.1 0.8 %copy-start.3 = (f32[1,128,128]{2,1,0:T(8,128)S(1)}, f32[1,128,128]{2,1,0:T(8,128)}, u32[]{:S(2)}) copy-start(f32[1,128,128]{2,1,0:T(8,128)} %rhs_ref.1) | copy-start | bytes 196612
  3.7 6.8 %collective-permute-start = (f32[80,128]{1,0:T(8,128)S(1)}, f32[80,128]{1,0:T(8,128)S(1)}, u32[]{:S(2)}, u32[]{:S(2)}) collective-permute-start(f32[80,128]{1,0:T(8,128)S(1)} %get-tuple-element.34), channel_id=1, source_target_pairs={{0,4},{1,5},{2,6},{3,7},{4,0},{5,1},{6,2},{7,3},{8,12},{9,13},{10,... | collective-permute-start | bytes 122888 | tf_op jit(solution)/shard_map/ppermute | solution.py:832
  6.8 5.4 %collective-permute-start.1 = (f32[80,128]{1,0:T(8,128)S(1)}, f32[80,128]{1,0:T(8,128)S(1)}, u32[]{:S(2)}, u32[]{:S(2)}) collective-permute-start(f32[80,128]{1,0:T(8,128)S(1)} %get-tuple-element.35), channel_id=1, source_target_pairs={{0,16},{1,17},{2,18},{3,19},{4,8},{5,9},{6,10},{7,11},{8,4},{9,5},... | collective-permute-start | bytes 122888 | tf_op jit(solution)/shard_map/ppermute | solution.py:833
  8.3 7.8 %collective-permute-start.4 = (f32[264,128]{1,0:T(8,128)S(1)}, f32[264,128]{1,0:T(8,128)S(1)}, u32[]{:S(2)}, u32[]{:S(2)}) collective-permute-start(f32[264,128]{1,0:T(8,128)S(1)} %get-tuple-element.39.refs_0_), channel_id=1, source_target_pairs={{0,16},{16,0},{1,17},{17,1},{2,18},{18,2},{3,19},{19,3},{4,20},{20... | collective-permute-start | bytes 405512 | tf_op jit(solution)/shard_map/ppermute | solution.py:856
  10.6 4.3 %collective-permute-start.5 = (f32[80,128]{1,0:T(8,128)S(1)}, f32[80,128]{1,0:T(8,128)S(1)}, u32[]{:S(2)}, u32[]{:S(2)}) collective-permute-start(f32[80,128]{1,0:T(8,128)S(1)} %collective-permute-done._.refs_2_), channel_id=1, source_target_pairs={{0,16},{16,0},{1,17},{17,1},{2,18},{18,2},{3,19},{19,3},{4,20},{20... | collective-permute-start | bytes 122888 | tf_op jit(solution)/shard_map/ppermute | solution.py:856
  12.2 4.0 %collective-permute-start.6 = (f32[80,128]{1,0:T(8,128)S(1)}, f32[80,128]{1,0:T(8,128)S(1)}, u32[]{:S(2)}, u32[]{:S(2)}) collective-permute-start(f32[80,128]{1,0:T(8,128)S(1)} %collective-permute-done.1.__.refs_4_), channel_id=1, source_target_pairs={{0,16},{16,0},{1,17},{17,1},{2,18},{18,2},{3,19},{19,3},{4,20},{20... | collective-permute-start | bytes 122888 | tf_op jit(solution)/shard_map/ppermute | solution.py:856
  12.9 1.0 %copy-start = (s32[8,128,128]{2,1,0:T(8,128)S(1)}, s32[8,128,128]{2,1,0:T(8,128)}, u32[]{:S(2)}) copy-start(s32[8,128,128]{2,1,0:T(8,128)} %valid_ref.1) | copy-start | bytes 1572868
  17.6 9.5 %collective-permute-start.7 = (f32[416,128]{1,0:T(8,128)S(1)}, f32[416,128]{1,0:T(8,128)S(1)}, u32[]{:S(2)}, u32[]{:S(2)}) collective-permute-start(f32[416,128]{1,0:T(8,128)S(1)} %get-tuple-element.40), channel_id=1, source_target_pairs={{0,1},{1,0},{2,3},{3,2},{4,5},{5,4},{6,7},{7,6},{8,9},{9,8},{10,11... | collective-permute-start | bytes 638984 | tf_op jit(solution)/shard_map/ppermute | solution.py:832
  17.7 9.4 %collective-permute-start.8 = (f32[416,128]{1,0:T(8,128)S(1)}, f32[416,128]{1,0:T(8,128)S(1)}, u32[]{:S(2)}, u32[]{:S(2)}) collective-permute-start(f32[416,128]{1,0:T(8,128)S(1)} %get-tuple-element.41), channel_id=1, source_target_pairs={{0,16},{1,2},{2,1},{3,19},{4,20},{5,6},{6,5},{7,23},{8,24},{9,10},... | collective-permute-start | bytes 638984 | tf_op jit(solution)/shard_map/ppermute | solution.py:833
  18.4 7.1 %collective-permute-start.2 = (f32[320,128]{1,0:T(8,128)S(1)}, f32[320,128]{1,0:T(8,128)S(1)}, u32[]{:S(2)}, u32[]{:S(2)}) collective-permute-start(f32[320,128]{1,0:T(8,128)S(1)} %get-tuple-element.37), channel_id=1, source_target_pairs={{0,4},{1,5},{2,6},{3,7},{4,0},{5,1},{6,2},{7,3},{8,12},{9,13},{10,... | collective-permute-start | bytes 491528 | tf_op jit(solution)/shard_map/ppermute | solution.py:832
  20.9 6.2 %collective-permute-start.3 = (f32[320,128]{1,0:T(8,128)S(1)}, f32[320,128]{1,0:T(8,128)S(1)}, u32[]{:S(2)}, u32[]{:S(2)}) collective-permute-start(f32[320,128]{1,0:T(8,128)S(1)} %get-tuple-element.38), channel_id=1, source_target_pairs={{0,16},{1,17},{2,18},{3,19},{4,8},{5,9},{6,10},{7,11},{8,4},{9,5},... | collective-permute-start | bytes 491528 | tf_op jit(solution)/shard_map/ppermute | solution.py:833
  27.9 5.8 %collective-permute-start.9 = (f32[832,128]{1,0:T(8,128)S(1)}, f32[832,128]{1,0:T(8,128)S(1)}, u32[]{:S(2)}, u32[]{:S(2)}) collective-permute-start(f32[832,128]{1,0:T(8,128)S(1)} %get-tuple-element.42), channel_id=1, source_target_pairs={{0,1},{1,0},{2,3},{3,2},{4,5},{5,4},{6,7},{7,6},{8,9},{9,8},{10,11... | collective-permute-start | bytes 1277960 | tf_op jit(solution)/shard_map/ppermute | solution.py:832
  28.0 9.6 %collective-permute-start.10 = (f32[832,128]{1,0:T(8,128)S(1)}, f32[832,128]{1,0:T(8,128)S(1)}, u32[]{:S(2)}, u32[]{:S(2)}) collective-permute-start(f32[832,128]{1,0:T(8,128)S(1)} %get-tuple-element.43), channel_id=1, source_target_pairs={{0,16},{1,2},{2,1},{3,19},{4,20},{5,6},{6,5},{7,23},{8,24},{9,10},... | collective-permute-start | bytes 1277960 | tf_op jit(solution)/shard_map/ppermute | solution.py:833
  29.3 12.3 %collective-permute-start.11 = (f32[256,128]{1,0:T(8,128)S(1)}, f32[256,128]{1,0:T(8,128)S(1)}, u32[]{:S(2)}, u32[]{:S(2)}) collective-permute-start(f32[256,128]{1,0:T(8,128)S(1)} %get-tuple-element.49), channel_id=1, source_target_pairs={{0,4},{1,5},{2,6},{3,7},{4,0},{5,1},{6,2},{7,3},{8,12},{9,13},{10,... | collective-permute-start | bytes 393224 | tf_op jit(solution)/shard_map/ppermute | solution.py:832
  29.5 12.0 %collective-permute-start.12 = (f32[256,128]{1,0:T(8,128)S(1)}, f32[256,128]{1,0:T(8,128)S(1)}, u32[]{:S(2)}, u32[]{:S(2)}) collective-permute-start(f32[256,128]{1,0:T(8,128)S(1)} %get-tuple-element.50), channel_id=1, source_target_pairs={{0,16},{1,17},{2,18},{3,19},{4,8},{5,9},{6,10},{7,11},{8,4},{9,5},... | collective-permute-start | bytes 393224 | tf_op jit(solution)/shard_map/ppermute | solution.py:833
  42.2 6.7 %collective-permute-start.13 = (f32[256,128]{1,0:T(8,128)S(1)}, f32[256,128]{1,0:T(8,128)S(1)}, u32[]{:S(2)}, u32[]{:S(2)}) collective-permute-start(f32[256,128]{1,0:T(8,128)S(1)} %get-tuple-element.51), channel_id=1, source_target_pairs={{0,1},{1,0},{2,3},{3,2},{4,5},{5,4},{6,7},{7,6},{8,9},{9,8},{10,11... | collective-permute-start | bytes 393224 | tf_op jit(solution)/shard_map/ppermute | solution.py:832
  42.3 6.6 %collective-permute-start.14 = (f32[256,128]{1,0:T(8,128)S(1)}, f32[256,128]{1,0:T(8,128)S(1)}, u32[]{:S(2)}, u32[]{:S(2)}) collective-permute-start(f32[256,128]{1,0:T(8,128)S(1)} %get-tuple-element.52), channel_id=1, source_target_pairs={{0,16},{1,2},{2,1},{3,19},{4,20},{5,6},{6,5},{7,23},{8,24},{9,10},... | collective-permute-start | bytes 393224 | tf_op jit(solution)/shard_map/ppermute | solution.py:833
  43.4 4.5 %collective-permute-start.15 = (f32[176,128]{1,0:T(8,128)S(1)}, f32[176,128]{1,0:T(8,128)S(1)}, u32[]{:S(2)}, u32[]{:S(2)}) collective-permute-start(f32[176,128]{1,0:T(8,128)S(1)} %get-tuple-element.53), channel_id=1, source_target_pairs={{0,4},{1,5},{2,6},{3,7},{4,0},{5,1},{6,2},{7,3},{8,12},{9,13},{10,... | collective-permute-start | bytes 270344 | tf_op jit(solution)/shard_map/ppermute | solution.py:832
  43.4 5.5 %collective-permute-start.16 = (f32[176,128]{1,0:T(8,128)S(1)}, f32[176,128]{1,0:T(8,128)S(1)}, u32[]{:S(2)}, u32[]{:S(2)}) collective-permute-start(f32[176,128]{1,0:T(8,128)S(1)} %get-tuple-element.54), channel_id=1, source_target_pairs={{0,16},{1,17},{2,18},{3,19},{4,8},{5,9},{6,10},{7,11},{8,4},{9,5},... | collective-permute-start | bytes 270344 | tf_op jit(solution)/shard_map/ppermute | solution.py:833
  49.6 2.0 %collective-permute-start.17 = (f32[304,128]{1,0:T(8,128)S(1)}, f32[304,128]{1,0:T(8,128)S(1)}, u32[]{:S(2)}, u32[]{:S(2)}) collective-permute-start(f32[304,128]{1,0:T(8,128)S(1)} %get-tuple-element.55), channel_id=1, source_target_pairs={{0,1},{1,0},{2,3},{3,2},{4,5},{5,4},{6,7},{7,6},{8,9},{9,8},{10,11... | collective-permute-start | bytes 466952 | tf_op jit(solution)/shard_map/ppermute | solution.py:832
  49.7 5.3 %collective-permute-start.18 = (f32[304,128]{1,0:T(8,128)S(1)}, f32[304,128]{1,0:T(8,128)S(1)}, u32[]{:S(2)}, u32[]{:S(2)}) collective-permute-start(f32[304,128]{1,0:T(8,128)S(1)} %get-tuple-element.56), channel_id=1, source_target_pairs={{0,16},{1,2},{2,1},{3,19},{4,20},{5,6},{6,5},{7,23},{8,24},{9,10},... | collective-permute-start | bytes 466952 | tf_op jit(solution)/shard_map/ppermute | solution.py:833
  51.5 29.8 %copy-start.2 = (f32[1,128,128]{2,1,0:T(8,128)S(1)}, f32[1,128,128]{2,1,0:T(8,128)}, u32[]{:S(2)}) copy-start(f32[1,128,128]{2,1,0:T(8,128)} %start_ref.3) | copy-start | bytes 196612
  62.5 1.4 %collective-permute-start.19 = (f32[208,128]{1,0:T(8,128)S(1)}, f32[208,128]{1,0:T(8,128)S(1)}, u32[]{:S(2)}, u32[]{:S(2)}) collective-permute-start(f32[208,128]{1,0:T(8,128)S(1)} %get-tuple-element.62), channel_id=1, source_target_pairs={{0,1},{1,0},{2,3},{3,2},{4,5},{5,4},{6,7},{7,6},{8,9},{9,8},{10,11... | collective-permute-start | bytes 319496 | tf_op jit(solution)/shard_map/ppermute | solution.py:832
  62.7 4.7 %collective-permute-start.20 = (f32[208,128]{1,0:T(8,128)S(1)}, f32[208,128]{1,0:T(8,128)S(1)}, u32[]{:S(2)}, u32[]{:S(2)}) collective-permute-start(f32[208,128]{1,0:T(8,128)S(1)} %get-tuple-element.63), channel_id=1, source_target_pairs={{0,16},{1,2},{2,1},{3,19},{4,20},{5,6},{6,5},{7,23},{8,24},{9,10},... | collective-permute-start | bytes 319496 | tf_op jit(solution)/shard_map/ppermute | solution.py:833

commit v5 on v4

--- a/solution.py
+++ b/solution.py
@@ -202,7 +202,7 @@
             backward(g)
         return carry
 
-    lax.fori_loop(0, guides, body, 0)
+    lax.fori_loop(0, guides, body, 0, unroll=4 if x is None or acc is None else 2)
 
 
 def store_field(x_ref, slot, at, n, even, odd):

time: 82.8 us -> 81.6 us (0.986)
  Pallas kernels: 25.7 us -> 24 us
    pallas_call x12, Pallas kernels: 25.7 us -> 24 us  [call(): pl.pallas_call(kernel, out_shape=[jax.ShapeDtypeStruct(shape, F32) for sh...]
  transfers between devices with their start and end apart: 21 -> 21, of which waited for: 10 -> 10; matrix products, arithmetic and copies ran while one was open for 2% -> 2% of each run, Pallas kernels for 11% -> 10%
where the time goes in v5:
time: 81.6 us; the launch traced here: 81.2 us
  Pallas kernels  24 us (29%)
  waiting for transfers between devices  23.3 us (29%)
  starting transfers between devices  17.7 us (22%)
  blocking collectives  10.2 us (12%)
  local copies, waits for them, and re-layouts  4.44 us (5%)
  between operations  1.49 us (2%)
    pallas_call x12, Pallas kernels, call(): pl.pallas_call(kernel, out_shape=[jax.ShapeDtypeStruct(shape, F32) for sh...  24 us
    ppermute x9, waiting for transfers between devices, swap(): lax.ppermute(b, axes, pairs(lambda i: i - 1 if i % 2 == 0 else i + 1))  13.9 us
    all_to_all x1, blocking collectives, shards(): sums = lax.all_to_all(sums, ('gx', 'gy'), 0, 0)  10.2 us
    ppermute x9, starting transfers between devices, swap(): lax.ppermute(b, axes, pairs(lambda i: i - 1 if i % 2 == 0 else i + 1))  8.57 us
    ppermute x9, waiting for transfers between devices, swap(): lax.ppermute(a, axes, pairs(lambda i: i ^ 1))  7.9 us
    ppermute x9, starting transfers between devices, swap(): lax.ppermute(a, axes, pairs(lambda i: i ^ 1))  6.35 us
    unnamed x10, local copies, waits for them, and re-layouts  4.26 us
    ppermute x3, starting transfers between devices, shards(): lax.ppermute(x, 'layer', [(i, (i + k) % slots) for i in range(slots)])  2.73 us
  transfers between devices with their start and end apart: 21, of which 10 were waited for; matrix products, arithmetic and copies ran while one was open for 2% of the time, Pallas kernels for 10%

profile of v5, /device:TPU:0, one launch (start us, length us, event | category | flops | bytes accessed | tf_op | source)
XLA Modules:
  0.0 81.2 jit_solution(9195873961681857050)
XLA Ops:
  1.3 0.8 %copy-done.1 = f32[1,128,128]{2,1,0:T(8,128)S(1)} copy-done((f32[1,128,128]{2,1,0:T(8,128)S(1)}, f32[1,128,128]{2,1,0:T(8,128)}, u32[]{:S(2)}) %copy-start.1) | copy-done | bytes 65560
  2.2 0.8 %copy-done.3 = f32[1,128,128]{2,1,0:T(8,128)S(1)} copy-done((f32[1,128,128]{2,1,0:T(8,128)S(1)}, f32[1,128,128]{2,1,0:T(8,128)}, u32[]{:S(2)}) %copy-start.3) | copy-done | bytes 65560
  3.0 0.7 shard_map.77
  3.7 3.1 %collective-permute-start = (f32[80,128]{1,0:T(8,128)S(1)}, f32[80,128]{1,0:T(8,128)S(1)}, u32[]{:S(2)}, u32[]{:S(2)}) collective-permute-start(f32[80,128]{1,0:T(8,128)S(1)} %get-tuple-element.34), channel_id=1, source_target_pairs={{0,4},{1,5},{2,6},{3,7},{4,0},{5,1},{6,2},{7,3},{8,12},{9,13},{10,... | collective-permute-start | bytes 122888 | tf_op jit(solution)/shard_map/ppermute | solution.py:832
  6.8 1.5 %collective-permute-start.1 = (f32[80,128]{1,0:T(8,128)S(1)}, f32[80,128]{1,0:T(8,128)S(1)}, u32[]{:S(2)}, u32[]{:S(2)}) collective-permute-start(f32[80,128]{1,0:T(8,128)S(1)} %get-tuple-element.35), channel_id=1, source_target_pairs={{0,16},{1,17},{2,18},{3,19},{4,8},{5,9},{6,10},{7,11},{8,4},{9,5},... | collective-permute-start | bytes 122888 | tf_op jit(solution)/shard_map/ppermute | solution.py:833
  8.9 0.8 copy.10
  9.7 0.8 copy.11
  10.6 1.6 %collective-permute-start.5 = (f32[80,128]{1,0:T(8,128)S(1)}, f32[80,128]{1,0:T(8,128)S(1)}, u32[]{:S(2)}, u32[]{:S(2)}) collective-permute-start(f32[80,128]{1,0:T(8,128)S(1)} %collective-permute-done._.refs_2_), channel_id=1, source_target_pairs={{0,16},{16,0},{1,17},{17,1},{2,18},{18,2},{3,19},{19,3},{4,20},{20... | collective-permute-start | bytes 122888 | tf_op jit(solution)/shard_map/ppermute | solution.py:856
  12.9 1.0 %copy-done = s32[8,128,128]{2,1,0:T(8,128)S(1)} copy-done((s32[8,128,128]{2,1,0:T(8,128)S(1)}, s32[8,128,128]{2,1,0:T(8,128)}, u32[]{:S(2)}) %copy-start) | copy-done | bytes 524312
  13.9 0.8 shard_map.78
  14.9 1.3 %collective-permute-done.6.refs_5_ = f32[80,128]{1,0:T(8,128)S(1)} collective-permute-done((f32[80,128]{1,0:T(8,128)S(1)}, f32[80,128]{1,0:T(8,128)S(1)}, u32[]{:S(2)}, u32[]{:S(2)}) %collective-permute-start.6) | collective-permute-done | bytes 40992 | tf_op jit(solution)/shard_map/ppermute | solution.py:856
  16.2 1.5 %shard_map.79 = (f32[416,128]{1,0:T(8,128)S(1)}, f32[416,128]{1,0:T(8,128)S(1)}) custom-call(s32[8]{0:T(128)S(1)} %compare_select_fusion.6.meta_ref, f32[264,128]{1,0:T(8,128)S(1)} %get-tuple-element.39.refs_0_, f32[264,128]{1,0:T(8,128)S(1)} %collective-permute-done.4.refs_1_, f32[80,128]{1,0:T(8,128)S(1)} %collective-permute-done._.refs_2_, ...), custom_call_target="tpu_custom_call" | custom-call | tf_op jit(solution)/shard_map/pallas_call | solution.py:803
  18.4 2.5 %collective-permute-start.2 = (f32[320,128]{1,0:T(8,128)S(1)}, f32[320,128]{1,0:T(8,128)S(1)}, u32[]{:S(2)}, u32[]{:S(2)}) collective-permute-start(f32[320,128]{1,0:T(8,128)S(1)} %get-tuple-element.37), channel_id=1, source_target_pairs={{0,4},{1,5},{2,6},{3,7},{4,0},{5,1},{6,2},{7,3},{8,12},{9,13},{10,... | collective-permute-start | bytes 491528 | tf_op jit(solution)/shard_map/ppermute | solution.py:832
  21.5 4.1 %collective-permute-done.2.va = f32[320,128]{1,0:T(8,128)S(1)} collective-permute-done((f32[320,128]{1,0:T(8,128)S(1)}, f32[320,128]{1,0:T(8,128)S(1)}, u32[]{:S(2)}, u32[]{:S(2)}) %collective-permute-start.2) | collective-permute-done | bytes 163872 | tf_op jit(solution)/shard_map/ppermute | solution.py:832
  25.5 1.6 %collective-permute-done.3.vb = f32[320,128]{1,0:T(8,128)S(1)} collective-permute-done((f32[320,128]{1,0:T(8,128)S(1)}, f32[320,128]{1,0:T(8,128)S(1)}, u32[]{:S(2)}, u32[]{:S(2)}) %collective-permute-start.3) | collective-permute-done | bytes 163872 | tf_op jit(solution)/shard_map/ppermute | solution.py:833
  28.0 1.3 %collective-permute-start.10 = (f32[832,128]{1,0:T(8,128)S(1)}, f32[832,128]{1,0:T(8,128)S(1)}, u32[]{:S(2)}, u32[]{:S(2)}) collective-permute-start(f32[832,128]{1,0:T(8,128)S(1)} %get-tuple-element.43), channel_id=1, source_target_pairs={{0,16},{1,2},{2,1},{3,19},{4,20},{5,6},{6,5},{7,23},{8,24},{9,10},... | collective-permute-start | bytes 1277960 | tf_op jit(solution)/shard_map/ppermute | solution.py:833
  30.2 3.0 %shard_map.81 = (f32[8,2,208,128]{3,2,1,0:T(8,128)S(1)}, f32[2,2,176,128]{3,2,1,0:T(8,128)S(1)}, f32[16,128]{1,0:T(8,128)S(1)}) custom-call(s32[8]{0:T(128)S(1)} %compare_select_fusion.6.meta_ref, s32[64]{0:T(128)S(1)} %pad_add_fusion.refs_6_.table_ref, f32[416,128]{1,0:T(8,128)S(1)} %collective-permute-done.7._.ga, ...), custom_call_target="tpu_custom_call" | custom-call | tf_op jit(solution)/shard_map/pallas_call | solution.py:803
  33.2 4.4 %collective-permute-done.10.nb.near_b = f32[832,128]{1,0:T(8,128)S(1)} collective-permute-done((f32[832,128]{1,0:T(8,128)S(1)}, f32[832,128]{1,0:T(8,128)S(1)}, u32[]{:S(2)}, u32[]{:S(2)}) %collective-permute-start.10) | collective-permute-done | bytes 426016 | tf_op jit(solution)/shard_map/ppermute | solution.py:833
  37.6 3.5 %shard_map.82 = (f32[1,2,128,128]{3,2,1,0:T(8,128)S(1)}, f32[176,128]{1,0:T(8,128)S(1)}, f32[176,128]{1,0:T(8,128)S(1)}, f32[2,128,128]{2,1,0:T(8,128)S(1)}, f32[8,128]{1,0:T(8,128)S(1)}) custom-call(s32[8]{0:T(128)S(1)} %compare_select_fusion.6.meta_ref, s32[64]{0:T(128)S(1)} %pad_add_fusion.refs_6_.table_ref, ...), custom_call_target="tpu_custom_call" | custom-call | tf_op jit(solution)/shard_map/pallas_call | solution.py:803
  41.8 1.1 %collective-permute-start.14 = (f32[256,128]{1,0:T(8,128)S(1)}, f32[256,128]{1,0:T(8,128)S(1)}, u32[]{:S(2)}, u32[]{:S(2)}) collective-permute-start(f32[256,128]{1,0:T(8,128)S(1)} %get-tuple-element.52), channel_id=1, source_target_pairs={{0,16},{1,2},{2,1},{3,19},{4,20},{5,6},{6,5},{7,23},{8,24},{9,10},... | collective-permute-start | bytes 393224 | tf_op jit(solution)/shard_map/ppermute | solution.py:833
  42.9 1.0 %collective-permute-start.16 = (f32[176,128]{1,0:T(8,128)S(1)}, f32[176,128]{1,0:T(8,128)S(1)}, u32[]{:S(2)}, u32[]{:S(2)}) collective-permute-start(f32[176,128]{1,0:T(8,128)S(1)} %get-tuple-element.54), channel_id=1, source_target_pairs={{0,16},{1,17},{2,18},{3,19},{4,8},{5,9},{6,10},{7,11},{8,4},{9,5},... | collective-permute-start | bytes 270344 | tf_op jit(solution)/shard_map/ppermute | solution.py:833
  43.9 3.5 %collective-permute-done.15.za = f32[176,128]{1,0:T(8,128)S(1)} collective-permute-done((f32[176,128]{1,0:T(8,128)S(1)}, f32[176,128]{1,0:T(8,128)S(1)}, u32[]{:S(2)}, u32[]{:S(2)}) %collective-permute-start.15) | collective-permute-done | bytes 90144 | tf_op jit(solution)/shard_map/ppermute | solution.py:832
  47.4 1.0 %collective-permute-done.16.zb = f32[176,128]{1,0:T(8,128)S(1)} collective-permute-done((f32[176,128]{1,0:T(8,128)S(1)}, f32[176,128]{1,0:T(8,128)S(1)}, u32[]{:S(2)}, u32[]{:S(2)}) %collective-permute-start.16) | collective-permute-done | bytes 90144 | tf_op jit(solution)/shard_map/ppermute | solution.py:833
  49.1 0.9 %collective-permute-start.18 = (f32[304,128]{1,0:T(8,128)S(1)}, f32[304,128]{1,0:T(8,128)S(1)}, u32[]{:S(2)}, u32[]{:S(2)}) collective-permute-start(f32[304,128]{1,0:T(8,128)S(1)} %get-tuple-element.56), channel_id=1, source_target_pairs={{0,16},{1,2},{2,1},{3,19},{4,20},{5,6},{6,5},{7,23},{8,24},{9,10},... | collective-permute-start | bytes 466952 | tf_op jit(solution)/shard_map/ppermute | solution.py:833
  50.1 0.9 %shard_map.84.valid_ref = f32[8,2,272,128]{3,2,1,0:T(8,128)S(1)} custom-call(s32[8]{0:T(128)S(1)} %compare_select_fusion.6.meta_ref, f32[4,2,128,128]{3,2,1,0:T(8,128)S(1)} %get-tuple-element.36.refs_7_.v_ref, f32[320,128]{1,0:T(8,128)S(1)} %collective-permute-done.2.va, f32[320,128]{1,0:T(8,128)S(1)} %collective-permute-done.3.vb, ...), custom_call_target="tpu_custom_call" | custom-call | tf_op jit(solution)/shard_map/pallas_call | solution.py:803
  51.0 3.4 %collective-permute-done.18.gb = f32[304,128]{1,0:T(8,128)S(1)} collective-permute-done((f32[304,128]{1,0:T(8,128)S(1)}, f32[304,128]{1,0:T(8,128)S(1)}, u32[]{:S(2)}, u32[]{:S(2)}) %collective-permute-start.18) | collective-permute-done | bytes 155680 | tf_op jit(solution)/shard_map/ppermute | solution.py:833
  54.4 7.2 %shard_map.86 = (f32[1,2,208,128]{3,2,1,0:T(8,128)S(1)}, f32[208,128]{1,0:T(8,128)S(1)}, f32[208,128]{1,0:T(8,128)S(1)}, f32[2,128,128]{2,1,0:T(8,128)S(1)}, f32[8,128]{1,0:T(8,128)S(1)}, /*index=5*/f32[8,128]{1,0:T(8,128)S(1)}) custom-call(s32[8]{0:T(128)S(1)} %compare_select_fusion.6.meta_ref, s32[64]{0:T(128)S(1)} %pad_add_fusion.refs_6_.table_ref, ...), custom_call_target="tpu_custom_call" | custom-call | tf_op jit(solution)/shard_map/pallas_call | solution.py:803
  61.8 0.9 %collective-permute-start.20 = (f32[208,128]{1,0:T(8,128)S(1)}, f32[208,128]{1,0:T(8,128)S(1)}, u32[]{:S(2)}, u32[]{:S(2)}) collective-permute-start(f32[208,128]{1,0:T(8,128)S(1)} %get-tuple-element.63), channel_id=1, source_target_pairs={{0,16},{1,2},{2,1},{3,19},{4,20},{5,6},{6,5},{7,23},{8,24},{9,10},... | collective-permute-start | bytes 319496 | tf_op jit(solution)/shard_map/ppermute | solution.py:833
  63.0 3.5 %collective-permute-done.20.gb = f32[208,128]{1,0:T(8,128)S(1)} collective-permute-done((f32[208,128]{1,0:T(8,128)S(1)}, f32[208,128]{1,0:T(8,128)S(1)}, u32[]{:S(2)}, u32[]{:S(2)}) %collective-permute-start.20) | collective-permute-done | bytes 106528 | tf_op jit(solution)/shard_map/ppermute | solution.py:833
  66.5 3.4 %shard_map.87 = (f32[2,128,128]{2,1,0:T(8,128)S(1)}, f32[16,8,128]{2,1,0:T(8,128)S(1)}) custom-call(s32[8]{0:T(128)S(1)} %compare_select_fusion.6.meta_ref, s32[64]{0:T(128)S(1)} %pad_add_fusion.refs_6_.table_ref, f32[1,2,208,128]{3,2,1,0:T(8,128)S(1)} %get-tuple-element.58.y_ref, f32[16,128]{1,0:T(8,128)S(1)} %get-tuple-element.46.reg_ref.__, ...), custom_call_target="tpu_custom_call" | custom-call | tf_op jit(solution)/shard_map/pallas_call | solution.py:803
  69.9 10.2 %all_to_all.5.sums_ref = f32[16,8,128]{2,1,0:T(8,128)S(1)} all-to-all(f32[16,8,128]{2,1,0:T(8,128)S(1)} %get-tuple-element.65), channel_id=1, replica_groups=mesh['layer'=2,'gx'=4,'gy'=4] {'gx','gy'}, dimensions={0} | all-to-all | bytes 131072 | tf_op jit(solution)/shard_map/all_to_all | solution.py:947
  80.2 1.0 %shard_map.88 = (f32[1,128,128]{2,1,0:T(8,128)}, f32[1,128,128]{2,1,0:T(8,128)}) custom-call(f32[1,128,128]{2,1,0:T(8,128)S(1)} %copy-done.2, f32[1,2,128,128]{3,2,1,0:T(8,128)S(1)} %get-tuple-element.47._.z_ref, f32[2,128,128]{2,1,0:T(8,128)S(1)} %get-tuple-element.48.res_ref, f32[2,128,128]{2,1,0:T(8,128)S(1)} %get-tuple-element.57.q_ref, ...), custom_call_target="tpu_custom_call" | custom-call | tf_op jit(solution)/shard_map/pallas_call | solution.py:803
  (37 shorter events, 6.5 us)
Async XLA Ops:
  1.3 0.8 %copy-start.1 = (f32[1,128,128]{2,1,0:T(8,128)S(1)}, f32[1,128,128]{2,1,0:T(8,128)}, u32[]{:S(2)}) copy-start(f32[1,128,128]{2,1,0:T(8,128)} %start_ref.3) | copy-start | bytes 196612
  2.1 0.8 %copy-start.3 = (f32[1,128,128]{2,1,0:T(8,128)S(1)}, f32[1,128,128]{2,1,0:T(8,128)}, u32[]{:S(2)}) copy-start(f32[1,128,128]{2,1,0:T(8,128)} %rhs_ref.1) | copy-start | bytes 196612
  3.7 6.8 %collective-permute-start = (f32[80,128]{1,0:T(8,128)S(1)}, f32[80,128]{1,0:T(8,128)S(1)}, u32[]{:S(2)}, u32[]{:S(2)}) collective-permute-start(f32[80,128]{1,0:T(8,128)S(1)} %get-tuple-element.34), channel_id=1, source_target_pairs={{0,4},{1,5},{2,6},{3,7},{4,0},{5,1},{6,2},{7,3},{8,12},{9,13},{10,... | collective-permute-start | bytes 122888 | tf_op jit(solution)/shard_map/ppermute | solution.py:832
  6.8 5.4 %collective-permute-start.1 = (f32[80,128]{1,0:T(8,128)S(1)}, f32[80,128]{1,0:T(8,128)S(1)}, u32[]{:S(2)}, u32[]{:S(2)}) collective-permute-start(f32[80,128]{1,0:T(8,128)S(1)} %get-tuple-element.35), channel_id=1, source_target_pairs={{0,16},{1,17},{2,18},{3,19},{4,8},{5,9},{6,10},{7,11},{8,4},{9,5},... | collective-permute-start | bytes 122888 | tf_op jit(solution)/shard_map/ppermute | solution.py:833
  8.3 7.8 %collective-permute-start.4 = (f32[264,128]{1,0:T(8,128)S(1)}, f32[264,128]{1,0:T(8,128)S(1)}, u32[]{:S(2)}, u32[]{:S(2)}) collective-permute-start(f32[264,128]{1,0:T(8,128)S(1)} %get-tuple-element.39.refs_0_), channel_id=1, source_target_pairs={{0,16},{16,0},{1,17},{17,1},{2,18},{18,2},{3,19},{19,3},{4,20},{20... | collective-permute-start | bytes 405512 | tf_op jit(solution)/shard_map/ppermute | solution.py:856
  10.6 4.3 %collective-permute-start.5 = (f32[80,128]{1,0:T(8,128)S(1)}, f32[80,128]{1,0:T(8,128)S(1)}, u32[]{:S(2)}, u32[]{:S(2)}) collective-permute-start(f32[80,128]{1,0:T(8,128)S(1)} %collective-permute-done._.refs_2_), channel_id=1, source_target_pairs={{0,16},{16,0},{1,17},{17,1},{2,18},{18,2},{3,19},{19,3},{4,20},{20... | collective-permute-start | bytes 122888 | tf_op jit(solution)/shard_map/ppermute | solution.py:856
  12.2 4.0 %collective-permute-start.6 = (f32[80,128]{1,0:T(8,128)S(1)}, f32[80,128]{1,0:T(8,128)S(1)}, u32[]{:S(2)}, u32[]{:S(2)}) collective-permute-start(f32[80,128]{1,0:T(8,128)S(1)} %collective-permute-done.1.__.refs_4_), channel_id=1, source_target_pairs={{0,16},{16,0},{1,17},{17,1},{2,18},{18,2},{3,19},{19,3},{4,20},{20... | collective-permute-start | bytes 122888 | tf_op jit(solution)/shard_map/ppermute | solution.py:856
  12.9 1.0 %copy-start = (s32[8,128,128]{2,1,0:T(8,128)S(1)}, s32[8,128,128]{2,1,0:T(8,128)}, u32[]{:S(2)}) copy-start(s32[8,128,128]{2,1,0:T(8,128)} %valid_ref.1) | copy-start | bytes 1572868
  17.6 9.5 %collective-permute-start.7 = (f32[416,128]{1,0:T(8,128)S(1)}, f32[416,128]{1,0:T(8,128)S(1)}, u32[]{:S(2)}, u32[]{:S(2)}) collective-permute-start(f32[416,128]{1,0:T(8,128)S(1)} %get-tuple-element.40), channel_id=1, source_target_pairs={{0,1},{1,0},{2,3},{3,2},{4,5},{5,4},{6,7},{7,6},{8,9},{9,8},{10,11... | collective-permute-start | bytes 638984 | tf_op jit(solution)/shard_map/ppermute | solution.py:832
  17.7 9.4 %collective-permute-start.8 = (f32[416,128]{1,0:T(8,128)S(1)}, f32[416,128]{1,0:T(8,128)S(1)}, u32[]{:S(2)}, u32[]{:S(2)}) collective-permute-start(f32[416,128]{1,0:T(8,128)S(1)} %get-tuple-element.41), channel_id=1, source_target_pairs={{0,16},{1,2},{2,1},{3,19},{4,20},{5,6},{6,5},{7,23},{8,24},{9,10},... | collective-permute-start | bytes 638984 | tf_op jit(solution)/shard_map/ppermute | solution.py:833
  18.4 7.1 %collective-permute-start.2 = (f32[320,128]{1,0:T(8,128)S(1)}, f32[320,128]{1,0:T(8,128)S(1)}, u32[]{:S(2)}, u32[]{:S(2)}) collective-permute-start(f32[320,128]{1,0:T(8,128)S(1)} %get-tuple-element.37), channel_id=1, source_target_pairs={{0,4},{1,5},{2,6},{3,7},{4,0},{5,1},{6,2},{7,3},{8,12},{9,13},{10,... | collective-permute-start | bytes 491528 | tf_op jit(solution)/shard_map/ppermute | solution.py:832
  20.9 6.2 %collective-permute-start.3 = (f32[320,128]{1,0:T(8,128)S(1)}, f32[320,128]{1,0:T(8,128)S(1)}, u32[]{:S(2)}, u32[]{:S(2)}) collective-permute-start(f32[320,128]{1,0:T(8,128)S(1)} %get-tuple-element.38), channel_id=1, source_target_pairs={{0,16},{1,17},{2,18},{3,19},{4,8},{5,9},{6,10},{7,11},{8,4},{9,5},... | collective-permute-start | bytes 491528 | tf_op jit(solution)/shard_map/ppermute | solution.py:833
  27.9 5.3 %collective-permute-start.9 = (f32[832,128]{1,0:T(8,128)S(1)}, f32[832,128]{1,0:T(8,128)S(1)}, u32[]{:S(2)}, u32[]{:S(2)}) collective-permute-start(f32[832,128]{1,0:T(8,128)S(1)} %get-tuple-element.42), channel_id=1, source_target_pairs={{0,1},{1,0},{2,3},{3,2},{4,5},{5,4},{6,7},{7,6},{8,9},{9,8},{10,11... | collective-permute-start | bytes 1277960 | tf_op jit(solution)/shard_map/ppermute | solution.py:832
  28.0 9.6 %collective-permute-start.10 = (f32[832,128]{1,0:T(8,128)S(1)}, f32[832,128]{1,0:T(8,128)S(1)}, u32[]{:S(2)}, u32[]{:S(2)}) collective-permute-start(f32[832,128]{1,0:T(8,128)S(1)} %get-tuple-element.43), channel_id=1, source_target_pairs={{0,16},{1,2},{2,1},{3,19},{4,20},{5,6},{6,5},{7,23},{8,24},{9,10},... | collective-permute-start | bytes 1277960 | tf_op jit(solution)/shard_map/ppermute | solution.py:833
  29.3 11.8 %collective-permute-start.11 = (f32[256,128]{1,0:T(8,128)S(1)}, f32[256,128]{1,0:T(8,128)S(1)}, u32[]{:S(2)}, u32[]{:S(2)}) collective-permute-start(f32[256,128]{1,0:T(8,128)S(1)} %get-tuple-element.49), channel_id=1, source_target_pairs={{0,4},{1,5},{2,6},{3,7},{4,0},{5,1},{6,2},{7,3},{8,12},{9,13},{10,... | collective-permute-start | bytes 393224 | tf_op jit(solution)/shard_map/ppermute | solution.py:832
  29.5 11.5 %collective-permute-start.12 = (f32[256,128]{1,0:T(8,128)S(1)}, f32[256,128]{1,0:T(8,128)S(1)}, u32[]{:S(2)}, u32[]{:S(2)}) collective-permute-start(f32[256,128]{1,0:T(8,128)S(1)} %get-tuple-element.50), channel_id=1, source_target_pairs={{0,16},{1,17},{2,18},{3,19},{4,8},{5,9},{6,10},{7,11},{8,4},{9,5},... | collective-permute-start | bytes 393224 | tf_op jit(solution)/shard_map/ppermute | solution.py:833
  41.7 6.7 %collective-permute-start.13 = (f32[256,128]{1,0:T(8,128)S(1)}, f32[256,128]{1,0:T(8,128)S(1)}, u32[]{:S(2)}, u32[]{:S(2)}) collective-permute-start(f32[256,128]{1,0:T(8,128)S(1)} %get-tuple-element.51), channel_id=1, source_target_pairs={{0,1},{1,0},{2,3},{3,2},{4,5},{5,4},{6,7},{7,6},{8,9},{9,8},{10,11... | collective-permute-start | bytes 393224 | tf_op jit(solution)/shard_map/ppermute | solution.py:832
  41.8 6.6 %collective-permute-start.14 = (f32[256,128]{1,0:T(8,128)S(1)}, f32[256,128]{1,0:T(8,128)S(1)}, u32[]{:S(2)}, u32[]{:S(2)}) collective-permute-start(f32[256,128]{1,0:T(8,128)S(1)} %get-tuple-element.52), channel_id=1, source_target_pairs={{0,16},{1,2},{2,1},{3,19},{4,20},{5,6},{6,5},{7,23},{8,24},{9,10},... | collective-permute-start | bytes 393224 | tf_op jit(solution)/shard_map/ppermute | solution.py:833
  42.9 4.5 %collective-permute-start.15 = (f32[176,128]{1,0:T(8,128)S(1)}, f32[176,128]{1,0:T(8,128)S(1)}, u32[]{:S(2)}, u32[]{:S(2)}) collective-permute-start(f32[176,128]{1,0:T(8,128)S(1)} %get-tuple-element.53), channel_id=1, source_target_pairs={{0,4},{1,5},{2,6},{3,7},{4,0},{5,1},{6,2},{7,3},{8,12},{9,13},{10,... | collective-permute-start | bytes 270344 | tf_op jit(solution)/shard_map/ppermute | solution.py:832
  42.9 5.5 %collective-permute-start.16 = (f32[176,128]{1,0:T(8,128)S(1)}, f32[176,128]{1,0:T(8,128)S(1)}, u32[]{:S(2)}, u32[]{:S(2)}) collective-permute-start(f32[176,128]{1,0:T(8,128)S(1)} %get-tuple-element.54), channel_id=1, source_target_pairs={{0,16},{1,17},{2,18},{3,19},{4,8},{5,9},{6,10},{7,11},{8,4},{9,5},... | collective-permute-start | bytes 270344 | tf_op jit(solution)/shard_map/ppermute | solution.py:833
  49.1 1.9 %collective-permute-start.17 = (f32[304,128]{1,0:T(8,128)S(1)}, f32[304,128]{1,0:T(8,128)S(1)}, u32[]{:S(2)}, u32[]{:S(2)}) collective-permute-start(f32[304,128]{1,0:T(8,128)S(1)} %get-tuple-element.55), channel_id=1, source_target_pairs={{0,1},{1,0},{2,3},{3,2},{4,5},{5,4},{6,7},{7,6},{8,9},{9,8},{10,11... | collective-permute-start | bytes 466952 | tf_op jit(solution)/shard_map/ppermute | solution.py:832
  49.1 5.3 %collective-permute-start.18 = (f32[304,128]{1,0:T(8,128)S(1)}, f32[304,128]{1,0:T(8,128)S(1)}, u32[]{:S(2)}, u32[]{:S(2)}) collective-permute-start(f32[304,128]{1,0:T(8,128)S(1)} %get-tuple-element.56), channel_id=1, source_target_pairs={{0,16},{1,2},{2,1},{3,19},{4,20},{5,6},{6,5},{7,23},{8,24},{9,10},... | collective-permute-start | bytes 466952 | tf_op jit(solution)/shard_map/ppermute | solution.py:833
  51.0 29.2 %copy-start.2 = (f32[1,128,128]{2,1,0:T(8,128)S(1)}, f32[1,128,128]{2,1,0:T(8,128)}, u32[]{:S(2)}) copy-start(f32[1,128,128]{2,1,0:T(8,128)} %start_ref.3) | copy-start | bytes 196612
  61.6 1.4 %collective-permute-start.19 = (f32[208,128]{1,0:T(8,128)S(1)}, f32[208,128]{1,0:T(8,128)S(1)}, u32[]{:S(2)}, u32[]{:S(2)}) collective-permute-start(f32[208,128]{1,0:T(8,128)S(1)} %get-tuple-element.62), channel_id=1, source_target_pairs={{0,1},{1,0},{2,3},{3,2},{4,5},{5,4},{6,7},{7,6},{8,9},{9,8},{10,11... | collective-permute-start | bytes 319496 | tf_op jit(solution)/shard_map/ppermute | solution.py:832
  61.8 4.7 %collective-permute-start.20 = (f32[208,128]{1,0:T(8,128)S(1)}, f32[208,128]{1,0:T(8,128)S(1)}, u32[]{:S(2)}, u32[]{:S(2)}) collective-permute-start(f32[208,128]{1,0:T(8,128)S(1)} %get-tuple-element.63), channel_id=1, source_target_pairs={{0,16},{1,2},{2,1},{3,19},{4,20},{5,6},{6,5},{7,23},{8,24},{9,10},... | collective-permute-start | bytes 319496 | tf_op jit(solution)/shard_map/ppermute | solution.py:833

commit v6 on v5

--- a/solution.py
+++ b/solution.py
@@ -765,10 +765,12 @@
                 own * fold(weight * (g_even * g_even + g_odd * g_odd) + 0.1 * (x[0] * x[0] + x[1] * x[1]))
             )
     square_ref[...] += total_of(squares)
-    row = lax.broadcasted_iota(jnp.int32, (8, LANES), 0)
-    packed = jnp.zeros((8, LANES), F32)
+    packed = jnp.zeros((1, LANES), F32)
     for at, part in enumerate((dot_rz[...], dot_zq[...], dot_yq[...], square_ref[...])):
-        packed = jnp.where(row == at, jnp.sum(part, axis=0, keepdims=True), packed)
+        part = jnp.sum(part, axis=0, keepdims=True)
+        part = part + roll(part, HALF)
+        part = part + roll(part, QUART)
+        packed = jnp.where((lane_iota() >> 5) == at, part, packed)
     for d in range(sums_ref.shape[0]):
         sums_ref[d] = packed
 
@@ -778,8 +780,9 @@
     total = sums_ref[0]
     for d in range(1, sums_ref.shape[0]):
         total = total + sums_ref[d]
-    total = jnp.sum(total, axis=1, keepdims=True)
-    rz, zq, yq, yp = (total[k : k + 1] for k in range(4))
+    rz, zq, yq, yp = (
+        jnp.sum(jnp.where((lane_iota() >> 5) == k, total, 0.0), axis=1, keepdims=True) for k in range(4)
+    )
     alpha = rz / zq
     rz_next = alpha * alpha * yq - rz
     grown = 1.0 + rz_next / rz
@@ -932,7 +935,7 @@
 
     image_y, sums = call(
         functools.partial(stage_third, slots),
-        ((2, rows, LANES), (n_gx * n_gy, 8, LANES)),
+        ((2, rows, LANES), (n_gx * n_gy, 1, LANES)),
         meta, table, y, weights, spread, dot_rz, dot_zq, dot_yq, ya, yb,
         scalars=2,
         scratch=[

time: 81.6 us -> 81.1 us (level)
  no operation moved by 1% of the time
where the time goes in v6:
time: 81.1 us; the launch traced here: 80.8 us
  Pallas kernels  24.1 us (30%)
  waiting for transfers between devices  23.3 us (29%)
  starting transfers between devices  17.7 us (22%)
  blocking collectives  9.75 us (12%)
  local copies, waits for them, and re-layouts  4.44 us (5%)
  between operations  1.48 us (2%)
    pallas_call x12, Pallas kernels, call(): pl.pallas_call(kernel, out_shape=[jax.ShapeDtypeStruct(shape, F32) for sh...  24.1 us
    ppermute x9, waiting for transfers between devices, swap(): lax.ppermute(b, axes, pairs(lambda i: i - 1 if i % 2 == 0 else i + 1))  13.9 us
    all_to_all x1, blocking collectives, shards(): sums = lax.all_to_all(sums, ('gx', 'gy'), 0, 0)  9.75 us
    ppermute x9, starting transfers between devices, swap(): lax.ppermute(b, axes, pairs(lambda i: i - 1 if i % 2 == 0 else i + 1))  8.6 us
    ppermute x9, waiting for transfers between devices, swap(): lax.ppermute(a, axes, pairs(lambda i: i ^ 1))  7.9 us
    ppermute x9, starting transfers between devices, swap(): lax.ppermute(a, axes, pairs(lambda i: i ^ 1))  6.35 us
    unnamed x10, local copies, waits for them, and re-layouts  4.26 us
    ppermute x3, starting transfers between devices, shards(): lax.ppermute(x, 'layer', [(i, (i + k) % slots) for i in range(slots)])  2.73 us
  transfers between devices with their start and end apart: 21, of which 10 were waited for; matrix products, arithmetic and copies ran while one was open for 2% of the time, Pallas kernels for 10%

profile of v6, /device:TPU:0, one launch (start us, length us, event | category | flops | bytes accessed | tf_op | source)
XLA Modules:
  0.0 80.8 jit_solution(10359466103716081347)
XLA Ops:
  1.3 0.8 %copy-done.1 = f32[1,128,128]{2,1,0:T(8,128)S(1)} copy-done((f32[1,128,128]{2,1,0:T(8,128)S(1)}, f32[1,128,128]{2,1,0:T(8,128)}, u32[]{:S(2)}) %copy-start.1) | copy-done | bytes 65560
  2.2 0.8 %copy-done.3 = f32[1,128,128]{2,1,0:T(8,128)S(1)} copy-done((f32[1,128,128]{2,1,0:T(8,128)S(1)}, f32[1,128,128]{2,1,0:T(8,128)}, u32[]{:S(2)}) %copy-start.3) | copy-done | bytes 65560
  3.0 0.7 shard_map.77
  3.7 3.1 %collective-permute-start = (f32[80,128]{1,0:T(8,128)S(1)}, f32[80,128]{1,0:T(8,128)S(1)}, u32[]{:S(2)}, u32[]{:S(2)}) collective-permute-start(f32[80,128]{1,0:T(8,128)S(1)} %get-tuple-element.34), channel_id=1, source_target_pairs={{0,4},{1,5},{2,6},{3,7},{4,0},{5,1},{6,2},{7,3},{8,12},{9,13},{10,... | collective-permute-start | bytes 122888 | tf_op jit(solution)/shard_map/ppermute | solution.py:835
  6.8 1.5 %collective-permute-start.1 = (f32[80,128]{1,0:T(8,128)S(1)}, f32[80,128]{1,0:T(8,128)S(1)}, u32[]{:S(2)}, u32[]{:S(2)}) collective-permute-start(f32[80,128]{1,0:T(8,128)S(1)} %get-tuple-element.35), channel_id=1, source_target_pairs={{0,16},{1,17},{2,18},{3,19},{4,8},{5,9},{6,10},{7,11},{8,4},{9,5},... | collective-permute-start | bytes 122888 | tf_op jit(solution)/shard_map/ppermute | solution.py:836
  8.9 0.8 copy.10
  9.7 0.8 copy.11
  10.6 1.6 %collective-permute-start.5 = (f32[80,128]{1,0:T(8,128)S(1)}, f32[80,128]{1,0:T(8,128)S(1)}, u32[]{:S(2)}, u32[]{:S(2)}) collective-permute-start(f32[80,128]{1,0:T(8,128)S(1)} %collective-permute-done._.refs_2_), channel_id=1, source_target_pairs={{0,16},{16,0},{1,17},{17,1},{2,18},{18,2},{3,19},{19,3},{4,20},{20... | collective-permute-start | bytes 122888 | tf_op jit(solution)/shard_map/ppermute | solution.py:859
  12.9 1.0 %copy-done = s32[8,128,128]{2,1,0:T(8,128)S(1)} copy-done((s32[8,128,128]{2,1,0:T(8,128)S(1)}, s32[8,128,128]{2,1,0:T(8,128)}, u32[]{:S(2)}) %copy-start) | copy-done | bytes 524312
  13.9 0.8 shard_map.78
  14.9 1.3 %collective-permute-done.6.refs_5_ = f32[80,128]{1,0:T(8,128)S(1)} collective-permute-done((f32[80,128]{1,0:T(8,128)S(1)}, f32[80,128]{1,0:T(8,128)S(1)}, u32[]{:S(2)}, u32[]{:S(2)}) %collective-permute-start.6) | collective-permute-done | bytes 40992 | tf_op jit(solution)/shard_map/ppermute | solution.py:859
  16.2 1.5 %shard_map.79 = (f32[416,128]{1,0:T(8,128)S(1)}, f32[416,128]{1,0:T(8,128)S(1)}) custom-call(s32[8]{0:T(128)S(1)} %compare_select_fusion.6.meta_ref, f32[264,128]{1,0:T(8,128)S(1)} %get-tuple-element.39.refs_0_, f32[264,128]{1,0:T(8,128)S(1)} %collective-permute-done.4.refs_1_, f32[80,128]{1,0:T(8,128)S(1)} %collective-permute-done._.refs_2_, ...), custom_call_target="tpu_custom_call" | custom-call | tf_op jit(solution)/shard_map/pallas_call | solution.py:806
  18.4 2.5 %collective-permute-start.2 = (f32[320,128]{1,0:T(8,128)S(1)}, f32[320,128]{1,0:T(8,128)S(1)}, u32[]{:S(2)}, u32[]{:S(2)}) collective-permute-start(f32[320,128]{1,0:T(8,128)S(1)} %get-tuple-element.37), channel_id=1, source_target_pairs={{0,4},{1,5},{2,6},{3,7},{4,0},{5,1},{6,2},{7,3},{8,12},{9,13},{10,... | collective-permute-start | bytes 491528 | tf_op jit(solution)/shard_map/ppermute | solution.py:835
  21.5 4.1 %collective-permute-done.2.va = f32[320,128]{1,0:T(8,128)S(1)} collective-permute-done((f32[320,128]{1,0:T(8,128)S(1)}, f32[320,128]{1,0:T(8,128)S(1)}, u32[]{:S(2)}, u32[]{:S(2)}) %collective-permute-start.2) | collective-permute-done | bytes 163872 | tf_op jit(solution)/shard_map/ppermute | solution.py:835
  25.5 1.6 %collective-permute-done.3.vb = f32[320,128]{1,0:T(8,128)S(1)} collective-permute-done((f32[320,128]{1,0:T(8,128)S(1)}, f32[320,128]{1,0:T(8,128)S(1)}, u32[]{:S(2)}, u32[]{:S(2)}) %collective-permute-start.3) | collective-permute-done | bytes 163872 | tf_op jit(solution)/shard_map/ppermute | solution.py:836
  28.0 1.3 %collective-permute-start.10 = (f32[832,128]{1,0:T(8,128)S(1)}, f32[832,128]{1,0:T(8,128)S(1)}, u32[]{:S(2)}, u32[]{:S(2)}) collective-permute-start(f32[832,128]{1,0:T(8,128)S(1)} %get-tuple-element.43), channel_id=1, source_target_pairs={{0,16},{1,2},{2,1},{3,19},{4,20},{5,6},{6,5},{7,23},{8,24},{9,10},... | collective-permute-start | bytes 1277960 | tf_op jit(solution)/shard_map/ppermute | solution.py:836
  30.2 3.0 %shard_map.81 = (f32[8,2,208,128]{3,2,1,0:T(8,128)S(1)}, f32[2,2,176,128]{3,2,1,0:T(8,128)S(1)}, f32[16,128]{1,0:T(8,128)S(1)}) custom-call(s32[8]{0:T(128)S(1)} %compare_select_fusion.6.meta_ref, s32[64]{0:T(128)S(1)} %pad_add_fusion.refs_6_.table_ref, f32[416,128]{1,0:T(8,128)S(1)} %collective-permute-done.7._.ga, ...), custom_call_target="tpu_custom_call" | custom-call | tf_op jit(solution)/shard_map/pallas_call | solution.py:806
  33.1 4.4 %collective-permute-done.10.nb.near_b = f32[832,128]{1,0:T(8,128)S(1)} collective-permute-done((f32[832,128]{1,0:T(8,128)S(1)}, f32[832,128]{1,0:T(8,128)S(1)}, u32[]{:S(2)}, u32[]{:S(2)}) %collective-permute-start.10) | collective-permute-done | bytes 426016 | tf_op jit(solution)/shard_map/ppermute | solution.py:836
  37.6 3.5 %shard_map.82 = (f32[1,2,128,128]{3,2,1,0:T(8,128)S(1)}, f32[176,128]{1,0:T(8,128)S(1)}, f32[176,128]{1,0:T(8,128)S(1)}, f32[2,128,128]{2,1,0:T(8,128)S(1)}, f32[8,128]{1,0:T(8,128)S(1)}) custom-call(s32[8]{0:T(128)S(1)} %compare_select_fusion.6.meta_ref, s32[64]{0:T(128)S(1)} %pad_add_fusion.refs_6_.table_ref, ...), custom_call_target="tpu_custom_call" | custom-call | tf_op jit(solution)/shard_map/pallas_call | solution.py:806
  41.8 1.1 %collective-permute-start.14 = (f32[256,128]{1,0:T(8,128)S(1)}, f32[256,128]{1,0:T(8,128)S(1)}, u32[]{:S(2)}, u32[]{:S(2)}) collective-permute-start(f32[256,128]{1,0:T(8,128)S(1)} %get-tuple-element.52), channel_id=1, source_target_pairs={{0,16},{1,2},{2,1},{3,19},{4,20},{5,6},{6,5},{7,23},{8,24},{9,10},... | collective-permute-start | bytes 393224 | tf_op jit(solution)/shard_map/ppermute | solution.py:836
  42.9 1.0 %collective-permute-start.16 = (f32[176,128]{1,0:T(8,128)S(1)}, f32[176,128]{1,0:T(8,128)S(1)}, u32[]{:S(2)}, u32[]{:S(2)}) collective-permute-start(f32[176,128]{1,0:T(8,128)S(1)} %get-tuple-element.54), channel_id=1, source_target_pairs={{0,16},{1,17},{2,18},{3,19},{4,8},{5,9},{6,10},{7,11},{8,4},{9,5},... | collective-permute-start | bytes 270344 | tf_op jit(solution)/shard_map/ppermute | solution.py:836
  43.9 3.5 %collective-permute-done.15.za = f32[176,128]{1,0:T(8,128)S(1)} collective-permute-done((f32[176,128]{1,0:T(8,128)S(1)}, f32[176,128]{1,0:T(8,128)S(1)}, u32[]{:S(2)}, u32[]{:S(2)}) %collective-permute-start.15) | collective-permute-done | bytes 90144 | tf_op jit(solution)/shard_map/ppermute | solution.py:835
  47.5 0.9 %collective-permute-done.16.zb = f32[176,128]{1,0:T(8,128)S(1)} collective-permute-done((f32[176,128]{1,0:T(8,128)S(1)}, f32[176,128]{1,0:T(8,128)S(1)}, u32[]{:S(2)}, u32[]{:S(2)}) %collective-permute-start.16) | collective-permute-done | bytes 90144 | tf_op jit(solution)/shard_map/ppermute | solution.py:836
  49.2 1.0 %collective-permute-start.18 = (f32[304,128]{1,0:T(8,128)S(1)}, f32[304,128]{1,0:T(8,128)S(1)}, u32[]{:S(2)}, u32[]{:S(2)}) collective-permute-start(f32[304,128]{1,0:T(8,128)S(1)} %get-tuple-element.56), channel_id=1, source_target_pairs={{0,16},{1,2},{2,1},{3,19},{4,20},{5,6},{6,5},{7,23},{8,24},{9,10},... | collective-permute-start | bytes 466952 | tf_op jit(solution)/shard_map/ppermute | solution.py:836
  50.1 0.9 %shard_map.84.valid_ref = f32[8,2,272,128]{3,2,1,0:T(8,128)S(1)} custom-call(s32[8]{0:T(128)S(1)} %compare_select_fusion.6.meta_ref, f32[4,2,128,128]{3,2,1,0:T(8,128)S(1)} %get-tuple-element.36.refs_7_.v_ref, f32[320,128]{1,0:T(8,128)S(1)} %collective-permute-done.2.va, f32[320,128]{1,0:T(8,128)S(1)} %collective-permute-done.3.vb, ...), custom_call_target="tpu_custom_call" | custom-call | tf_op jit(solution)/shard_map/pallas_call | solution.py:806
  51.1 3.4 %collective-permute-done.18.gb = f32[304,128]{1,0:T(8,128)S(1)} collective-permute-done((f32[304,128]{1,0:T(8,128)S(1)}, f32[304,128]{1,0:T(8,128)S(1)}, u32[]{:S(2)}, u32[]{:S(2)}) %collective-permute-start.18) | collective-permute-done | bytes 155680 | tf_op jit(solution)/shard_map/ppermute | solution.py:836
  54.5 7.2 %shard_map.86 = (f32[1,2,208,128]{3,2,1,0:T(8,128)S(1)}, f32[208,128]{1,0:T(8,128)S(1)}, f32[208,128]{1,0:T(8,128)S(1)}, f32[2,128,128]{2,1,0:T(8,128)S(1)}, f32[8,128]{1,0:T(8,128)S(1)}, /*index=5*/f32[8,128]{1,0:T(8,128)S(1)}) custom-call(s32[8]{0:T(128)S(1)} %compare_select_fusion.6.meta_ref, s32[64]{0:T(128)S(1)} %pad_add_fusion.refs_6_.table_ref, ...), custom_call_target="tpu_custom_call" | custom-call | tf_op jit(solution)/shard_map/pallas_call | solution.py:806
  61.9 0.9 %collective-permute-start.20 = (f32[208,128]{1,0:T(8,128)S(1)}, f32[208,128]{1,0:T(8,128)S(1)}, u32[]{:S(2)}, u32[]{:S(2)}) collective-permute-start(f32[208,128]{1,0:T(8,128)S(1)} %get-tuple-element.63), channel_id=1, source_target_pairs={{0,16},{1,2},{2,1},{3,19},{4,20},{5,6},{6,5},{7,23},{8,24},{9,10},... | collective-permute-start | bytes 319496 | tf_op jit(solution)/shard_map/ppermute | solution.py:836
  63.0 3.5 %collective-permute-done.20.gb = f32[208,128]{1,0:T(8,128)S(1)} collective-permute-done((f32[208,128]{1,0:T(8,128)S(1)}, f32[208,128]{1,0:T(8,128)S(1)}, u32[]{:S(2)}, u32[]{:S(2)}) %collective-permute-start.20) | collective-permute-done | bytes 106528 | tf_op jit(solution)/shard_map/ppermute | solution.py:836
  66.6 3.5 %shard_map.87 = (f32[2,128,128]{2,1,0:T(8,128)S(1)}, f32[16,1,128]{2,1,0:T(1,128)S(1)}) custom-call(s32[8]{0:T(128)S(1)} %compare_select_fusion.6.meta_ref, s32[64]{0:T(128)S(1)} %pad_add_fusion.refs_6_.table_ref, f32[1,2,208,128]{3,2,1,0:T(8,128)S(1)} %get-tuple-element.58.y_ref, f32[16,128]{1,0:T(8,128)S(1)} %get-tuple-element.46.reg_ref.__, ...), custom_call_target="tpu_custom_call" | custom-call | tf_op jit(solution)/shard_map/pallas_call | solution.py:806
  70.0 9.8 %all_to_all.5.sums_ref = f32[16,1,128]{2,1,0:T(1,128)S(1)} all-to-all(f32[16,1,128]{2,1,0:T(1,128)S(1)} %get-tuple-element.65), channel_id=1, replica_groups=mesh['layer'=2,'gx'=4,'gy'=4] {'gx','gy'}, dimensions={0} | all-to-all | bytes 16384 | tf_op jit(solution)/shard_map/all_to_all | solution.py:950
  79.8 1.0 %shard_map.88 = (f32[1,128,128]{2,1,0:T(8,128)}, f32[1,128,128]{2,1,0:T(8,128)}) custom-call(f32[1,128,128]{2,1,0:T(8,128)S(1)} %copy-done.2, f32[1,2,128,128]{3,2,1,0:T(8,128)S(1)} %get-tuple-element.47._.z_ref, f32[2,128,128]{2,1,0:T(8,128)S(1)} %get-tuple-element.48.res_ref, f32[2,128,128]{2,1,0:T(8,128)S(1)} %get-tuple-element.57.q_ref, ...), custom_call_target="tpu_custom_call" | custom-call | tf_op jit(solution)/shard_map/pallas_call | solution.py:806
  (37 shorter events, 6.5 us)
Async XLA Ops:
  1.3 0.8 %copy-start.1 = (f32[1,128,128]{2,1,0:T(8,128)S(1)}, f32[1,128,128]{2,1,0:T(8,128)}, u32[]{:S(2)}) copy-start(f32[1,128,128]{2,1,0:T(8,128)} %start_ref.3) | copy-start | bytes 196612
  2.1 0.8 %copy-start.3 = (f32[1,128,128]{2,1,0:T(8,128)S(1)}, f32[1,128,128]{2,1,0:T(8,128)}, u32[]{:S(2)}) copy-start(f32[1,128,128]{2,1,0:T(8,128)} %rhs_ref.1) | copy-start | bytes 196612
  3.7 6.8 %collective-permute-start = (f32[80,128]{1,0:T(8,128)S(1)}, f32[80,128]{1,0:T(8,128)S(1)}, u32[]{:S(2)}, u32[]{:S(2)}) collective-permute-start(f32[80,128]{1,0:T(8,128)S(1)} %get-tuple-element.34), channel_id=1, source_target_pairs={{0,4},{1,5},{2,6},{3,7},{4,0},{5,1},{6,2},{7,3},{8,12},{9,13},{10,... | collective-permute-start | bytes 122888 | tf_op jit(solution)/shard_map/ppermute | solution.py:835
  6.8 5.4 %collective-permute-start.1 = (f32[80,128]{1,0:T(8,128)S(1)}, f32[80,128]{1,0:T(8,128)S(1)}, u32[]{:S(2)}, u32[]{:S(2)}) collective-permute-start(f32[80,128]{1,0:T(8,128)S(1)} %get-tuple-element.35), channel_id=1, source_target_pairs={{0,16},{1,17},{2,18},{3,19},{4,8},{5,9},{6,10},{7,11},{8,4},{9,5},... | collective-permute-start | bytes 122888 | tf_op jit(solution)/shard_map/ppermute | solution.py:836
  8.3 7.8 %collective-permute-start.4 = (f32[264,128]{1,0:T(8,128)S(1)}, f32[264,128]{1,0:T(8,128)S(1)}, u32[]{:S(2)}, u32[]{:S(2)}) collective-permute-start(f32[264,128]{1,0:T(8,128)S(1)} %get-tuple-element.39.refs_0_), channel_id=1, source_target_pairs={{0,16},{16,0},{1,17},{17,1},{2,18},{18,2},{3,19},{19,3},{4,20},{20... | collective-permute-start | bytes 405512 | tf_op jit(solution)/shard_map/ppermute | solution.py:859
  10.6 4.3 %collective-permute-start.5 = (f32[80,128]{1,0:T(8,128)S(1)}, f32[80,128]{1,0:T(8,128)S(1)}, u32[]{:S(2)}, u32[]{:S(2)}) collective-permute-start(f32[80,128]{1,0:T(8,128)S(1)} %collective-permute-done._.refs_2_), channel_id=1, source_target_pairs={{0,16},{16,0},{1,17},{17,1},{2,18},{18,2},{3,19},{19,3},{4,20},{20... | collective-permute-start | bytes 122888 | tf_op jit(solution)/shard_map/ppermute | solution.py:859
  12.2 4.0 %collective-permute-start.6 = (f32[80,128]{1,0:T(8,128)S(1)}, f32[80,128]{1,0:T(8,128)S(1)}, u32[]{:S(2)}, u32[]{:S(2)}) collective-permute-start(f32[80,128]{1,0:T(8,128)S(1)} %collective-permute-done.1.__.refs_4_), channel_id=1, source_target_pairs={{0,16},{16,0},{1,17},{17,1},{2,18},{18,2},{3,19},{19,3},{4,20},{20... | collective-permute-start | bytes 122888 | tf_op jit(solution)/shard_map/ppermute | solution.py:859
  12.9 1.0 %copy-start = (s32[8,128,128]{2,1,0:T(8,128)S(1)}, s32[8,128,128]{2,1,0:T(8,128)}, u32[]{:S(2)}) copy-start(s32[8,128,128]{2,1,0:T(8,128)} %valid_ref.1) | copy-start | bytes 1572868
  17.6 9.5 %collective-permute-start.7 = (f32[416,128]{1,0:T(8,128)S(1)}, f32[416,128]{1,0:T(8,128)S(1)}, u32[]{:S(2)}, u32[]{:S(2)}) collective-permute-start(f32[416,128]{1,0:T(8,128)S(1)} %get-tuple-element.40), channel_id=1, source_target_pairs={{0,1},{1,0},{2,3},{3,2},{4,5},{5,4},{6,7},{7,6},{8,9},{9,8},{10,11... | collective-permute-start | bytes 638984 | tf_op jit(solution)/shard_map/ppermute | solution.py:835
  17.7 9.4 %collective-permute-start.8 = (f32[416,128]{1,0:T(8,128)S(1)}, f32[416,128]{1,0:T(8,128)S(1)}, u32[]{:S(2)}, u32[]{:S(2)}) collective-permute-start(f32[416,128]{1,0:T(8,128)S(1)} %get-tuple-element.41), channel_id=1, source_target_pairs={{0,16},{1,2},{2,1},{3,19},{4,20},{5,6},{6,5},{7,23},{8,24},{9,10},... | collective-permute-start | bytes 638984 | tf_op jit(solution)/shard_map/ppermute | solution.py:836
  18.4 7.1 %collective-permute-start.2 = (f32[320,128]{1,0:T(8,128)S(1)}, f32[320,128]{1,0:T(8,128)S(1)}, u32[]{:S(2)}, u32[]{:S(2)}) collective-permute-start(f32[320,128]{1,0:T(8,128)S(1)} %get-tuple-element.37), channel_id=1, source_target_pairs={{0,4},{1,5},{2,6},{3,7},{4,0},{5,1},{6,2},{7,3},{8,12},{9,13},{10,... | collective-permute-start | bytes 491528 | tf_op jit(solution)/shard_map/ppermute | solution.py:835
  20.9 6.2 %collective-permute-start.3 = (f32[320,128]{1,0:T(8,128)S(1)}, f32[320,128]{1,0:T(8,128)S(1)}, u32[]{:S(2)}, u32[]{:S(2)}) collective-permute-start(f32[320,128]{1,0:T(8,128)S(1)} %get-tuple-element.38), channel_id=1, source_target_pairs={{0,16},{1,17},{2,18},{3,19},{4,8},{5,9},{6,10},{7,11},{8,4},{9,5},... | collective-permute-start | bytes 491528 | tf_op jit(solution)/shard_map/ppermute | solution.py:836
  27.9 5.3 %collective-permute-start.9 = (f32[832,128]{1,0:T(8,128)S(1)}, f32[832,128]{1,0:T(8,128)S(1)}, u32[]{:S(2)}, u32[]{:S(2)}) collective-permute-start(f32[832,128]{1,0:T(8,128)S(1)} %get-tuple-element.42), channel_id=1, source_target_pairs={{0,1},{1,0},{2,3},{3,2},{4,5},{5,4},{6,7},{7,6},{8,9},{9,8},{10,11... | collective-permute-start | bytes 1277960 | tf_op jit(solution)/shard_map/ppermute | solution.py:835
  28.0 9.6 %collective-permute-start.10 = (f32[832,128]{1,0:T(8,128)S(1)}, f32[832,128]{1,0:T(8,128)S(1)}, u32[]{:S(2)}, u32[]{:S(2)}) collective-permute-start(f32[832,128]{1,0:T(8,128)S(1)} %get-tuple-element.43), channel_id=1, source_target_pairs={{0,16},{1,2},{2,1},{3,19},{4,20},{5,6},{6,5},{7,23},{8,24},{9,10},... | collective-permute-start | bytes 1277960 | tf_op jit(solution)/shard_map/ppermute | solution.py:836
  29.3 11.8 %collective-permute-start.11 = (f32[256,128]{1,0:T(8,128)S(1)}, f32[256,128]{1,0:T(8,128)S(1)}, u32[]{:S(2)}, u32[]{:S(2)}) collective-permute-start(f32[256,128]{1,0:T(8,128)S(1)} %get-tuple-element.49), channel_id=1, source_target_pairs={{0,4},{1,5},{2,6},{3,7},{4,0},{5,1},{6,2},{7,3},{8,12},{9,13},{10,... | collective-permute-start | bytes 393224 | tf_op jit(solution)/shard_map/ppermute | solution.py:835
  29.5 11.6 %collective-permute-start.12 = (f32[256,128]{1,0:T(8,128)S(1)}, f32[256,128]{1,0:T(8,128)S(1)}, u32[]{:S(2)}, u32[]{:S(2)}) collective-permute-start(f32[256,128]{1,0:T(8,128)S(1)} %get-tuple-element.50), channel_id=1, source_target_pairs={{0,16},{1,17},{2,18},{3,19},{4,8},{5,9},{6,10},{7,11},{8,4},{9,5},... | collective-permute-start | bytes 393224 | tf_op jit(solution)/shard_map/ppermute | solution.py:836
  41.8 6.7 %collective-permute-start.13 = (f32[256,128]{1,0:T(8,128)S(1)}, f32[256,128]{1,0:T(8,128)S(1)}, u32[]{:S(2)}, u32[]{:S(2)}) collective-permute-start(f32[256,128]{1,0:T(8,128)S(1)} %get-tuple-element.51), channel_id=1, source_target_pairs={{0,1},{1,0},{2,3},{3,2},{4,5},{5,4},{6,7},{7,6},{8,9},{9,8},{10,11... | collective-permute-start | bytes 393224 | tf_op jit(solution)/shard_map/ppermute | solution.py:835
  41.8 6.6 %collective-permute-start.14 = (f32[256,128]{1,0:T(8,128)S(1)}, f32[256,128]{1,0:T(8,128)S(1)}, u32[]{:S(2)}, u32[]{:S(2)}) collective-permute-start(f32[256,128]{1,0:T(8,128)S(1)} %get-tuple-element.52), channel_id=1, source_target_pairs={{0,16},{1,2},{2,1},{3,19},{4,20},{5,6},{6,5},{7,23},{8,24},{9,10},... | collective-permute-start | bytes 393224 | tf_op jit(solution)/shard_map/ppermute | solution.py:836
  42.9 4.5 %collective-permute-start.15 = (f32[176,128]{1,0:T(8,128)S(1)}, f32[176,128]{1,0:T(8,128)S(1)}, u32[]{:S(2)}, u32[]{:S(2)}) collective-permute-start(f32[176,128]{1,0:T(8,128)S(1)} %get-tuple-element.53), channel_id=1, source_target_pairs={{0,4},{1,5},{2,6},{3,7},{4,0},{5,1},{6,2},{7,3},{8,12},{9,13},{10,... | collective-permute-start | bytes 270344 | tf_op jit(solution)/shard_map/ppermute | solution.py:835
  42.9 5.5 %collective-permute-start.16 = (f32[176,128]{1,0:T(8,128)S(1)}, f32[176,128]{1,0:T(8,128)S(1)}, u32[]{:S(2)}, u32[]{:S(2)}) collective-permute-start(f32[176,128]{1,0:T(8,128)S(1)} %get-tuple-element.54), channel_id=1, source_target_pairs={{0,16},{1,17},{2,18},{3,19},{4,8},{5,9},{6,10},{7,11},{8,4},{9,5},... | collective-permute-start | bytes 270344 | tf_op jit(solution)/shard_map/ppermute | solution.py:836
  49.1 2.0 %collective-permute-start.17 = (f32[304,128]{1,0:T(8,128)S(1)}, f32[304,128]{1,0:T(8,128)S(1)}, u32[]{:S(2)}, u32[]{:S(2)}) collective-permute-start(f32[304,128]{1,0:T(8,128)S(1)} %get-tuple-element.55), channel_id=1, source_target_pairs={{0,1},{1,0},{2,3},{3,2},{4,5},{5,4},{6,7},{7,6},{8,9},{9,8},{10,11... | collective-permute-start | bytes 466952 | tf_op jit(solution)/shard_map/ppermute | solution.py:835
  49.2 5.3 %collective-permute-start.18 = (f32[304,128]{1,0:T(8,128)S(1)}, f32[304,128]{1,0:T(8,128)S(1)}, u32[]{:S(2)}, u32[]{:S(2)}) collective-permute-start(f32[304,128]{1,0:T(8,128)S(1)} %get-tuple-element.56), channel_id=1, source_target_pairs={{0,16},{1,2},{2,1},{3,19},{4,20},{5,6},{6,5},{7,23},{8,24},{9,10},... | collective-permute-start | bytes 466952 | tf_op jit(solution)/shard_map/ppermute | solution.py:836
  51.0 28.7 %copy-start.2 = (f32[1,128,128]{2,1,0:T(8,128)S(1)}, f32[1,128,128]{2,1,0:T(8,128)}, u32[]{:S(2)}) copy-start(f32[1,128,128]{2,1,0:T(8,128)} %start_ref.3) | copy-start | bytes 196612
  61.7 1.4 %collective-permute-start.19 = (f32[208,128]{1,0:T(8,128)S(1)}, f32[208,128]{1,0:T(8,128)S(1)}, u32[]{:S(2)}, u32[]{:S(2)}) collective-permute-start(f32[208,128]{1,0:T(8,128)S(1)} %get-tuple-element.62), channel_id=1, source_target_pairs={{0,1},{1,0},{2,3},{3,2},{4,5},{5,4},{6,7},{7,6},{8,9},{9,8},{10,11... | collective-permute-start | bytes 319496 | tf_op jit(solution)/shard_map/ppermute | solution.py:835
  61.9 4.7 %collective-permute-start.20 = (f32[208,128]{1,0:T(8,128)S(1)}, f32[208,128]{1,0:T(8,128)S(1)}, u32[]{:S(2)}, u32[]{:S(2)}) collective-permute-start(f32[208,128]{1,0:T(8,128)S(1)} %get-tuple-element.63), channel_id=1, source_target_pairs={{0,16},{1,2},{2,1},{3,19},{4,20},{5,6},{6,5},{7,23},{8,24},{9,10},... | collective-permute-start | bytes 319496 | tf_op jit(solution)/shard_map/ppermute | solution.py:836
